TPU v7x, 32 devices: a whole 2x2x4 slice. The times are simulated.
32 devices in a mesh: gx: 4 (over z), gy: 4 (over y, core), gz: 2 (over x).
Axes of the slice: x: 2, y: 2, z: 4, core: 2. Of those that a mesh axis runs over, the one named last changes fastest.
Arguments:
- coarse_source: float32 [64, 128, 256], P('gx', 'gy', 'gz'), may hold values from -6 to 6
- coarse_shift: float32 [64, 128, 256], P('gx', 'gy', 'gz'), may hold values from 0.1 to 4
- coarse_start: float32 [64, 128, 256], P('gx', 'gy', 'gz'), may hold values from -3 to 3
- fine_source: float32 [128, 32768], P(('gx', 'gy', 'gz')), may hold values from -6 to 6
- fine_shift: float32 [128, 32768], P(('gx', 'gy', 'gz')), may hold values from 0.1 to 4
- fine_start: float32 [128, 32768], P(('gx', 'gy', 'gz')), may hold values from -3 to 3
- box_corner: int32 [32, 4, 3], P(('gx', 'gy', 'gz')), may hold values from 0 to 480, as said below
- box_owner: int32 [32, 4], P(('gx', 'gy', 'gz')), may hold values from 0 to 8, as said below
Outputs:
- potential: float32 [64, 128, 256], P('gx', 'gy', 'gz')
- fine_solution: float32 [128, 32768], P(('gx', 'gy', 'gz'))
- residual_norms: float32 [2], replicated
Inputs may be any that keep to these rules, and one draw needn't show every extreme that they name: `box_owner`: each device has at least one live slot; in every group of 8 devices that share a gx index some device has 4 live slots; the live owners of one device are distinct; no device is the owner of more than 4 live boxes, and in every group some device is the owner of exactly 4 live boxes. `box_corner`: each corner is a multiple of 32 and its footprint lies in the coarse block of the device that lists it; the 4 footprints of one device are distinct.
All inputs are finite; a program needn't handle non-finite values.
Results may differ from a plain program's by a relative error of at most 0.0001.
Values sent between devices are 32-bit elements; how exact they have to be, the bound alone decides.
No kernel may reach another device: no remote copies, remote signals or barrier semaphores. Data moves between devices by JAX's collectives and lax.ppermute only.
A program may use at most 128 MiB of HBM per device.

v0:
```python
import jax
import jax.numpy as jnp
from jax import lax
from jax.sharding import PartitionSpec as P

FOOT = 16
CYCLES = 2
CSWEEPS = 4
FSWEEPS = 3


OMEGA = 0.8
HIGHEST = lax.Precision.HIGHEST


def extended(block, sides, width):
    for axis, dim in sides:
        count = lax.axis_size(axis)
        forward = [(i, i + 1) for i in range(count - 1)]
        backward = [(target, source) for source, target in forward]
        low = lax.ppermute(
            lax.slice_in_dim(block, block.shape[dim] - width, None, axis=dim), axis, forward
        )
        high = lax.ppermute(lax.slice_in_dim(block, 0, width, axis=dim), axis, backward)
        block = jnp.concatenate([low, block, high], axis=dim)
    return block


def to_blocks(field):
    extent = field.shape
    shaped = field.reshape(
        extent[0] // FOOT, FOOT, extent[1] // FOOT, FOOT, extent[2] // FOOT, FOOT
    )
    return shaped.transpose(0, 2, 4, 1, 3, 5).reshape(-1, FOOT * FOOT * FOOT)


def from_blocks(blocks, extent):
    shaped = blocks.reshape(
        extent[0] // FOOT, extent[1] // FOOT, extent[2] // FOOT, FOOT, FOOT, FOOT
    )
    return shaped.transpose(0, 3, 1, 4, 2, 5).reshape(extent)


def inject(parents):
    number = parents.shape[0]
    shaped = parents.reshape(number, FOOT, 1, FOOT, 1, FOOT, 1)
    spread = jnp.broadcast_to(shaped, (number, FOOT, 2, FOOT, 2, FOOT, 2))
    return spread.reshape(number, 8 * FOOT * FOOT * FOOT)


def restrict(values):
    number = values.shape[0]
    return (
        values.reshape(number, FOOT, 2, FOOT, 2, FOOT, 2)
        .mean(axis=(2, 4, 6))
        .reshape(number, FOOT * FOOT * FOOT)
    )


def fine_residual(values, parents, source, shift):
    ghost = inject(parents)
    side = 2 * FOOT
    position = jnp.arange(side * side * side, dtype=jnp.int32)[None, :]
    summed = jnp.zeros_like(values)
    for stride in (1, side, side * side):
        coordinate = position // stride % side
        upper = jnp.roll(values, -stride, axis=1)
        lower = jnp.roll(values, stride, axis=1)
        summed = (
            summed
            + jnp.where(coordinate < side - 1, upper, ghost)
            + jnp.where(coordinate > 0, lower, ghost)
        )
    return source - (6.0 + shift) * values + summed


def beside_sum(padded):
    summed = padded[2:, 1:-1, 1:-1] + padded[:-2, 1:-1, 1:-1]
    summed = summed + padded[1:-1, 2:, 1:-1] + padded[1:-1, :-2, 1:-1]
    return summed + padded[1:-1, 1:-1, 2:] + padded[1:-1, 1:-1, :-2]


def edge_mask(start, count, total):
    coords = start - 2 + jnp.arange(count + 4, dtype=jnp.int32)
    return (coords >= 0) & (coords < total)


def inside_mask(extent):
    mask_x = edge_mask(lax.axis_index("gx") * extent[0], extent[0], extent[0] * lax.axis_size("gx"))
    mask_y = edge_mask(lax.axis_index("gy") * extent[1], extent[1], extent[1] * lax.axis_size("gy"))
    mask_z = edge_mask(lax.axis_index("gz") * extent[2], extent[2], extent[2] * lax.axis_size("gz"))
    return mask_x[:, None, None] & mask_y[None, :, None] & mask_z[None, None, :]


def local(
    coarse_source,
    coarse_shift,
    coarse_start,
    fine_source,
    fine_shift,
    fine_start,
    box_corner,
    box_owner,
):
    extent = coarse_source.shape
    size_y = lax.axis_size("gy")
    size_z = lax.axis_size("gz")
    group = size_y * size_z
    slots = box_owner.shape[1]
    anchor = jnp.stack(
        [
            lax.axis_index("gx") * extent[0],
            lax.axis_index("gy") * extent[1],
            lax.axis_index("gz") * extent[2],
        ]
    )
    along_y = extent[1] // FOOT
    along_z = extent[2] // FOOT
    places = extent[0] // FOOT * along_y * along_z
    block = (box_corner[0] // 2 - anchor[None, :]) // FOOT
    location = (block[:, 0] * along_y + block[:, 1]) * along_z + block[:, 2]
    live = (box_owner[0] < group).astype(jnp.float32)
    peer_ids = jnp.arange(group, dtype=jnp.int32)
    route = (box_owner[0][None, :] == peer_ids[:, None]).astype(jnp.float32) * live[None, :]
    locate = (jnp.arange(places, dtype=jnp.int32)[:, None] == location[None, :]).astype(jnp.float32)
    collect = jnp.dot(route, locate.T, precision=HIGHEST)
    deposit = collect.T
    live_out = jnp.sum(route, axis=1, keepdims=True)
    diagonal = 6.0 + coarse_shift
    fine_diagonal = 6.0 + fine_shift

    def send_parents(potential):
        outgoing = jnp.dot(collect, to_blocks(potential), precision=HIGHEST)
        parents, flags = (
            lax.all_to_all(outgoing, ("gy", "gz"), split_axis=0, concat_axis=0, tiled=True),
            lax.all_to_all(live_out, ("gy", "gz"), split_axis=0, concat_axis=0, tiled=True),
        )
        return (parents, flags)

    inside = inside_mask(extent)
    inner = inside[1:-1, 1:-1, 1:-1]
    shift_wide = extended(diagonal, (("gx", 0), ("gy", 1), ("gz", 2)), 2)
    scale = jnp.where(inside, shift_wide, 6.0)
    scale_inner = scale[1:-1, 1:-1, 1:-1]
    potential = coarse_start
    values = fine_start
    earlier = None
    norms = []
    pick = None
    occupied = None
    for cycle in range(CYCLES):
        received, flags = send_parents(potential)
        if pick is None:
            flag_vec = flags[:, 0]
            before = jnp.cumsum(flag_vec) - flag_vec
            pick = (jnp.arange(slots, dtype=jnp.float32)[:, None] == before[None, :]).astype(
                jnp.float32
            ) * flag_vec[None, :]
            occupied = jnp.sum(pick, axis=1, keepdims=True)
        parents = jnp.dot(pick, received, precision=HIGHEST)
        if cycle > 0:
            values = values + inject(parents - earlier)
        for sweep in range(FSWEEPS):
            values = (
                values
                + OMEGA * fine_residual(values, parents, fine_source, fine_shift) / fine_diagonal
            )
        remainder = fine_residual(values, parents, fine_source, fine_shift)
        sent_back = jnp.dot(pick.T, restrict(remainder) * occupied, precision=HIGHEST)
        returned = lax.all_to_all(sent_back, ("gy", "gz"), split_axis=0, concat_axis=0, tiled=True)
        composite = coarse_source + from_blocks(
            jnp.dot(deposit, returned, precision=HIGHEST), extent
        )
        smooth_potential = potential
        source_wide = extended(composite, (("gx", 0), ("gy", 1), ("gz", 2)), 2)
        source_inner = source_wide[1:-1, 1:-1, 1:-1]
        for sweep_pair in range(CSWEEPS // 2):
            field = extended(smooth_potential, (("gx", 0), ("gy", 1), ("gz", 2)), 2)
            centre = field[1:-1, 1:-1, 1:-1]
            first = source_inner - scale_inner * centre + beside_sum(field)
            middle = jnp.where(inner, centre + OMEGA * first / scale_inner, 0.0)
            residual = composite - diagonal * middle[1:-1, 1:-1, 1:-1] + beside_sum(middle)
            smooth_potential = middle[1:-1, 1:-1, 1:-1] + OMEGA * residual / diagonal
        potential = smooth_potential
        squares = jnp.sum(residual * residual)
        local_sum = squares + jnp.sum(occupied * remainder * remainder)
        norms.append(lax.psum(local_sum, ("gx", "gy", "gz")))
        earlier = parents
    received, flags = send_parents(potential)
    parents = jnp.dot(pick, received, precision=HIGHEST)
    values = (values + inject(parents - earlier)) * occupied
    cells = float(extent[0] * extent[1] * extent[2] * lax.axis_size("gx") * size_y * size_z)
    return (potential, values, jnp.sqrt(jnp.stack(norms) / cells))


def solution(mesh):
    in_specs = (
        P("gx", "gy", "gz"),
        P("gx", "gy", "gz"),
        P("gx", "gy", "gz"),
        P(("gx", "gy", "gz"), None),
        P(("gx", "gy", "gz"), None),
        P(("gx", "gy", "gz"), None),
        P(("gx", "gy", "gz"), None, None),
        P(("gx", "gy", "gz"), None),
    )
    out_specs = (P("gx", "gy", "gz"), P(("gx", "gy", "gz"), None), P())
    return jax.shard_map(local, mesh=mesh, in_specs=in_specs, out_specs=out_specs, check_vma=False)
```

profile of v0, /device:TPU:0, one launch (start us, length us, event | category | flops | bytes accessed | tf_op | source)
XLA Modules:
  0.0 499.2 jit_solution(5402457770921700320)
XLA Ops:
  2.1 4.9 collective-permute-start
  10.4 3.7 all-to-all-start
  17.0 5.2 %collective-permute-start.12 = (f32[2,32,128]{2,1,0:T(8,128)}, f32[2,32,128]{2,1,0:T(8,128)S(1)}, u32[]{:S(2)}, u32[]{:S(2)}) collective-permute-start(f32[2,32,128]{2,1,0:T(8,128)} %get-tuple-element.158), channel_id=1, source_target_pairs={{0,8},{8,16},{16,24},{1,9},{9,17},{17,25},{2,10},{10,18},{18,26},{... | collective-permute-start | bytes 98312 | tf_op jit(solution)/shard_map/ppermute | solution.py:21
  32.2 3.2 reshape.366
  37.3 4.2 all-to-all-start.1
  44.6 3.0 collective-permute-start.2
  49.6 4.9 collective-permute-start.14
  56.3 9.7 %broadcast_in_dim.322 = f32[4,16,2,16,2,16,2]{0,6,5,4,3,2,1:T(2,128)} broadcast(f32[4,16,16,16]{0,3,2,1:T(8,128)S(1)} %bitcast.135), dimensions={0,1,3,5} | broadcast | bytes 589824 | tf_op jit(solution)/shard_map/broadcast_in_dim | solution.py:47
  66.1 9.6 %copy.581 = f32[4,32768]{1,0:T(4,128)S(1)} copy(f32[4,32768]{0,1:T(8,128)} %bitcast.128) | data formatting | bytes 1048576 | tf_op jit(solution)/shard_map/reshape | solution.py:48
  75.8 3.9 fusion.106
  80.7 2.6 fusion.105
  84.2 2.6 fusion.104
  87.8 2.5 fusion.70
  90.3 8.6 %copy.605 = f32[4,32768]{0,1:T(8,128)} copy(f32[4,32768]{1,0:T(4,128)S(1)} %fusion.70) | data formatting | bytes 1048576 | tf_op jit(solution)/shard_map/add | solution.py:74
  98.9 13.6 %reduce_sum.77 = f32[4,16,16,16]{0,3,2,1:T(8,128)} reduce(f32[4,16,2,16,2,16,2]{0,6,5,4,3,2,1:T(2,128)} %bitcast.132, f32[]{:T(128)} %constant.236.clone.1), dimensions={2,4,6}, to_apply=%region_2.3 | reduce | flops 114688 | bytes 589828 | tf_op jit(solution)/shard_map/reduce_sum | solution.py:55
  117.0 4.0 all-to-all-start.2
  122.0 4.4 collective-permute-start.4
  129.1 3.4 convolution_bitcast_fusion.6
  134.0 2.2 reshape.369
  137.6 4.5 collective-permute-start.6
  145.2 3.0 collective-permute-start.8
  149.8 5.5 %collective-permute-start.16 = (f32[20,36,2]{2,1,0:T(8,128)S(1)}, f32[20,36,2]{2,1,0:T(8,128)S(1)}, u32[]{:S(2)}, u32[]{:S(2)}) collective-permute-start(f32[20,36,2]{2,1,0:T(8,128)S(1)} %get-tuple-element.130), channel_id=1, source_target_pairs={{0,1},{2,3},{4,5},{6,7},{8,9},{10,11},{12,13},{14,15},{16,17},{18,... | collective-permute-start | bytes 17288 | tf_op jit(solution)/shard_map/ppermute | solution.py:21
  156.8 4.6 collective-permute-start.10
  164.9 6.9 %collective-permute-done.11 = f32[20,36,2]{2,1,0:T(8,128)S(1)} collective-permute-done((f32[20,36,2]{2,1,0:T(8,128)S(1)}, f32[20,36,2]{2,1,0:T(8,128)S(1)}, u32[]{:S(2)}, u32[]{:S(2)}) %collective-permute-start.11) | collective-permute-done | bytes 5792 | tf_op jit(solution)/shard_map/ppermute | solution.py:24
  173.7 5.1 %fusion.37 = (f32[18,34,130]{2,1,0:T(8,128)S(1)}, f32[18,34,130]{2,1,0:T(8,128)S(1)}) fusion(f32[20,36,2]{2,1,0:T(8,128)} %collective-permute-done.4, f32[20,2,128]{2,1,0:T(2,128)S(1)} %copy-done.25, f32[20,32,128]{2,1,0:T(8,128)S(1)} %copy-done.10, f32[20,2,128]{2,1,0:T(2,128)S(1)} %copy-done.27, f32[20,36,2]{2,1,0:T(8,128)} %collective-permute-done.5, ...), kind=kLoop, calls=%fused_computation.104 | loop fusion | flops 2466360 | bytes 3447720 | tf_op jit(solution)/shard_map/jit(_where)/select_n | solution.py:181
  180.7 4.9 collective-permute-start.18
  188.4 3.0 collective-permute-start.20
  192.5 4.4 collective-permute-start.22
  198.7 7.6 %collective-permute-done.22 = f32[20,36,2]{2,1,0:T(8,128)S(1)} collective-permute-done((f32[20,36,2]{2,1,0:T(8,128)S(1)}, f32[20,36,2]{2,1,0:T(8,128)S(1)}, u32[]{:S(2)}, u32[]{:S(2)}) %collective-permute-start.22) | collective-permute-done | bytes 5792 | tf_op jit(solution)/shard_map/ppermute | solution.py:21
  206.4 4.1 collective-permute-done.23
  211.0 2.0 fusion.30
  216.1 3.3 copy.691
  219.5 3.2 reshape.371
  223.7 3.4 all-to-all-start.3
  229.0 5.4 %collective-permute-start.24 = (f32[2,32,128]{2,1,0:T(8,128)}, f32[2,32,128]{2,1,0:T(8,128)}, u32[]{:S(2)}, u32[]{:S(2)}) collective-permute-start(f32[2,32,128]{2,1,0:T(8,128)} %get-tuple-element.154), channel_id=1, source_target_pairs={{0,8},{8,16},{16,24},{1,9},{9,17},{17,25},{2,10},{10,18},{18,26},{... | collective-permute-start | bytes 98312 | tf_op jit(solution)/shard_map/ppermute | solution.py:21
  237.3 10.4 %broadcast_in_dim.331 = f32[4,16,2,16,2,16,2]{0,6,5,4,3,2,1:T(2,128)} broadcast(f32[4,16,16,16]{0,3,2,1:T(8,128)} %bitcast.133), dimensions={0,1,3,5} | broadcast | bytes 589824 | tf_op jit(solution)/shard_map/broadcast_in_dim | solution.py:47
  247.7 9.5 %copy.613 = f32[4,32768]{1,0:T(4,128)S(1)} copy(f32[4,32768]{0,1:T(8,128)} %bitcast.129) | data formatting | bytes 1048576 | tf_op jit(solution)/shard_map/reshape | solution.py:48
  264.7 10.4 %broadcast_in_dim.333 = f32[4,16,2,16,2,16,2]{0,6,5,4,3,2,1:T(2,128)} broadcast(f32[4,16,16,16]{0,3,2,1:T(8,128)} %bitcast.136), dimensions={0,1,3,5} | broadcast | bytes 589824 | tf_op jit(solution)/shard_map/broadcast_in_dim | solution.py:47
  275.0 9.5 %copy.615 = f32[4,32768]{1,0:T(4,128)S(1)} copy(f32[4,32768]{0,1:T(8,128)} %bitcast.130) | data formatting | bytes 1048576 | tf_op jit(solution)/shard_map/reshape | solution.py:48
  284.5 3.9 fusion.103
  289.4 2.6 fusion.102
  293.0 2.6 fusion.101
  296.8 4.1 fusion.39
  300.8 9.1 %copy.639 = f32[4,32768]{0,1:T(8,128)} copy(f32[4,32768]{1,0:T(4,128)} %get-tuple-element.21) | data formatting | bytes 1048576 | tf_op jit(solution)/shard_map/add | solution.py:74
  309.9 13.8 %reduce_sum.80 = f32[4,16,16,16]{0,3,2,1:T(8,128)} reduce(f32[4,16,2,16,2,16,2]{0,6,5,4,3,2,1:T(2,128)} %bitcast.127, f32[]{:T(128)} %constant.236.clone.1), dimensions={2,4,6}, to_apply=%region_4.5 | reduce | flops 114688 | bytes 589828 | tf_op jit(solution)/shard_map/reduce_sum | solution.py:55
  328.2 4.1 all-to-all-start.4
  334.5 3.0 collective-permute-start.26
  338.9 3.4 convolution_bitcast_fusion.5
  343.8 2.2 reshape.375
  347.4 4.5 collective-permute-start.30
  354.8 3.1 collective-permute-start.32
  358.1 3.9 collective-permute-start.28
  365.1 4.6 collective-permute-start.34
  371.3 4.8 collective-permute-done.29
  377.4 7.5 %collective-permute-done.35 = f32[20,36,2]{2,1,0:T(8,128)S(1)} collective-permute-done((f32[20,36,2]{2,1,0:T(8,128)S(1)}, f32[20,36,2]{2,1,0:T(8,128)S(1)}, u32[]{:S(2)}, u32[]{:S(2)}) %collective-permute-start.35) | collective-permute-done | bytes 5792 | tf_op jit(solution)/shard_map/ppermute | solution.py:24
  384.9 2.8 fusion.23
  389.5 5.2 %collective-permute-start.36 = (f32[2,32,128]{2,1,0:T(8,128)S(1)}, f32[2,32,128]{2,1,0:T(8,128)S(1)}, u32[]{:S(2)}, u32[]{:S(2)}) collective-permute-start(f32[2,32,128]{2,1,0:T(8,128)S(1)} %get-tuple-element.150), channel_id=1, source_target_pairs={{0,8},{8,16},{16,24},{1,9},{9,17},{17,25},{2,10},{10,18},{18,26},{... | collective-permute-start | bytes 98312 | tf_op jit(solution)/shard_map/ppermute | solution.py:21
  397.6 3.0 collective-permute-start.38
  404.8 8.1 %collective-permute-done.40 = f32[20,36,2]{2,1,0:T(8,128)S(1)} collective-permute-done((f32[20,36,2]{2,1,0:T(8,128)S(1)}, f32[20,36,2]{2,1,0:T(8,128)S(1)}, u32[]{:S(2)}, u32[]{:S(2)}) %collective-permute-start.40) | collective-permute-done | bytes 5792 | tf_op jit(solution)/shard_map/ppermute | solution.py:21
  412.8 4.1 collective-permute-done.41
  427.2 3.4 all-to-all-start.5
  433.0 43.1 %all-reduce = (f32[1]{0:T(128)}, f32[1]{0:T(128)}) all-reduce(f32[1]{0:T(128)} %bitcast.40, f32[1]{0:T(128)} %bitcast.39), channel_id=1, replica_groups=mesh['gx'=4,'gy'=4,'gz'=2] {'gx','gy','gz'}, use_global_device_ids=true, to_apply=%region_10.11 | all-reduce | flops 2 | bytes 16 | tf_op jit(solution)/shard_map/psum | solution.py:187
  478.9 9.5 %broadcast_in_dim.335 = f32[4,16,2,16,2,16,2]{0,6,5,4,3,2,1:T(2,128)} broadcast(f32[4,16,16,16]{0,3,2,1:T(8,128)S(1)} %bitcast.134), dimensions={0,1,3,5} | broadcast | bytes 589824 | tf_op jit(solution)/shard_map/broadcast_in_dim | solution.py:47
  488.3 9.5 %copy.647 = f32[4,32768]{1,0:T(4,128)S(1)} copy(f32[4,32768]{0,1:T(8,128)} %bitcast.131) | data formatting | bytes 1048576 | tf_op jit(solution)/shard_map/reshape | solution.py:48
  (319 shorter events, 121.2 us)
Async XLA Ops:
  0.6 23.3 %copy-start.2 = (f32[4,32768]{1,0:T(4,128)S(1)}, f32[4,32768]{1,0:T(4,128)}, u32[]{:S(2)}) copy-start(f32[4,32768]{1,0:T(4,128)} %param.13) | copy-start | bytes 1572868
  2.1 41.1 %collective-permute-start = (f32[2,32,128]{2,1,0:T(8,128)}, f32[2,32,128]{2,1,0:T(8,128)S(1)}, u32[]{:S(2)}, u32[]{:S(2)}) collective-permute-start(f32[2,32,128]{2,1,0:T(8,128)} %get-tuple-element.163), channel_id=1, source_target_pairs={{0,8},{8,16},{16,24},{1,9},{9,17},{17,25},{2,10},{10,18},{18,26},{... | collective-permute-start | bytes 98312 | tf_op jit(solution)/shard_map/ppermute | solution.py:21
  7.0 36.2 %collective-permute-start.1 = (f32[2,32,128]{2,1,0:T(8,128)}, f32[2,32,128]{2,1,0:T(8,128)S(1)}, u32[]{:S(2)}, u32[]{:S(2)}) collective-permute-start(f32[2,32,128]{2,1,0:T(8,128)} %get-tuple-element.162), channel_id=1, source_target_pairs={{8,0},{16,8},{24,16},{9,1},{17,9},{25,17},{10,2},{18,10},{26,18},{... | collective-permute-start | bytes 98312 | tf_op jit(solution)/shard_map/ppermute | solution.py:24
  10.4 26.3 %all-to-all-start = ((f32[8,1,1]{2,1,0:T(1,128)}), f32[8,1,1]{2,1,0:T(1,128)S(1)}, u32[]{:S(2)}, u32[]{:S(2)}) async-start(f32[8,1,1]{2,1,0:T(1,128)} %copy.577), calls=%async_computation | async-start | bytes 8192 | tf_op jit(solution)/shard_map/all_to_all | solution.py:136
  15.7 31.9 %collective-permute-start.13 = (f32[2,32,128]{2,1,0:T(8,128)}, f32[2,32,128]{2,1,0:T(8,128)S(1)}, u32[]{:S(2)}, u32[]{:S(2)}) collective-permute-start(f32[2,32,128]{2,1,0:T(8,128)} %get-tuple-element.159), channel_id=1, source_target_pairs={{8,0},{16,8},{24,16},{9,1},{17,9},{25,17},{10,2},{18,10},{26,18},{... | collective-permute-start | bytes 98312 | tf_op jit(solution)/shard_map/ppermute | solution.py:24
  17.0 30.7 %collective-permute-start.12 = (f32[2,32,128]{2,1,0:T(8,128)}, f32[2,32,128]{2,1,0:T(8,128)S(1)}, u32[]{:S(2)}, u32[]{:S(2)}) collective-permute-start(f32[2,32,128]{2,1,0:T(8,128)} %get-tuple-element.158), channel_id=1, source_target_pairs={{0,8},{8,16},{16,24},{1,9},{9,17},{17,25},{2,10},{10,18},{18,26},{... | collective-permute-start | bytes 98312 | tf_op jit(solution)/shard_map/ppermute | solution.py:21
  37.3 18.0 %all-to-all-start.1 = ((f32[8,1,4096]{2,1,0:T(1,128)}), f32[8,1,4096]{2,1,0:T(1,128)S(1)}, u32[]{:S(2)}, u32[]{:S(2)}) async-start(f32[8,1,4096]{2,1,0:T(1,128)} %copy.579), calls=%async_computation.1 | async-start | bytes 262144 | tf_op jit(solution)/shard_map/all_to_all | solution.py:135
  43.3 11.2 %collective-permute-start.3 = (f32[20,2,128]{2,1,0:T(2,128)S(1)}, f32[20,2,128]{2,1,0:T(2,128)S(1)}, u32[]{:S(2)}, u32[]{:S(2)}) collective-permute-start(f32[20,2,128]{2,1,0:T(2,128)S(1)} %get-tuple-element.149), channel_id=1, source_target_pairs={{2,0},{4,2},{6,4},{3,1},{5,3},{7,5},{10,8},{12,10},{14,12},{11,9},... | collective-permute-start | bytes 61448 | tf_op jit(solution)/shard_map/ppermute | solution.py:24
  44.6 9.9 %collective-permute-start.2 = (f32[20,2,128]{2,1,0:T(2,128)S(1)}, f32[20,2,128]{2,1,0:T(2,128)S(1)}, u32[]{:S(2)}, u32[]{:S(2)}) collective-permute-start(f32[20,2,128]{2,1,0:T(2,128)S(1)} %get-tuple-element.148), channel_id=1, source_target_pairs={{0,2},{2,4},{4,6},{1,3},{3,5},{5,7},{8,10},{10,12},{12,14},{9,11},... | collective-permute-start | bytes 61448 | tf_op jit(solution)/shard_map/ppermute | solution.py:21
  47.7 94.5 %copy-start.20 = (f32[2,32,128]{2,1,0:T(8,128)}, f32[2,32,128]{2,1,0:T(8,128)S(1)}, u32[]{:S(2)}) copy-start(f32[2,32,128]{2,1,0:T(8,128)S(1)} %collective-permute-done.13) | copy-start | bytes 98308
  47.7 94.5 %copy-start.22 = (f32[2,32,128]{2,1,0:T(8,128)}, f32[2,32,128]{2,1,0:T(8,128)S(1)}, u32[]{:S(2)}) copy-start(f32[2,32,128]{2,1,0:T(8,128)S(1)} %collective-permute-done.12) | copy-start | bytes 98308
  48.3 89.2 %collective-permute-start.15 = (f32[20,2,128]{2,1,0:T(2,128)}, f32[20,2,128]{2,1,0:T(2,128)}, u32[]{:S(2)}, u32[]{:S(2)}) collective-permute-start(f32[20,2,128]{2,1,0:T(2,128)} %get-tuple-element.145), channel_id=1, source_target_pairs={{2,0},{4,2},{6,4},{3,1},{5,3},{7,5},{10,8},{12,10},{14,12},{11,9},... | collective-permute-start | bytes 61448 | tf_op jit(solution)/shard_map/ppermute | solution.py:24
  49.6 92.5 %collective-permute-start.14 = (f32[20,2,128]{2,1,0:T(2,128)}, f32[20,2,128]{2,1,0:T(2,128)}, u32[]{:S(2)}, u32[]{:S(2)}) collective-permute-start(f32[20,2,128]{2,1,0:T(2,128)} %get-tuple-element.144), channel_id=1, source_target_pairs={{0,2},{2,4},{4,6},{1,3},{3,5},{5,7},{8,10},{10,12},{12,14},{9,11},... | collective-permute-start | bytes 61448 | tf_op jit(solution)/shard_map/ppermute | solution.py:21
  117.0 10.7 %all-to-all-start.2 = ((f32[8,1,4096]{2,1,0:T(1,128)}), f32[8,1,4096]{2,1,0:T(1,128)S(1)}, u32[]{:S(2)}, u32[]{:S(2)}) async-start(f32[8,1,4096]{2,1,0:T(1,128)} %copy.606), calls=%async_computation.2 | async-start | bytes 262144 | tf_op jit(solution)/shard_map/all_to_all | solution.py:170
  122.0 34.8 %collective-permute-start.4 = (f32[20,36,2]{2,1,0:T(8,128)}, f32[20,36,2]{2,1,0:T(8,128)}, u32[]{:S(2)}, u32[]{:S(2)}) collective-permute-start(f32[20,36,2]{2,1,0:T(8,128)} %get-tuple-element.135), channel_id=1, source_target_pairs={{0,1},{2,3},{4,5},{6,7},{8,9},{10,11},{12,13},{14,15},{16,17},{18,... | collective-permute-start | bytes 17288 | tf_op jit(solution)/shard_map/ppermute | solution.py:21
  126.4 35.0 %collective-permute-start.5 = (f32[20,36,2]{2,1,0:T(8,128)}, f32[20,36,2]{2,1,0:T(8,128)}, u32[]{:S(2)}, u32[]{:S(2)}) collective-permute-start(f32[20,36,2]{2,1,0:T(8,128)} %get-tuple-element.134), channel_id=1, source_target_pairs={{1,0},{3,2},{5,4},{7,6},{9,8},{11,10},{13,12},{15,14},{17,16},{19,... | collective-permute-start | bytes 17288 | tf_op jit(solution)/shard_map/ppermute | solution.py:24
  136.3 6.7 %collective-permute-start.7 = (f32[2,32,128]{2,1,0:T(8,128)S(1)}, f32[2,32,128]{2,1,0:T(8,128)S(1)}, u32[]{:S(2)}, u32[]{:S(2)}) collective-permute-start(f32[2,32,128]{2,1,0:T(8,128)S(1)} %get-tuple-element.161), channel_id=1, source_target_pairs={{8,0},{16,8},{24,16},{9,1},{17,9},{25,17},{10,2},{18,10},{26,18},{... | collective-permute-start | bytes 98312 | tf_op jit(solution)/shard_map/ppermute | solution.py:24
  137.6 6.1 %collective-permute-start.6 = (f32[2,32,128]{2,1,0:T(8,128)S(1)}, f32[2,32,128]{2,1,0:T(8,128)S(1)}, u32[]{:S(2)}, u32[]{:S(2)}) collective-permute-start(f32[2,32,128]{2,1,0:T(8,128)S(1)} %get-tuple-element.160), channel_id=1, source_target_pairs={{0,8},{8,16},{16,24},{1,9},{9,17},{17,25},{2,10},{10,18},{18,26},{... | collective-permute-start | bytes 98312 | tf_op jit(solution)/shard_map/ppermute | solution.py:21
  143.7 17.7 %copy-start.10 = (f32[20,32,128]{2,1,0:T(8,128)S(1)}, f32[20,32,128]{2,1,0:T(8,128)}, u32[]{:S(2)}) copy-start(f32[20,32,128]{2,1,0:T(8,128)} %copy-done.9) | copy-start | bytes 983044
  143.8 17.7 %copy-start.25 = (f32[20,2,128]{2,1,0:T(2,128)S(1)}, f32[20,2,128]{2,1,0:T(2,128)}, u32[]{:S(2)}) copy-start(f32[20,2,128]{2,1,0:T(2,128)} %copy-done.24) | copy-start | bytes 61444
  143.8 17.7 %copy-start.27 = (f32[20,2,128]{2,1,0:T(2,128)S(1)}, f32[20,2,128]{2,1,0:T(2,128)}, u32[]{:S(2)}) copy-start(f32[20,2,128]{2,1,0:T(2,128)} %copy-done.26) | copy-start | bytes 61444
  143.8 6.0 %collective-permute-start.9 = (f32[20,2,128]{2,1,0:T(2,128)S(1)}, f32[20,2,128]{2,1,0:T(2,128)S(1)}, u32[]{:S(2)}, u32[]{:S(2)}) collective-permute-start(f32[20,2,128]{2,1,0:T(2,128)S(1)} %get-tuple-element.147), channel_id=1, source_target_pairs={{2,0},{4,2},{6,4},{3,1},{5,3},{7,5},{10,8},{12,10},{14,12},{11,9},... | collective-permute-start | bytes 61448 | tf_op jit(solution)/shard_map/ppermute | solution.py:24
  145.2 10.0 %collective-permute-start.8 = (f32[20,2,128]{2,1,0:T(2,128)S(1)}, f32[20,2,128]{2,1,0:T(2,128)S(1)}, u32[]{:S(2)}, u32[]{:S(2)}) collective-permute-start(f32[20,2,128]{2,1,0:T(2,128)S(1)} %get-tuple-element.146), channel_id=1, source_target_pairs={{0,2},{2,4},{4,6},{1,3},{3,5},{5,7},{8,10},{10,12},{12,14},{9,11},... | collective-permute-start | bytes 61448 | tf_op jit(solution)/shard_map/ppermute | solution.py:21
  148.4 14.6 %collective-permute-start.17 = (f32[20,36,2]{2,1,0:T(8,128)S(1)}, f32[20,36,2]{2,1,0:T(8,128)S(1)}, u32[]{:S(2)}, u32[]{:S(2)}) collective-permute-start(f32[20,36,2]{2,1,0:T(8,128)S(1)} %get-tuple-element.131), channel_id=1, source_target_pairs={{1,0},{3,2},{5,4},{7,6},{9,8},{11,10},{13,12},{15,14},{17,16},{19,... | collective-permute-start | bytes 17288 | tf_op jit(solution)/shard_map/ppermute | solution.py:24
  149.7 24.0 %copy-start.21 = (f32[2,32,128]{2,1,0:T(8,128)S(1)}, f32[2,32,128]{2,1,0:T(8,128)}, u32[]{:S(2)}) copy-start(f32[2,32,128]{2,1,0:T(8,128)} %copy-done.20) | copy-start | bytes 98308
  149.8 24.0 %copy-start.23 = (f32[2,32,128]{2,1,0:T(8,128)S(1)}, f32[2,32,128]{2,1,0:T(8,128)}, u32[]{:S(2)}) copy-start(f32[2,32,128]{2,1,0:T(8,128)} %copy-done.22) | copy-start | bytes 98308
  149.8 15.2 %collective-permute-start.16 = (f32[20,36,2]{2,1,0:T(8,128)S(1)}, f32[20,36,2]{2,1,0:T(8,128)S(1)}, u32[]{:S(2)}, u32[]{:S(2)}) collective-permute-start(f32[20,36,2]{2,1,0:T(8,128)S(1)} %get-tuple-element.130), channel_id=1, source_target_pairs={{0,1},{2,3},{4,5},{6,7},{8,9},{10,11},{12,13},{14,15},{16,17},{18,... | collective-permute-start | bytes 17288 | tf_op jit(solution)/shard_map/ppermute | solution.py:21
  155.5 16.3 %collective-permute-start.11 = (f32[20,36,2]{2,1,0:T(8,128)S(1)}, f32[20,36,2]{2,1,0:T(8,128)S(1)}, u32[]{:S(2)}, u32[]{:S(2)}) collective-permute-start(f32[20,36,2]{2,1,0:T(8,128)S(1)} %get-tuple-element.133), channel_id=1, source_target_pairs={{1,0},{3,2},{5,4},{7,6},{9,8},{11,10},{13,12},{15,14},{17,16},{19,... | collective-permute-start | bytes 17288 | tf_op jit(solution)/shard_map/ppermute | solution.py:24
  156.8 16.9 %collective-permute-start.10 = (f32[20,36,2]{2,1,0:T(8,128)S(1)}, f32[20,36,2]{2,1,0:T(8,128)S(1)}, u32[]{:S(2)}, u32[]{:S(2)}) collective-permute-start(f32[20,36,2]{2,1,0:T(8,128)S(1)} %get-tuple-element.132), channel_id=1, source_target_pairs={{0,1},{2,3},{4,5},{6,7},{8,9},{10,11},{12,13},{14,15},{16,17},{18,... | collective-permute-start | bytes 17288 | tf_op jit(solution)/shard_map/ppermute | solution.py:21
  163.1 15.8 %copy-start.3 = (f32[16,32,128]{2,1,0:T(8,128)S(1)}, f32[16,32,128]{2,1,0:T(8,128)}, u32[]{:S(2)}) copy-start(f32[16,32,128]{2,1,0:T(8,128)} %param.9) | copy-start | bytes 786436
  178.9 32.1 %copy-start.4 = (f32[18,34,130]{2,1,0:T(8,128)}, f32[18,34,130]{2,1,0:T(8,128)S(1)}, u32[]{:S(2)}) copy-start(f32[18,34,130]{2,1,0:T(8,128)S(1)} %get-tuple-element.25) | copy-start | bytes 954724
  179.4 6.2 %collective-permute-start.19 = (f32[2,32,128]{2,1,0:T(8,128)S(1)}, f32[2,32,128]{2,1,0:T(8,128)S(1)}, u32[]{:S(2)}, u32[]{:S(2)}) collective-permute-start(f32[2,32,128]{2,1,0:T(8,128)S(1)} %get-tuple-element.157), channel_id=1, source_target_pairs={{8,0},{16,8},{24,16},{9,1},{17,9},{25,17},{10,2},{18,10},{26,18},{... | collective-permute-start | bytes 98312 | tf_op jit(solution)/shard_map/ppermute | solution.py:24
  180.7 6.4 %collective-permute-start.18 = (f32[2,32,128]{2,1,0:T(8,128)S(1)}, f32[2,32,128]{2,1,0:T(8,128)S(1)}, u32[]{:S(2)}, u32[]{:S(2)}) collective-permute-start(f32[2,32,128]{2,1,0:T(8,128)S(1)} %get-tuple-element.156), channel_id=1, source_target_pairs={{0,8},{8,16},{16,24},{1,9},{9,17},{17,25},{2,10},{10,18},{18,26},{... | collective-permute-start | bytes 98312 | tf_op jit(solution)/shard_map/ppermute | solution.py:21
  187.1 4.3 collective-permute-start.21
  188.4 3.9 collective-permute-start.20
  192.5 13.8 %collective-permute-start.22 = (f32[20,36,2]{2,1,0:T(8,128)S(1)}, f32[20,36,2]{2,1,0:T(8,128)S(1)}, u32[]{:S(2)}, u32[]{:S(2)}) collective-permute-start(f32[20,36,2]{2,1,0:T(8,128)S(1)} %get-tuple-element.129), channel_id=1, source_target_pairs={{0,1},{2,3},{4,5},{6,7},{8,9},{10,11},{12,13},{14,15},{16,17},{18,... | collective-permute-start | bytes 17288 | tf_op jit(solution)/shard_map/ppermute | solution.py:21
  197.0 13.5 %collective-permute-start.23 = (f32[20,36,2]{2,1,0:T(8,128)S(1)}, f32[20,36,2]{2,1,0:T(8,128)S(1)}, u32[]{:S(2)}, u32[]{:S(2)}) collective-permute-start(f32[20,36,2]{2,1,0:T(8,128)S(1)} %get-tuple-element.128), channel_id=1, source_target_pairs={{1,0},{3,2},{5,4},{7,6},{9,8},{11,10},{13,12},{15,14},{17,16},{19,... | collective-permute-start | bytes 17288 | tf_op jit(solution)/shard_map/ppermute | solution.py:24
  219.4 15.0 %copy-start.17 = (f32[4,4096]{1,0:T(4,128)S(1)}, f32[4,4096]{1,0:T(4,128)}, u32[]{:S(2)}) copy-start(f32[4,4096]{1,0:T(4,128)} %copy-done.16) | copy-start | bytes 196612
  219.4 15.0 %copy-start.35 = (f32[8]{0:T(128)S(1)}, f32[8]{0:T(128)}, u32[]{:S(2)}) copy-start(f32[8]{0:T(128)} %copy-done.33) | copy-start | bytes 100
  219.4 15.0 %copy-start.40 = (f32[8]{0:T(128)S(1)}, f32[8]{0:T(128)}, u32[]{:S(2)}) copy-start(f32[8]{0:T(128)} %copy-done.38) | copy-start | bytes 100
  223.7 10.7 %all-to-all-start.3 = ((f32[8,1,4096]{2,1,0:T(1,128)}), f32[8,1,4096]{2,1,0:T(1,128)S(1)}, u32[]{:S(2)}, u32[]{:S(2)}) async-start(f32[8,1,4096]{2,1,0:T(1,128)} %copy.611), calls=%async_computation.3 | async-start | bytes 262144 | tf_op jit(solution)/shard_map/all_to_all | solution.py:135
  227.7 104.7 %collective-permute-start.25 = (f32[2,32,128]{2,1,0:T(8,128)}, f32[2,32,128]{2,1,0:T(8,128)}, u32[]{:S(2)}, u32[]{:S(2)}) collective-permute-start(f32[2,32,128]{2,1,0:T(8,128)} %get-tuple-element.155), channel_id=1, source_target_pairs={{8,0},{16,8},{24,16},{9,1},{17,9},{25,17},{10,2},{18,10},{26,18},{... | collective-permute-start | bytes 98312 | tf_op jit(solution)/shard_map/ppermute | solution.py:24
  229.0 103.4 %collective-permute-start.24 = (f32[2,32,128]{2,1,0:T(8,128)}, f32[2,32,128]{2,1,0:T(8,128)}, u32[]{:S(2)}, u32[]{:S(2)}) collective-permute-start(f32[2,32,128]{2,1,0:T(8,128)} %get-tuple-element.154), channel_id=1, source_target_pairs={{0,8},{8,16},{16,24},{1,9},{9,17},{17,25},{2,10},{10,18},{18,26},{... | collective-permute-start | bytes 98312 | tf_op jit(solution)/shard_map/ppermute | solution.py:21
  309.9 13.9 %copy-start.50 = (f32[4]{0:T(128)S(1)}, f32[4]{0:T(128)}, u32[]{:S(2)}) copy-start(f32[4]{0:T(128)} %broadcast_multiply_fusion) | copy-start | bytes 52
  328.2 9.3 %all-to-all-start.4 = ((f32[8,1,4096]{2,1,0:T(1,128)}), f32[8,1,4096]{2,1,0:T(1,128)S(1)}, u32[]{:S(2)}, u32[]{:S(2)}) async-start(f32[8,1,4096]{2,1,0:T(1,128)} %copy.640), calls=%async_computation.4 | async-start | bytes 262144 | tf_op jit(solution)/shard_map/all_to_all | solution.py:170
  333.2 18.8 %collective-permute-start.27 = (f32[20,2,128]{2,1,0:T(2,128)S(1)}, f32[20,2,128]{2,1,0:T(2,128)S(1)}, u32[]{:S(2)}, u32[]{:S(2)}) collective-permute-start(f32[20,2,128]{2,1,0:T(2,128)S(1)} %get-tuple-element.141), channel_id=1, source_target_pairs={{2,0},{4,2},{6,4},{3,1},{5,3},{7,5},{10,8},{12,10},{14,12},{11,9},... | collective-permute-start | bytes 61448 | tf_op jit(solution)/shard_map/ppermute | solution.py:24
  334.5 17.5 %collective-permute-start.26 = (f32[20,2,128]{2,1,0:T(2,128)S(1)}, f32[20,2,128]{2,1,0:T(2,128)S(1)}, u32[]{:S(2)}, u32[]{:S(2)}) collective-permute-start(f32[20,2,128]{2,1,0:T(2,128)S(1)} %get-tuple-element.140), channel_id=1, source_target_pairs={{0,2},{2,4},{4,6},{1,3},{3,5},{5,7},{8,10},{10,12},{12,14},{9,11},... | collective-permute-start | bytes 61448 | tf_op jit(solution)/shard_map/ppermute | solution.py:21
  346.1 6.7 %collective-permute-start.31 = (f32[2,32,128]{2,1,0:T(8,128)S(1)}, f32[2,32,128]{2,1,0:T(8,128)S(1)}, u32[]{:S(2)}, u32[]{:S(2)}) collective-permute-start(f32[2,32,128]{2,1,0:T(8,128)S(1)} %get-tuple-element.153), channel_id=1, source_target_pairs={{8,0},{16,8},{24,16},{9,1},{17,9},{25,17},{10,2},{18,10},{26,18},{... | collective-permute-start | bytes 98312 | tf_op jit(solution)/shard_map/ppermute | solution.py:24
  347.4 6.1 %collective-permute-start.30 = (f32[2,32,128]{2,1,0:T(8,128)S(1)}, f32[2,32,128]{2,1,0:T(8,128)S(1)}, u32[]{:S(2)}, u32[]{:S(2)}) collective-permute-start(f32[2,32,128]{2,1,0:T(8,128)S(1)} %get-tuple-element.152), channel_id=1, source_target_pairs={{0,8},{8,16},{16,24},{1,9},{9,17},{17,25},{2,10},{10,18},{18,26},{... | collective-permute-start | bytes 98312 | tf_op jit(solution)/shard_map/ppermute | solution.py:21
  353.5 10.0 %collective-permute-start.33 = (f32[20,2,128]{2,1,0:T(2,128)S(1)}, f32[20,2,128]{2,1,0:T(2,128)S(1)}, u32[]{:S(2)}, u32[]{:S(2)}) collective-permute-start(f32[20,2,128]{2,1,0:T(2,128)S(1)} %get-tuple-element.139), channel_id=1, source_target_pairs={{2,0},{4,2},{6,4},{3,1},{5,3},{7,5},{10,8},{12,10},{14,12},{11,9},... | collective-permute-start | bytes 61448 | tf_op jit(solution)/shard_map/ppermute | solution.py:24
  354.8 8.7 %collective-permute-start.32 = (f32[20,2,128]{2,1,0:T(2,128)S(1)}, f32[20,2,128]{2,1,0:T(2,128)S(1)}, u32[]{:S(2)}, u32[]{:S(2)}) collective-permute-start(f32[20,2,128]{2,1,0:T(2,128)S(1)} %get-tuple-element.138), channel_id=1, source_target_pairs={{0,2},{2,4},{4,6},{1,3},{3,5},{5,7},{8,10},{10,12},{12,14},{9,11},... | collective-permute-start | bytes 61448 | tf_op jit(solution)/shard_map/ppermute | solution.py:21
  358.1 13.2 %collective-permute-start.28 = (f32[20,36,2]{2,1,0:T(8,128)S(1)}, f32[20,36,2]{2,1,0:T(8,128)S(1)}, u32[]{:S(2)}, u32[]{:S(2)}) collective-permute-start(f32[20,36,2]{2,1,0:T(8,128)S(1)} %get-tuple-element.127), channel_id=1, source_target_pairs={{0,1},{2,3},{4,5},{6,7},{8,9},{10,11},{12,13},{14,15},{16,17},{18,... | collective-permute-start | bytes 17288 | tf_op jit(solution)/shard_map/ppermute | solution.py:21
  362.1 22.9 %copy-start.5 = (f32[18,34,130]{2,1,0:T(8,128)S(1)}, f32[18,34,130]{2,1,0:T(8,128)}, u32[]{:S(2)}) copy-start(f32[18,34,130]{2,1,0:T(8,128)} %copy-done.4) | copy-start | bytes 954724
  362.1 14.1 %collective-permute-start.29 = (f32[20,36,2]{2,1,0:T(8,128)S(1)}, f32[20,36,2]{2,1,0:T(8,128)S(1)}, u32[]{:S(2)}, u32[]{:S(2)}) collective-permute-start(f32[20,36,2]{2,1,0:T(8,128)S(1)} %get-tuple-element.126), channel_id=1, source_target_pairs={{1,0},{3,2},{5,4},{7,6},{9,8},{11,10},{13,12},{15,14},{17,16},{19,... | collective-permute-start | bytes 17288 | tf_op jit(solution)/shard_map/ppermute | solution.py:24
  363.8 21.2 %collective-permute-start.35 = (f32[20,36,2]{2,1,0:T(8,128)S(1)}, f32[20,36,2]{2,1,0:T(8,128)S(1)}, u32[]{:S(2)}, u32[]{:S(2)}) collective-permute-start(f32[20,36,2]{2,1,0:T(8,128)S(1)} %get-tuple-element.125), channel_id=1, source_target_pairs={{1,0},{3,2},{5,4},{7,6},{9,8},{11,10},{13,12},{15,14},{17,16},{19,... | collective-permute-start | bytes 17288 | tf_op jit(solution)/shard_map/ppermute | solution.py:24
  365.1 19.9 %collective-permute-start.34 = (f32[20,36,2]{2,1,0:T(8,128)S(1)}, f32[20,36,2]{2,1,0:T(8,128)S(1)}, u32[]{:S(2)}, u32[]{:S(2)}) collective-permute-start(f32[20,36,2]{2,1,0:T(8,128)S(1)} %get-tuple-element.124), channel_id=1, source_target_pairs={{0,1},{2,3},{4,5},{6,7},{8,9},{10,11},{12,13},{14,15},{16,17},{18,... | collective-permute-start | bytes 17288 | tf_op jit(solution)/shard_map/ppermute | solution.py:21
  388.2 6.5 %collective-permute-start.37 = (f32[2,32,128]{2,1,0:T(8,128)S(1)}, f32[2,32,128]{2,1,0:T(8,128)S(1)}, u32[]{:S(2)}, u32[]{:S(2)}) collective-permute-start(f32[2,32,128]{2,1,0:T(8,128)S(1)} %get-tuple-element.151), channel_id=1, source_target_pairs={{8,0},{16,8},{24,16},{9,1},{17,9},{25,17},{10,2},{18,10},{26,18},{... | collective-permute-start | bytes 98312 | tf_op jit(solution)/shard_map/ppermute | solution.py:24
  389.5 6.8 %collective-permute-start.36 = (f32[2,32,128]{2,1,0:T(8,128)S(1)}, f32[2,32,128]{2,1,0:T(8,128)S(1)}, u32[]{:S(2)}, u32[]{:S(2)}) collective-permute-start(f32[2,32,128]{2,1,0:T(8,128)S(1)} %get-tuple-element.150), channel_id=1, source_target_pairs={{0,8},{8,16},{16,24},{1,9},{9,17},{17,25},{2,10},{10,18},{18,26},{... | collective-permute-start | bytes 98312 | tf_op jit(solution)/shard_map/ppermute | solution.py:21
  396.3 4.3 collective-permute-start.39
  397.6 3.9 collective-permute-start.38
  401.7 11.1 %collective-permute-start.40 = (f32[20,36,2]{2,1,0:T(8,128)S(1)}, f32[20,36,2]{2,1,0:T(8,128)S(1)}, u32[]{:S(2)}, u32[]{:S(2)}) collective-permute-start(f32[20,36,2]{2,1,0:T(8,128)S(1)} %get-tuple-element.123), channel_id=1, source_target_pairs={{0,1},{2,3},{4,5},{6,7},{8,9},{10,11},{12,13},{14,15},{16,17},{18,... | collective-permute-start | bytes 17288 | tf_op jit(solution)/shard_map/ppermute | solution.py:21
  403.2 13.8 %collective-permute-start.41 = (f32[20,36,2]{2,1,0:T(8,128)S(1)}, f32[20,36,2]{2,1,0:T(8,128)S(1)}, u32[]{:S(2)}, u32[]{:S(2)}) collective-permute-start(f32[20,36,2]{2,1,0:T(8,128)S(1)} %get-tuple-element.122), channel_id=1, source_target_pairs={{1,0},{3,2},{5,4},{7,6},{9,8},{11,10},{13,12},{15,14},{17,16},{19,... | collective-permute-start | bytes 17288 | tf_op jit(solution)/shard_map/ppermute | solution.py:24
  424.6 53.3 %copy-start.19 = (f32[4,4096]{1,0:T(4,128)S(1)}, f32[4,4096]{1,0:T(4,128)}, u32[]{:S(2)}) copy-start(f32[4,4096]{1,0:T(4,128)} %get-tuple-element.165) | copy-start | bytes 196612
  427.2 50.7 %all-to-all-start.5 = ((f32[8,1,4096]{2,1,0:T(1,128)}), f32[8,1,4096]{2,1,0:T(1,128)S(1)}, u32[]{:S(2)}, u32[]{:S(2)}) async-start(f32[8,1,4096]{2,1,0:T(1,128)} %copy.645), calls=%async_computation.5 | async-start | bytes 262144 | tf_op jit(solution)/shard_map/all_to_all | solution.py:135
  (37 other events, 227.0 us)
where the time goes:
time: 507 us; the launch traced here: 499 us
  local copies, waits for them, and re-layouts  159 us (31%)
  starting transfers between devices  138 us (27%)
  other arithmetic  86.4 us (17%)
  waiting for transfers between devices  54.9 us (11%)
  blocking collectives  43.1 us (9%)
  matrix products  13.1 us (3%)
  between operations  5.18 us (1%)
    ppermute x21, starting transfers between devices, extended(): lax.ppermute(lax.slice_in_dim(block, block.shape[dim] - width, None, axis...  86.7 us
    broadcast_in_dim x8, local copies, waits for them, and re-layouts, inject(): spread = jnp.broadcast_to(shaped, (number, FOOT, 2, FOOT, 2, FOOT, 2))  45.1 us
    psum x1, blocking collectives, local(): norms.append(lax.psum(local_sum, ('gx', 'gy', 'gz')))  43.1 us
    reshape x4, local copies, waits for them, and re-layouts, inject(): return spread.reshape(number, 8 * FOOT * FOOT * FOOT)  38 us
    ppermute x21, starting transfers between devices, extended(): lax.ppermute(lax.slice_in_dim(block, 0, width, axis=dim), axis, backward)  28.1 us
    ppermute x21, waiting for transfers between devices, extended(): lax.ppermute(lax.slice_in_dim(block, 0, width, axis=dim), axis, backward)  27.5 us
    reduce_sum x2, other arithmetic, restrict(): return values.reshape(number, FOOT, 2, FOOT, 2, FOOT, 2).mean(axis=(2, 4,...  27.5 us
    ppermute x21, waiting for transfers between devices, extended(): lax.ppermute(lax.slice_in_dim(block, block.shape[dim] - width, None, axis...  27.3 us
  transfers between devices with their start and end apart: 48, of which 16 were waited for; matrix products, arithmetic and copies ran while one was open for 41% of the time, Pallas kernels for 0%

commit v1 on v0

v1 whole, which is shorter than its diff:
```python
import jax
import jax.numpy as jnp
from jax import lax
from jax.experimental import pallas as pl
from jax.experimental.pallas import tpu as pltpu
from jax.sharding import PartitionSpec as P

FOOT = 16
CYCLES = 2
CSWEEPS = 4
FSWEEPS = 3
OMEGA = 0.8

SUB = 8
LANES = 128
SIDE = 2 * FOOT
WIDE = 4
GROUP_AXES = ("gy", "gz")

VMEM = pl.BlockSpec(memory_space=pltpu.VMEM)
SMEM = pl.BlockSpec(memory_space=pltpu.SMEM)
F32 = jnp.float32


def out(*shape, dtype=F32):
    return jax.ShapeDtypeStruct(shape, dtype)


def call(body, name, ins, outs, scratch=(), flops=0):
    return pl.pallas_call(
        body,
        name=name,
        in_specs=[spec for spec, _ in ins],
        out_specs=[spec for spec, _ in outs],
        out_shape=[shape for _, shape in outs],
        scratch_shapes=list(scratch),
        cost_estimate=pl.CostEstimate(flops=flops, transcendentals=0, bytes_accessed=0),
    )(*[value for _, value in ins])


def lane_id():
    return lax.broadcasted_iota(jnp.int32, (SUB, LANES), 1)


def sub_id():
    return lax.broadcasted_iota(jnp.int32, (SUB, LANES), 0)


def gather(values, index, axis):
    return jnp.take_along_axis(values, index, axis=axis)


def swap_pairs(count):
    first = [(i, i ^ 1) for i in range(count)]
    second = [(i, (i + 1) % count if i % 2 else (i - 1) % count) for i in range(count)]
    return first, second


def swap(axis, first, second):
    count = lax.axis_size(axis)
    pairs_a, pairs_b = swap_pairs(count)
    got_a = lax.ppermute(first, axis, pairs_a)
    got_b = lax.ppermute(second, axis, pairs_b) if count > 2 else got_a
    return got_a, got_b


def pick_low(odd, got_a, got_b):
    return jnp.where(odd, got_a, got_b)


def pick_high(odd, got_a, got_b):
    return jnp.where(odd, got_b, got_a)


def extract(field, write, block_x, block_y, block_z):
    lanes = lane_id() // FOOT
    for quad in range(FOOT // 4):
        packed = None
        for inner in range(4):
            for part in range(FOOT // SUB):
                piece = field[FOOT * block_x + 4 * quad + inner, block_y * (FOOT // SUB) + part]
                spot = 2 * inner + part
                piece = pltpu.roll(piece, (FOOT * spot + LANES - FOOT * block_z) % LANES, 1)
                packed = piece if packed is None else jnp.where(lanes == spot, piece, packed)
        write(quad, packed)


def send_start_body(dims):
    ex, nt, group, slots, nbx, nby, nbz = dims

    def body(pos, corner, owner, start, shift, source, send, side_a, side_b):
        odd = pos[0] % 2 == 1
        for index, field in enumerate((start, shift, source)):
            low = field[0:WIDE]
            high = field[ex - WIDE : ex]
            side_a[index] = jnp.where(odd, low, high)
            side_b[index] = jnp.where(odd, high, low)
        lanes = lane_id()
        note = jnp.zeros((SUB, LANES), F32)
        blocks = []
        for slot in range(slots):
            block = (
                corner[0, slot, 0] // SIDE - pos[0] * nbx,
                corner[0, slot, 1] // SIDE - pos[1] * nby,
                corner[0, slot, 2] // SIDE - pos[2] * nbz,
            )
            blocks.append(block)
            for index, value in enumerate((owner[0, slot],) + block):
                note = jnp.where(lanes == 4 * slot + index, value.astype(F32), note)
        for target in range(group):
            send[target, 0:4] = jnp.zeros((4, SUB, LANES), F32)
            send[target, 4] = note
        for slot in range(slots):
            target = owner[0, slot]

            @pl.when(target < group)
            def _():
                def write(quad, packed):
                    send[target, quad] = packed

                extract(start, write, *blocks[slot])

    return body


def x_plane(field, got_a, got_b, odd, ex, xi):
    if xi < WIDE:
        return pick_low(odd, got_a[xi], got_b[xi])
    if xi < ex + WIDE:
        return field[xi - WIDE]
    return pick_high(odd, got_a[xi - ex - WIDE], got_b[xi - ex - WIDE])


def y_send_body(count, ex, nt):
    def body(pos, *refs):
        fields, (xa, xb, ya, yb) = refs[:count], refs[count:]
        odd_x = pos[0] % 2 == 1
        odd_y = pos[1] % 2 == 1
        for index in range(count):
            for xi in range(ex + 2 * WIDE):
                plane = x_plane(fields[index], xa.at[index], xb.at[index], odd_x, ex, xi)
                low, high = plane[0], plane[nt - 1]
                ya[index, xi] = jnp.where(odd_y, low, high)
                yb[index, xi] = jnp.where(odd_y, high, low)

    return body


def seam_tile(ya, yb, odd_y, xi):
    low = pick_low(odd_y, ya[xi], yb[xi])
    high = pick_high(odd_y, ya[xi], yb[xi])
    return jnp.where(sub_id() < WIDE, high, low)


def z_send_body(count, ex, nt, both):
    def body(pos, *refs):
        fields, refs = refs[:count], refs[count:]
        xa, xb, ya, yb = refs[:4]
        outs = refs[4:]
        odd_x = pos[0] % 2 == 1
        odd_y = pos[1] % 2 == 1
        odd_z = pos[2] % 2
        lanes = lane_id() // WIDE
        per = LANES // WIDE
        for index in range(count):
            unit = 0
            packed = [None] * len(outs)
            total = (ex + 2 * WIDE) * (nt + 1)
            for xi in range(ex + 2 * WIDE):
                plane = x_plane(fields[index], xa.at[index], xb.at[index], odd_x, ex, xi)
                for tile in range(nt + 1):
                    if tile < nt:
                        value = plane[tile]
                    else:
                        value = seam_tile(ya.at[index], yb.at[index], odd_y, xi)
                    spot = unit % per
                    for which in range(len(outs)):
                        high = 1 - odd_z if which == 0 else odd_z
                        moved = pltpu.roll(value, (WIDE * spot + WIDE * high) % LANES, 1)
                        if spot == 0:
                            packed[which] = moved
                        else:
                            packed[which] = jnp.where(lanes == spot, moved, packed[which])
                        if spot == per - 1 or unit == total - 1:
                            outs[which][index, unit // per] = packed[which]
                    unit += 1

    return body


def halo_body(count, ex, nt, both, sizes, first):
    ny_rows = SUB * nt

    def inside_xy(pos, xi, tile):
        gx = pos[0] * ex + xi - WIDE
        ok = (gx >= 0) & (gx < sizes[0] * ex)
        row = sub_id()
        if tile < nt:
            return ok, None
        y = pos[1] * ny_rows + jnp.where(row < WIDE, ny_rows + row, row - SUB)
        return ok, (y >= 0) & (y < sizes[1] * ny_rows)

    def body(pos, *refs):
        fields, refs = refs[:count], refs[count:]
        xa, xb, ya, yb = refs[:4]
        zs = refs[4 : 6 if both else 5]
        outs = refs[6 if both else 5 :]
        odd_x = pos[0] % 2 == 1
        odd_y = pos[1] % 2 == 1
        odd_z = pos[2] % 2
        lanes = lane_id()
        per = LANES // WIDE
        has_high = pos[2] < sizes[2] - 1
        has_low = pos[2] > 0
        z_mask = ((lanes < WIDE) & has_high) | ((lanes >= LANES - WIDE) & has_low)
        unit = 0
        for xi in range(ex + 2 * WIDE):
            planes = [
                x_plane(fields[index], xa.at[index], xb.at[index], odd_x, ex, xi)
                for index in range(count)
            ]
            for tile in range(nt + 1):
                ok, rows = inside_xy(pos, xi, tile)
                if rows is None:
                    good = jnp.broadcast_to(ok, (SUB, LANES))
                else:
                    good = rows & ok
                spot = unit % per
                for index in range(count):
                    if tile < nt:
                        main = planes[index][tile]
                    else:
                        main = seam_tile(ya.at[index], yb.at[index], odd_y, xi)
                    parts = []
                    for which in range(len(zs)):
                        high = 1 - odd_z if which == 0 else odd_z
                        shift = (LANES - WIDE * spot + LANES - WIDE * (1 - high)) % LANES
                        parts.append(pltpu.roll(zs[which][index, unit // per], shift, 1))
                    if len(parts) == 1:
                        halo = parts[0]
                    else:
                        halo = jnp.where(
                            lanes < LANES // 2,
                            jnp.where(odd_z == 1, parts[1], parts[0]),
                            jnp.where(odd_z == 1, parts[0], parts[1]),
                        )
                    where_main = (xi, 0, slice(SUB * tile, SUB * tile + SUB))
                    where_halo = (xi, 1, slice(SUB * tile, SUB * tile + SUB))
                    if index == 0:
                        outs[0][where_main] = jnp.where(good, main, 0.0)
                        outs[0][where_halo] = jnp.where(good & z_mask, halo, 0.0)
                    elif index == 1:
                        diag = 6.0 + main
                        outs[1][where_main] = diag
                        outs[2][where_main] = jnp.where(good, OMEGA / diag, 0.0)
                        diag = 6.0 + jnp.where(z_mask, halo, 0.0)
                        outs[1][where_halo] = diag
                        outs[2][where_halo] = jnp.where(good & z_mask, OMEGA / diag, 0.0)
                    else:
                        outs[3][where_main] = main
                        outs[3][where_halo] = jnp.where(z_mask, halo, 0.0)
                unit += 1

    return body


def around(value, ghost, masks):
    below, above, low_lanes, high_lanes, first, last = masks
    total = jnp.where(below, ghost, pltpu.roll(value, 1, 1))
    total = total + jnp.where(above, ghost, pltpu.roll(value, LANES - 1, 1))
    moved = pltpu.roll(value, SIDE, 1)
    moved = jnp.where(low_lanes, pltpu.roll(moved, 1, 0), moved)
    total = total + jnp.where(first, ghost, moved)
    moved = pltpu.roll(value, LANES - SIDE, 1)
    moved = jnp.where(high_lanes, pltpu.roll(moved, SUB - 1, 0), moved)
    return total + jnp.where(last, ghost, moved)


def fine_masks():
    lanes, rows = lane_id(), sub_id()
    low_lanes = lanes < SIDE
    high_lanes = lanes >= LANES - SIDE
    return (
        lanes % SIDE == 0,
        lanes % SIDE == SIDE - 1,
        low_lanes,
        high_lanes,
        low_lanes & (rows == 0),
        high_lanes & (rows == SUB - 1),
    )


def assign(rank, table, group, slots, found):
    count = jnp.int32(0)
    for home in range(group):
        for slot in range(slots):
            hit = table[home, 4 * slot] == rank

            @pl.when(hit)
            def _():
                found(count, home, slot)

            count = count + hit.astype(jnp.int32)
    return count


def unpack(packed, ghosts, slots):
    lanes, rows = lane_id(), sub_id()
    column = (lanes % SIDE) // 2
    row = (2 * rows + lanes // (LANES // 2)) % SUB
    upper = rows >= SUB // 2

    def box(index, carry):
        for quad in range(FOOT // 4):
            value = packed[index, quad]
            for inner in range(4):
                low = gather(value, 32 * inner + column, 1)
                high = gather(value, 32 * inner + FOOT + column, 1)
                plane = jnp.where(upper, gather(high, row, 0), gather(low, row, 0))
                ghosts[index, 4 * quad + inner] = plane
        return carry

    lax.fori_loop(0, slots, box, 0)


def fine_body(dims, first):
    group, slots, nby, nbz, size_z = dims

    def body(pos, *refs):
        if first:
            got, source, shift, start = refs[:4]
            ret, state, ghosts, squares, table = refs[4:9]
            (packed, other, diag, rate, kept, homes, copied, sems) = refs[9:]
        else:
            table, got, source, shift, old_state, old_ghosts = refs[:6]
            ret, state, ghosts, squares = refs[6:10]
            (packed, other, diag, rate, kept, homes) = refs[10:]
        rank = pos[1] * size_z + pos[2]
        if first:
            for home in range(group):
                pltpu.make_async_copy(got.at[home, 4, 0], copied.at[home], sems.at[home]).start()
        packed[...] = jnp.zeros(packed.shape, F32)

        def load(index, carry):
            for x in range(SIDE):
                at = pl.ds(SIDE * x + index, SUB, stride=slots)
                six = 6.0 + shift[at, :]
                diag[index, x] = six
                rate[index, x] = OMEGA / six
                kept[index, x] = source[at, :]
                if first:
                    other[index, 1 + x] = start[at, :]
            return carry

        lax.fori_loop(0, slots, load, 0)
        if first:
            for home in range(group):
                pltpu.make_async_copy(got.at[home, 4, 0], copied.at[home], sems.at[home]).wait()
            for home in range(group):
                for index in range(4 * slots):
                    table[home, index] = copied[home, index].astype(jnp.int32)

        def found(count, home, slot):
            packed[count] = got[home, 0:4]
            homes[count, 0] = jnp.int32(home)
            homes[count, 1] = table[home, 4 * slot + 2]
            homes[count, 2] = table[home, 4 * slot + 3]

        for slot in range(slots):
            homes[slot, 0] = jnp.int32(0)
            homes[slot, 1] = jnp.int32(0)
            homes[slot, 2] = jnp.int32(0)
        live = assign(rank, table, group, slots, found)
        unpack(packed, ghosts, slots)
        masks = fine_masks()
        lanes, rows = lane_id(), sub_id()

        def begin(index, carry):
            if not first:
                for x in range(SIDE):
                    change = ghosts[index, x // 2] - old_ghosts[index, x // 2]
                    other[index, 1 + x] = old_state[index, 1 + x] + change
            for buffer in (other, state):
                buffer[index, 0] = ghosts[index, 0]
                buffer[index, SIDE + 1] = ghosts[index, FOOT - 1]
            return carry

        lax.fori_loop(0, slots, begin, 0)

        def residual(buffer, index, x):
            value = buffer[index, 1 + x]
            near = around(value, ghosts[index, x // 2], masks)
            near = near + buffer[index, x] + buffer[index, 2 + x]
            return value, kept[index, x] - diag[index, x] * value + near

        buffers = [other, state]
        for sweep in range(FSWEEPS):
            here, there = buffers[sweep % 2], buffers[1 - sweep % 2]

            def step(index, carry):
                for x in range(SIDE):
                    value, rest = residual(here, index, x)
                    there[index, 1 + x] = value + rate[index, x] * rest
                return carry

            lax.fori_loop(0, slots, step, 0)
        final = buffers[FSWEEPS % 2]
        assert final is state

        ret_rows = [[None] * slots for _ in range(group)]

        def finish(index, total):
            zone_y = jnp.where(homes[index, 1] == 0, 0, SUB - 2)
            zone_z = jnp.where(homes[index, 2] == 0, 0, FOOT - WIDE)
            column = (rows % 2) * (LANES // 2)
            take_all = column + 2 * (lanes % FOOT)
            take_z = column + 2 * (zone_z + lanes % WIDE)
            row_y = zone_y + (rows % 4) // 2
            row_low = rows // 2
            row_high = SUB // 2 + rows // 2
            mine = jnp.zeros((SUB, LANES), F32)
            y_slab = jnp.zeros((SUB, LANES), F32)
            z_slab = jnp.zeros((SUB, LANES), F32)
            whole = None
            for xp in range(FOOT):
                value, left = residual(final, index, 2 * xp)
                mine = mine + left * left
                value, right = residual(final, index, 2 * xp + 1)
                mine = mine + right * right
                both = left + right
                both = both + pltpu.roll(both, LANES - 1, 1)
                both = 0.125 * (both + pltpu.roll(both, LANES - SIDE, 1))
                piece = gather(gather(both, row_y, 0), take_all, 1)
                y_slab = jnp.where((lanes // FOOT == xp // 2) & (rows // 4 == xp % 2), piece, y_slab)
                for part in range(2):
                    picked = gather(both, row_high if part else row_low, 0)
                    piece = gather(picked, take_all, 1)
                    spot = 2 * (xp % 4) + part
                    whole = piece if spot == 0 else jnp.where(lanes // FOOT == spot, piece, whole)
                    piece = gather(picked, take_z, 1)
                    z_slab = jnp.where(lanes // WIDE == 2 * xp + part, piece, z_slab)
                if xp % 4 == 3:
                    packed[index, xp // 4] = whole
            home_z = homes[index, 0] % size_z
            for target in range(group):
                ret[target, 4 + index] = jnp.where(home_z == target % size_z, y_slab, z_slab)
            return total + jnp.where(index < live, mine, 0.0)

        squares[...] = lax.fori_loop(0, slots, finish, jnp.zeros((SUB, LANES), F32))
        for target in range(group):
            ret[target, 0:4] = jnp.zeros((4, SUB, LANES), F32)
        for index in range(slots):

            @pl.when(index < live)
            def _():
                ret[homes[index, 0], 0:4] = packed[index]

    return body


def last_body(dims):
    group, slots, size_z = dims

    def body(pos, table, got, state, ghosts, result, packed, fresh):
        rank = pos[1] * size_z + pos[2]
        packed[...] = jnp.zeros(packed.shape, F32)

        def found(count, home, slot):
            packed[count] = got[home, 0:4]

        live = assign(rank, table, group, slots, found)
        unpack(packed, fresh, slots)

        def box(index, carry):
            for x in range(SIDE):
                value = state[index, 1 + x] + (fresh[index, x // 2] - ghosts[index, x // 2])
                value = jnp.where(index < live, value, 0.0)
                result[pl.ds(SIDE * x + index, SUB, stride=slots), :] = value
            return carry

        lax.fori_loop(0, slots, box, 0)

    return body


def place_body(dims):
    ex, nt, group, slots, size_y, size_z, nby, nbz = dims
    tiles = FOOT // SUB

    def body(pos, table, got, added, side_a, side_b):
        odd = pos[0] % 2 == 1
        rank = pos[1] * size_z + pos[2]
        lanes, rows = lane_id(), sub_id()
        added[...] = jnp.zeros(added.shape, F32)

        def slot_of(home, slot):
            owner = table[home, 4 * slot]
            count = jnp.int32(0)
            for lower in range(group):
                for index in range(slots):
                    hit = (table[lower, 4 * index] == owner) & (lower < home)
                    count = count + hit.astype(jnp.int32)
            return count

        def own(slot, carry):
            owner = table[rank, 4 * slot]

            @pl.when(owner < group)
            def _():
                base_x = FOOT * table[rank, 4 * slot + 1]
                base_y = tiles * table[rank, 4 * slot + 2]
                base_z = FOOT * table[rank, 4 * slot + 3]
                keep = (lanes >= base_z) & (lanes < base_z + FOOT)
                for quad in range(4):
                    value = got[owner, quad]
                    for inner in range(4):
                        for part in range(tiles):
                            spot = 2 * inner + part
                            moved = pltpu.roll(value, (base_z + LANES - FOOT * spot) % LANES, 1)
                            at = (base_x + 4 * quad + inner, 0, base_y + part)
                            added[at] = added[at] + jnp.where(keep, moved, 0.0)

            return carry

        lax.fori_loop(0, slots, own, 0)

        for dy in (-1, 0, 1):
            for dz in (-1, 0, 1):
                if dy == 0 and dz == 0:
                    continue
                home_y = pos[1] + dy
                home_z = pos[2] + dz
                exists = (home_y >= 0) & (home_y < size_y) & (home_z >= 0) & (home_z < size_z)
                home = jnp.where(exists, home_y * size_z + home_z, 0)

                def near(slot, carry):
                    owner = table[home, 4 * slot]
                    block_y = table[home, 4 * slot + 2]
                    block_z = table[home, 4 * slot + 3]
                    wanted = exists & (owner < group)
                    if dy != 0:
                        wanted = wanted & (block_y == (nby - 1 if dy < 0 else 0))
                    if dz != 0:
                        wanted = wanted & (block_z == (nbz - 1 if dz < 0 else 0))

                    @pl.when(wanted)
                    def _():
                        value = got[owner, 4 + slot_of(home, slot)]
                        base_x = FOOT * table[home, 4 * slot + 1]
                        goal = 0 if dy > 0 else 1
                        if dz == 0:
                            base_z = FOOT * block_z
                            keep = (lanes >= base_z) & (lanes < base_z + FOOT)
                            keep = keep & (rows // 4 == goal)
                            turned = pltpu.roll(value, 4, 0)
                            for x in range(FOOT):
                                use = value if x % 2 == goal else turned
                                shift = (base_z + LANES - FOOT * (x // 2)) % LANES
                                moved = pltpu.roll(use, shift, 1)
                                at = (base_x + x, 0, nt)
                                added[at] = added[at] + jnp.where(keep, moved, 0.0)
                        else:
                            where_z = 0 if dz > 0 else LANES - WIDE
                            keep = (lanes >= where_z) & (lanes < where_z + WIDE)
                            for x in range(FOOT):
                                for part in range(tiles):
                                    shift = (where_z + LANES - WIDE * (2 * x + part)) % LANES
                                    if dy == 0:
                                        moved = pltpu.roll(value, shift, 1)
                                        at = (base_x + x, 1, tiles * block_y + part)
                                        added[at] = added[at] + jnp.where(keep, moved, 0.0)
                                    elif part == (0 if dy > 0 else tiles - 1):
                                        moved = pltpu.roll(value, shift, 1)
                                        both = keep & (rows // 4 == goal)
                                        at = (base_x + x, 1, nt)
                                        added[at] = added[at] + jnp.where(both, moved, 0.0)

                    return carry

                lax.fori_loop(0, slots, near, 0)

        for low_side in (True, False):
            packed = None
            for index in range(WIDE - 1):
                plane = index if low_side else ex - (WIDE - 1) + index
                for tile in range(nt + 1):
                    spot = index * (nt + 1) + tile
                    moved = pltpu.roll(added[plane, 1, tile], WIDE + 2 * WIDE * spot, 1)
                    if spot == 0:
                        packed = moved
                    else:
                        packed = jnp.where(lanes // (2 * WIDE) == spot, moved, packed)
            units = (WIDE - 1) * (nt + 1)
            if low_side:
                low_packed = packed
            else:
                high_packed = packed
        for index in range(WIDE - 1):
            for tile in range(nt + 1):
                low = added[index, 0, tile]
                high = added[ex - (WIDE - 1) + index, 0, tile]
                spot = index * (nt + 1) + tile
                side_a[spot] = jnp.where(odd, low, high)
                side_b[spot] = jnp.where(odd, high, low)
        side_a[units] = jnp.where(odd, low_packed, high_packed)
        side_b[units] = jnp.where(odd, high_packed, low_packed)

    return body


def coarse_body(dims, more):
    ex, nt, group, slots, size_z = dims
    span = ex + 2 * WIDE
    rows_all = SUB * (nt + 1)

    def body(pos, table, wide, diag, rate, source, added, xa, xb, fine_sq, *refs):
        if more:
            potential, send, side_a, side_b = refs[:4]
        else:
            potential, send = refs[:2]
        comp, one, two = refs[-3:]
        odd = pos[0] % 2 == 1
        rank = pos[1] * size_z + pos[2]
        lanes = lane_id()
        halo_lanes = (lanes < WIDE) | (lanes >= LANES - WIDE)
        units = (WIDE - 1) * (nt + 1)

        def fill(x, carry):
            for zone in range(2):
                for tile in range(nt + 1):
                    at = (WIDE + x, zone, pl.ds(SUB * tile, SUB))
                    comp[at] = source[at] + added[x, zone, tile]
            return carry

        lax.fori_loop(0, ex, fill, 0)
        low_tail = pick_low(odd, xa[units], xb[units])
        high_tail = pick_high(odd, xa[units], xb[units])
        for index in range(WIDE - 1):
            for tile in range(nt + 1):
                spot = index * (nt + 1) + tile
                shift = (LANES - WIDE - 2 * WIDE * spot) % LANES
                rows = slice(SUB * tile, SUB * tile + SUB)
                xi = 1 + index
                comp[xi, 0, rows] = source[xi, 0, rows] + pick_low(odd, xa[spot], xb[spot])
                tail = jnp.where(halo_lanes, pltpu.roll(low_tail, shift, 1), 0.0)
                comp[xi, 1, rows] = source[xi, 1, rows] + tail
                xi = WIDE + ex + index
                comp[xi, 0, rows] = source[xi, 0, rows] + pick_high(odd, xa[spot], xb[spot])
                tail = jnp.where(halo_lanes, pltpu.roll(high_tail, shift, 1), 0.0)
                comp[xi, 1, rows] = source[xi, 1, rows] + tail

        edge = lax.broadcasted_iota(jnp.int32, (rows_all, LANES), 1)

        def update(here, xi):
            main, halo = here[xi, 0], here[xi, 1]
            main_up, halo_up = pltpu.roll(main, 1, 1), pltpu.roll(halo, 1, 1)
            main_dn, halo_dn = pltpu.roll(main, LANES - 1, 1), pltpu.roll(halo, LANES - 1, 1)
            at_low, at_high = edge == 0, edge == LANES - 1
            result = []
            for zone, value in ((0, main), (1, halo)):
                if zone == 0:
                    near = jnp.where(at_low, halo_up, main_up) + jnp.where(at_high, halo_dn, main_dn)
                else:
                    near = jnp.where(at_low, main_up, halo_up) + jnp.where(at_high, main_dn, halo_dn)
                near = near + pltpu.roll(value, 1, 0) + pltpu.roll(value, rows_all - 1, 0)
                near = near + here[xi - 1, zone] + here[xi + 1, zone]
                rest = comp[xi, zone] - diag[xi, zone] * value + near
                result.append((value, rest))
            return result

        buffers = [wide, one, two, one]
        for sweep in range(CSWEEPS - 1):
            here, there = buffers[sweep], buffers[sweep + 1]

            def step(xi, carry):
                for zone, (value, rest) in enumerate(update(here, xi)):
                    there[xi, zone] = value + rate[xi, zone] * rest
                return carry

            lax.fori_loop(1 + sweep, span - 1 - sweep, step, 0)
        here = buffers[CSWEEPS - 1]

        def step(x, total):
            value, rest = update(here, WIDE + x)[0]
            value = value + rate[WIDE + x, 0] * rest
            for tile in range(nt):
                rows = slice(SUB * tile, SUB * tile + SUB)
                potential[x, tile] = value[rows]
                total = total + rest[rows] * rest[rows]
            return total

        total = lax.fori_loop(0, ex, step, fine_sq[...])
        for target in range(group):
            send[target, 0:4] = jnp.zeros((4, SUB, LANES), F32)
            send[target, 4] = total
        for slot in range(slots):
            target = table[rank, 4 * slot]

            @pl.when(target < group)
            def _():
                def write(quad, packed):
                    send[target, quad] = packed

                block = [table[rank, 4 * slot + 1 + index] for index in range(3)]
                extract(potential, write, *block)

        if more:
            low = potential[0:WIDE]
            high = potential[ex - WIDE : ex]
            side_a[0] = jnp.where(odd, low, high)
            side_b[0] = jnp.where(odd, high, low)

    return body


def local(
    coarse_source,
    coarse_shift,
    coarse_start,
    fine_source,
    fine_shift,
    fine_start,
    box_corner,
    box_owner,
):
    ex, ey, ez = coarse_source.shape
    size_x, size_y, size_z = (lax.axis_size(axis) for axis in ("gx", "gy", "gz"))
    group = size_y * size_z
    slots, fine = fine_source.shape
    nbx, nby, nbz = ex // FOOT, ey // FOOT, ez // FOOT
    nt = ey // SUB
    assert ez == LANES and nby > 1 and fine == SIDE**3
    both = size_z > 2
    span = ex + 2 * WIDE
    sizes = (size_x, size_y, size_z)
    pos = jnp.stack([lax.axis_index(axis) for axis in ("gx", "gy", "gz")]).astype(jnp.int32)

    def tiled(field):
        return field.reshape(ex, nt, SUB, LANES)

    def rows(field):
        count = fine // LANES
        return field.reshape(slots, count, LANES).transpose(1, 0, 2).reshape(count * slots, LANES)

    def exchange(value):
        return lax.all_to_all(value, GROUP_AXES, split_axis=0, concat_axis=0, tiled=True)

    start, shift, source = tiled(coarse_start), tiled(coarse_shift), tiled(coarse_source)
    f_source, f_shift, f_start = rows(fine_source), rows(fine_shift), rows(fine_start)

    def halos(fields, side_a, side_b, outs, label):
        count = len(fields)
        xa, xb = swap("gx", side_a, side_b)
        ins = [(SMEM, pos)] + [(VMEM, field) for field in fields]
        ya, yb = call(
            y_send_body(count, ex, nt),
            label + "_y",
            ins + [(VMEM, xa), (VMEM, xb)],
            [(VMEM, out(count, span, SUB, LANES))] * 2,
        )
        ya, yb = swap("gy", ya, yb)
        units = -(-span * (nt + 1) // (LANES // WIDE))
        zs = call(
            z_send_body(count, ex, nt, both),
            label + "_z",
            ins + [(VMEM, value) for value in (xa, xb, ya, yb)],
            [(VMEM, out(count, units, SUB, LANES))] * (2 if both else 1),
        )
        if both:
            zs = list(swap("gz", *zs))
        else:
            zs = [swap("gz", zs[0], zs[0])[0]]
        return call(
            halo_body(count, ex, nt, both, sizes, count > 1),
            label + "_all",
            ins + [(VMEM, value) for value in (xa, xb, ya, yb, *zs)],
            [(VMEM, out(span, 2, SUB * (nt + 1), LANES))] * outs,
        )

    chunk = out(group, 5, SUB, LANES)
    send, side_a, side_b = call(
        send_start_body((ex, nt, group, slots, nbx, nby, nbz)),
        "send_start",
        [(SMEM, pos), (SMEM, box_corner), (SMEM, box_owner)]
        + [(VMEM, value) for value in (start, shift, source)],
        [(VMEM, chunk)] + [(VMEM, out(3, WIDE, nt, SUB, LANES))] * 2,
    )
    got = exchange(send)
    wide, diag, rate, source_wide = halos([start, shift, source], side_a, side_b, 4, "fixed")

    box_shape = (slots, SIDE, SUB, LANES)
    state_shape = (slots, SIDE + 2, SUB, LANES)
    box_scratch = [
        pltpu.VMEM((slots, 4, SUB, LANES), F32),
        pltpu.VMEM(state_shape, F32),
        pltpu.VMEM(box_shape, F32),
        pltpu.VMEM(box_shape, F32),
        pltpu.VMEM(box_shape, F32),
        pltpu.SMEM((slots, 3), jnp.int32),
    ]
    box_outs = [
        (VMEM, out(group, 4 + slots, SUB, LANES)),
        (VMEM, out(*state_shape)),
        (VMEM, out(slots, FOOT, SUB, LANES)),
        (VMEM, out(SUB, LANES)),
    ]
    norms = []
    table = None
    for cycle in range(CYCLES):
        first = cycle == 0
        body = fine_body((group, slots, nby, nbz, size_z), first)
        if first:
            ret, state, ghosts, squares, table = call(
                body,
                "fine_first",
                [(SMEM, pos)] + [(VMEM, value) for value in (got, f_source, f_shift, f_start)],
                box_outs + [(SMEM, out(group, 4 * slots, dtype=jnp.int32))],
                box_scratch
                + [pltpu.SMEM((group, LANES), F32), pltpu.SemaphoreType.DMA((group,))],
            )
        else:
            norms.append(jnp.sum(got[:, 4]))
            ret, state, ghosts, squares = call(
                body,
                "fine_next",
                [(SMEM, pos), (SMEM, table)]
                + [(VMEM, value) for value in (got, f_source, f_shift, state, ghosts)],
                box_outs,
                box_scratch,
            )
        back = exchange(ret)
        units = (WIDE - 1) * (nt + 1) + 1
        added, side_a, side_b = call(
            place_body((ex, nt, group, slots, size_y, size_z, nby, nbz)),
            "place",
            [(SMEM, pos), (SMEM, table), (VMEM, back)],
            [(VMEM, out(ex, 2, nt + 1, SUB, LANES))] + [(VMEM, out(units, SUB, LANES))] * 2,
        )
        xa, xb = swap("gx", side_a, side_b)
        more = cycle < CYCLES - 1
        wide_shape = (span, 2, SUB * (nt + 1), LANES)
        result = call(
            coarse_body((ex, nt, group, slots, size_z), more),
            "coarse",
            [(SMEM, pos), (SMEM, table)]
            + [(VMEM, v) for v in (wide, diag, rate, source_wide, added, xa, xb, squares)],
            [(VMEM, out(ex, nt, SUB, LANES)), (VMEM, chunk)]
            + [(VMEM, out(1, WIDE, nt, SUB, LANES))] * (2 if more else 0),
            [pltpu.VMEM(wide_shape, F32)] * 3,
        )
        potential, send = result[:2]
        got = exchange(send)
        if more:
            (wide,) = halos([potential], result[2], result[3], 1, "next")
    (values,) = call(
        last_body((group, slots, size_z)),
        "last",
        [(SMEM, pos), (SMEM, table)] + [(VMEM, value) for value in (got, state, ghosts)],
        [(VMEM, out(slots * fine // LANES, LANES))],
        [
            pltpu.VMEM((slots, 4, SUB, LANES), F32),
            pltpu.VMEM((slots, FOOT, SUB, LANES), F32),
        ],
    )
    norms.append(jnp.sum(got[:, 4]))
    total = jnp.broadcast_to(jnp.stack(norms)[None, :], (SUB, CYCLES))
    bit = 1
    while bit < size_x:
        total = total + lax.ppermute(total, "gx", [(i, i ^ bit) for i in range(size_x)])
        bit *= 2
    cells = float(ex * ey * ez * size_x * size_y * size_z)
    values = values.reshape(fine // LANES, slots, LANES).transpose(1, 0, 2).reshape(slots, fine)
    return potential.reshape(ex, ey, ez), values, jnp.sqrt(total[0] / cells)


def solution(mesh):
    in_specs = (
        P("gx", "gy", "gz"),
        P("gx", "gy", "gz"),
        P("gx", "gy", "gz"),
        P(("gx", "gy", "gz"), None),
        P(("gx", "gy", "gz"), None),
        P(("gx", "gy", "gz"), None),
        P(("gx", "gy", "gz"), None, None),
        P(("gx", "gy", "gz"), None),
    )
    out_specs = (P("gx", "gy", "gz"), P(("gx", "gy", "gz"), None), P())
    return jax.shard_map(local, mesh=mesh, in_specs=in_specs, out_specs=out_specs, check_vma=False)
```

time: 507 us -> 158 us (0.31); the launches traced: 499 us -> 156 us
  local copies, waits for them, and re-layouts: 159 us -> 9.19 us
  starting transfers between devices: 138 us -> 32.2 us
  other arithmetic: 86.4 us -> 4.44 us
  Pallas kernels: 0 us -> 68 us
  waiting for transfers between devices: 54.9 us -> 21.8 us
  blocking collectives: 43.1 us -> 19.8 us
  matrix products: 13.1 us -> 0 us
    ppermute x42 -> x16, starting transfers between devices: 115 us -> 21.6 us  [the longest x6 10.9 us: swap(): got_b = lax.ppermute(second, axis, pairs_b) if count > 2 else got_a]
    pallas_call x0 -> x14, Pallas kernels: none -> 68 us  [call(): pl.pallas_call(body, name=name, in_specs=[spec for spec, _ in ins], out_s...]
    reshape x15 -> x0, local copies, waits for them, and re-layouts: 62.8 us -> none  [the longest x4 38 us: inject(): return spread.reshape(number, 8 * FOOT * FOOT * FOOT)]
    broadcast_in_dim x8 -> x1, local copies, waits for them, and re-layouts: 45.1 us -> 0.01 us  [local(): total = jnp.broadcast_to(jnp.stack(norms)[None, :], (SUB, CYCLES))]
    psum x1 -> x0, blocking collectives: 43.1 us -> none  [local(): norms.append(lax.psum(local_sum, ('gx', 'gy', 'gz')))]
    ppermute x42 -> x16, waiting for transfers between devices: 54.9 us -> 17.9 us  [the longest x6 8.02 us: swap(): got_b = lax.ppermute(second, axis, pairs_b) if count > 2 else got_a]
    reduce_sum x7 -> x2, other arithmetic: 34.5 us -> 2 us  [local(): norms.append(jnp.sum(got[:, 4]))]
    add x16 -> x2, other arithmetic: 23.3 us -> 0.01 us  [local(): total + lax.ppermute(total, 'gx', [(i, i ^ bit) for i in range(size_x)])]
  transfers between devices with their start and end apart: 48 -> 19, of which waited for: 16 -> 7; matrix products, arithmetic and copies ran while one was open for 41% -> 1% of each run, Pallas kernels for 0% -> 22%
where the time goes in v1:
time: 158 us; the launch traced here: 156 us
  Pallas kernels  68 us (43%)
  starting transfers between devices  32.2 us (20%)
  waiting for transfers between devices  21.8 us (14%)
  blocking collectives  19.8 us (13%)
  local copies, waits for them, and re-layouts  9.19 us (6%)
  other arithmetic  4.44 us (3%)
    pallas_call x14, Pallas kernels, call(): pl.pallas_call(body, name=name, in_specs=[spec for spec, _ in ins], out_s...  68 us
    all_to_all x2, blocking collectives, exchange(): lax.all_to_all(value, GROUP_AXES, split_axis=0, concat_axis=0, tiled=True)  19.8 us
    ppermute x6, starting transfers between devices, swap(): got_b = lax.ppermute(second, axis, pairs_b) if count > 2 else got_a  10.9 us
    all_to_all x3, starting transfers between devices, exchange(): lax.all_to_all(value, GROUP_AXES, split_axis=0, concat_axis=0, tiled=True)  10.7 us
    unnamed x41, local copies, waits for them, and re-layouts  9.18 us
    ppermute x6, waiting for transfers between devices, swap(): got_b = lax.ppermute(second, axis, pairs_b) if count > 2 else got_a  8.02 us
    ppermute x8, starting transfers between devices, swap(): got_a = lax.ppermute(first, axis, pairs_a)  8 us
    ppermute x8, waiting for transfers between devices, swap(): got_a = lax.ppermute(first, axis, pairs_a)  7.37 us
  transfers between devices with their start and end apart: 19, of which 7 were waited for; matrix products, arithmetic and copies ran while one was open for 1% of the time, Pallas kernels for 22%

profile of v1, /device:TPU:0, one launch (start us, length us, event | category | flops | bytes accessed | tf_op | source)
XLA Modules:
  0.0 156.3 jit_solution(1752594694182387672)
XLA Ops:
  0.6 0.7 copy-done.17
  1.3 0.7 copy.11.corner
  2.0 0.6 pad_add_fusion.pos
  2.5 2.3 %send_start.1 = (f32[8,5,8,128]{3,2,1,0:T(8,128)}, f32[3,4,4,8,128]{4,3,2,1,0:T(8,128)}, f32[3,4,4,8,128]{4,3,2,1,0:T(8,128)}) custom-call(s32[3]{0:T(128)} %pad_add_fusion.pos, s32[1,4,3]{2,1,0:T(4,128)} %copy.11.corner, s32[1,4]{1,0:T(1,128)} %owner.1, f32[16,4,8,128]{3,2,1,0:T(8,128)} %bitcast.31, f32[16,4,8,128]{3,2,1,0:T(8,128)} %bitcast.35, ...), custom_call_target="tpu_custom_call" | custom-call | tf_op jit(solution)/shard_map/send_start/pallas_call | solution.py:30
  4.8 3.2 %collective-permute-start = (f32[3,4,4,8,128]{4,3,2,1,0:T(8,128)}, f32[3,4,4,8,128]{4,3,2,1,0:T(8,128)S(1)}, u32[]{:S(2)}, u32[]{:S(2)}) collective-permute-start(f32[3,4,4,8,128]{4,3,2,1,0:T(8,128)} %get-tuple-element.37), channel_id=1, source_target_pairs={{0,8},{8,0},{16,24},{24,16},{1,9},{9,1},{17,25},{25,17},{2,10},{10... | collective-permute-start | bytes 589832 | tf_op jit(solution)/shard_map/ppermute | solution.py:62
  8.0 2.3 %collective-permute-start.1 = (f32[3,4,4,8,128]{4,3,2,1,0:T(8,128)}, f32[3,4,4,8,128]{4,3,2,1,0:T(8,128)S(1)}, u32[]{:S(2)}, u32[]{:S(2)}) collective-permute-start(f32[3,4,4,8,128]{4,3,2,1,0:T(8,128)} %get-tuple-element.38), channel_id=1, source_target_pairs={{0,24},{8,16},{16,8},{24,0},{1,25},{9,17},{17,9},{25,1},{2,26},{10... | collective-permute-start | bytes 589832 | tf_op jit(solution)/shard_map/ppermute | solution.py:63
  10.3 3.7 %all-to-all-start = ((f32[8,5,8,128]{3,2,1,0:T(8,128)}), f32[8,5,8,128]{3,2,1,0:T(8,128)S(1)}, u32[]{:S(2)}, u32[]{:S(2)}) async-start(f32[8,5,8,128]{3,2,1,0:T(8,128)} %get-tuple-element.35), calls=%async_computation | async-start | bytes 327680 | tf_op jit(solution)/shard_map/all_to_all | solution.py:746
  14.0 5.6 %collective-permute-done.1.refs_4_ = f32[3,4,4,8,128]{4,3,2,1,0:T(8,128)S(1)} collective-permute-done((f32[3,4,4,8,128]{4,3,2,1,0:T(8,128)}, f32[3,4,4,8,128]{4,3,2,1,0:T(8,128)S(1)}, u32[]{:S(2)}, u32[]{:S(2)}) %collective-permute-start.1) | collective-permute-done | bytes 196640 | tf_op jit(solution)/shard_map/ppermute | solution.py:63
  19.6 0.7 copy-done.1
  20.3 2.1 %fixed_y.1 = (f32[3,24,8,128]{3,2,1,0:T(8,128)}, f32[3,24,8,128]{3,2,1,0:T(8,128)}) custom-call(s32[3]{0:T(128)} %pad_add_fusion.pos, f32[16,4,8,128]{3,2,1,0:T(8,128)} %bitcast.32, f32[16,4,8,128]{3,2,1,0:T(8,128)} %bitcast.36, f32[16,4,8,128]{3,2,1,0:T(8,128)} %bitcast.40, f32[3,4,4,8,128]{4,3,2,1,0:T(8,128)} %copy-done, f32[3,4,4,8,128]{4,3,2,1,0:T(8,128)} %copy-done.1), custom_call_target="tpu_custom_call" | custom-call | tf_op jit(solution)/shard_map/fixed_y/pallas_call | solution.py:30
  22.4 0.0 collective-permute-start.2
  22.4 1.5 collective-permute-start.3
  24.0 0.7 copy-done.6
  24.6 9.7 %fine_first.1 = (f32[8,8,8,128]{3,2,1,0:T(8,128)}, f32[4,34,8,128]{3,2,1,0:T(8,128)}, f32[4,16,8,128]{3,2,1,0:T(8,128)}, f32[8,128]{1,0:T(8,128)}, s32[8,16]{1,0:T(8,128)}) custom-call(s32[3]{0:T(128)} %pad_add_fusion.pos, f32[8,5,8,128]{3,2,1,0:T(8,128)} %copy-done.6, f32[1024,128]{1,0:T(8,128)} %bitcast.43, f32[1024,128]{1,0:T(8,128)} %bitcast.45, ...), custom_call_target="tpu_custom_call" | custom-call | tf_op jit(solution)/shard_map/fine_first/pallas_call | solution.py:30
  34.3 10.4 %all_to_all.25.got = f32[8,8,8,128]{3,2,1,0:T(8,128)} all-to-all(f32[8,8,8,128]{3,2,1,0:T(8,128)} %get-tuple-element.45), channel_id=1, replica_groups=mesh['gx'=4,'gy'=4,'gz'=2] {'gy','gz'}, dimensions={0} | all-to-all | bytes 524288 | tf_op jit(solution)/shard_map/all_to_all | solution.py:746
  44.7 3.3 %place.2 = (f32[16,2,5,8,128]{4,3,2,1,0:T(8,128)}, f32[16,8,128]{2,1,0:T(8,128)}, f32[16,8,128]{2,1,0:T(8,128)}) custom-call(s32[3]{0:T(128)} %pad_add_fusion.pos, s32[8,16]{1,0:T(8,128)} %get-tuple-element.36.table.refs_0_, f32[8,8,8,128]{3,2,1,0:T(8,128)} %all_to_all.25.got), custom_call_target="tpu_custom_call" | custom-call | tf_op jit(solution)/shard_map/place/pallas_call | solution.py:30
  48.0 0.0 collective-permute-start.5
  48.0 2.8 %collective-permute-start.6 = (f32[16,8,128]{2,1,0:T(8,128)}, f32[16,8,128]{2,1,0:T(8,128)S(1)}, u32[]{:S(2)}, u32[]{:S(2)}) collective-permute-start(f32[16,8,128]{2,1,0:T(8,128)} %get-tuple-element.48), channel_id=1, source_target_pairs={{0,24},{8,16},{16,8},{24,0},{1,25},{9,17},{17,9},{25,1},{2,26},{10... | collective-permute-start | bytes 196616 | tf_op jit(solution)/shard_map/ppermute | solution.py:63
  50.8 0.7 copy-done.2
  51.5 0.7 copy-done.3
  52.2 2.6 %fixed_z.1 = f32[3,4,8,128]{3,2,1,0:T(8,128)} custom-call(s32[3]{0:T(128)} %pad_add_fusion.pos, f32[16,4,8,128]{3,2,1,0:T(8,128)} %bitcast.33, f32[16,4,8,128]{3,2,1,0:T(8,128)} %bitcast.37, f32[16,4,8,128]{3,2,1,0:T(8,128)} %bitcast.41, f32[3,4,4,8,128]{4,3,2,1,0:T(8,128)} %copy-done, f32[3,4,4,8,128]{4,3,2,1,0:T(8,128)} %copy-done.1, ...), custom_call_target="tpu_custom_call" | custom-call | tf_op jit(solution)/shard_map/fixed_z/pallas_call | solution.py:30
  54.7 1.4 collective-permute-start.4
  56.1 2.9 %collective-permute-done.4.refs_7_ = f32[3,4,8,128]{3,2,1,0:T(8,128)S(1)} collective-permute-done((f32[3,4,8,128]{3,2,1,0:T(8,128)}, f32[3,4,8,128]{3,2,1,0:T(8,128)S(1)}, u32[]{:S(2)}, u32[]{:S(2)}) %collective-permute-start.4) | collective-permute-done | bytes 49184 | tf_op jit(solution)/shard_map/ppermute | solution.py:62
  59.0 0.6 copy-done.15
  59.7 3.8 %fixed_all.1 = (f32[24,2,40,128]{3,2,1,0:T(8,128)}, f32[24,2,40,128]{3,2,1,0:T(8,128)}, f32[24,2,40,128]{3,2,1,0:T(8,128)}, f32[24,2,40,128]{3,2,1,0:T(8,128)}) custom-call(s32[3]{0:T(128)} %pad_add_fusion.pos, f32[16,4,8,128]{3,2,1,0:T(8,128)} %bitcast.34, f32[16,4,8,128]{3,2,1,0:T(8,128)} %bitcast.38, f32[16,4,8,128]{3,2,1,0:T(8,128)} %bitcast.42, ...), custom_call_target="tpu_custom_call" | custom-call | tf_op jit(solution)/shard_map/fixed_all/pallas_call | solution.py:30
  63.5 0.0 collective-permute-done.6.xb
  63.5 0.6 copy-done.11
  64.1 0.0 copy-done.12
  64.1 11.5 %coarse.2 = (f32[16,4,8,128]{3,2,1,0:T(8,128)}, f32[8,5,8,128]{3,2,1,0:T(8,128)}, f32[1,4,4,8,128]{4,3,2,1,0:T(8,128)}, f32[1,4,4,8,128]{4,3,2,1,0:T(8,128)}) custom-call(s32[3]{0:T(128)} %pad_add_fusion.pos, s32[8,16]{1,0:T(8,128)} %get-tuple-element.36.table.refs_0_, f32[24,2,40,128]{3,2,1,0:T(8,128)} %get-tuple-element.41.wide, ...), custom_call_target="tpu_custom_call" | custom-call | tf_op jit(solution)/shard_map/coarse/pallas_call | solution.py:30
  75.6 9.4 %all_to_all.26.refs_1_ = f32[8,5,8,128]{3,2,1,0:T(8,128)} all-to-all(f32[8,5,8,128]{3,2,1,0:T(8,128)} %get-tuple-element.55), channel_id=1, replica_groups=mesh['gx'=4,'gy'=4,'gz'=2] {'gy','gz'}, dimensions={0} | all-to-all | bytes 327680 | tf_op jit(solution)/shard_map/all_to_all | solution.py:746
  85.0 9.1 %fine_next.1 = (f32[8,8,8,128]{3,2,1,0:T(8,128)}, f32[4,34,8,128]{3,2,1,0:T(8,128)}, f32[4,16,8,128]{3,2,1,0:T(8,128)}, f32[8,128]{1,0:T(8,128)}) custom-call(s32[3]{0:T(128)} %pad_add_fusion.pos, s32[8,16]{1,0:T(8,128)} %get-tuple-element.36.table.refs_0_, f32[8,5,8,128]{3,2,1,0:T(8,128)} %all_to_all.26.refs_1_, f32[1024,128]{1,0:T(8,128)} %bitcast.44, ...), custom_call_target="tpu_custom_call" | custom-call | tf_op jit(solution)/shard_map/fine_next/pallas_call | solution.py:30
  94.1 3.6 %all-to-all-start.3 = ((f32[8,8,8,128]{3,2,1,0:T(8,128)}), f32[8,8,8,128]{3,2,1,0:T(8,128)S(1)}, u32[]{:S(2)}, u32[]{:S(2)}) async-start(f32[8,8,8,128]{3,2,1,0:T(8,128)} %get-tuple-element.58), calls=%async_computation.3 | async-start | bytes 524288 | tf_op jit(solution)/shard_map/all_to_all | solution.py:746
  97.7 0.7 collective-permute-start.7
  98.4 1.4 collective-permute-start.8
  99.8 2.2 %collective-permute-done.7.refs_1_ = f32[1,4,4,8,128]{4,3,2,1,0:T(8,128)S(1)} collective-permute-done((f32[1,4,4,8,128]{4,3,2,1,0:T(8,128)S(1)}, f32[1,4,4,8,128]{4,3,2,1,0:T(8,128)S(1)}, u32[]{:S(2)}, u32[]{:S(2)}) %collective-permute-start.7) | collective-permute-done | bytes 65568 | tf_op jit(solution)/shard_map/ppermute | solution.py:62
  102.1 2.4 %collective-permute-done.8.refs_2_ = f32[1,4,4,8,128]{4,3,2,1,0:T(8,128)S(1)} collective-permute-done((f32[1,4,4,8,128]{4,3,2,1,0:T(8,128)S(1)}, f32[1,4,4,8,128]{4,3,2,1,0:T(8,128)S(1)}, u32[]{:S(2)}, u32[]{:S(2)}) %collective-permute-start.8) | collective-permute-done | bytes 65568 | tf_op jit(solution)/shard_map/ppermute | solution.py:63
  104.5 0.6 copy-done.8
  105.1 1.7 %next_y.1 = (f32[1,24,8,128]{3,2,1,0:T(8,128)}, f32[1,24,8,128]{3,2,1,0:T(8,128)}) custom-call(s32[3]{0:T(128)} %pad_add_fusion.pos, f32[16,4,8,128]{3,2,1,0:T(8,128)} %get-tuple-element.50.refs_0_, f32[1,4,4,8,128]{4,3,2,1,0:T(8,128)} %copy-done.7, f32[1,4,4,8,128]{4,3,2,1,0:T(8,128)} %copy-done.8), custom_call_target="tpu_custom_call" | custom-call | tf_op jit(solution)/shard_map/next_y/pallas_call | solution.py:30
  106.8 0.0 collective-permute-start.9
  106.8 2.0 %collective-permute-start.10 = (f32[1,24,8,128]{3,2,1,0:T(8,128)}, f32[1,24,8,128]{3,2,1,0:T(8,128)S(1)}, u32[]{:S(2)}, u32[]{:S(2)}) collective-permute-start(f32[1,24,8,128]{3,2,1,0:T(8,128)} %get-tuple-element.54), channel_id=1, source_target_pairs={{0,6},{2,4},{4,2},{6,0},{1,7},{3,5},{5,3},{7,1},{8,14},{10,12},{12... | collective-permute-start | bytes 294920 | tf_op jit(solution)/shard_map/ppermute | solution.py:63
  108.8 0.7 copy-done.4
  109.5 3.3 %place.3 = (f32[16,2,5,8,128]{4,3,2,1,0:T(8,128)}, f32[16,8,128]{2,1,0:T(8,128)}, f32[16,8,128]{2,1,0:T(8,128)}) custom-call(s32[3]{0:T(128)} %pad_add_fusion.pos, s32[8,16]{1,0:T(8,128)} %get-tuple-element.36.table.refs_0_, f32[8,8,8,128]{3,2,1,0:T(8,128)} %copy-done.4), custom_call_target="tpu_custom_call" | custom-call | tf_op jit(solution)/shard_map/place/pallas_call | solution.py:30
  112.8 1.0 collective-permute-start.12
  113.7 0.9 collective-permute-start.13
  114.7 0.6 copy-done.9
  115.3 0.6 copy-done.10
  115.9 1.9 %next_z.1 = f32[1,4,8,128]{3,2,1,0:T(8,128)} custom-call(s32[3]{0:T(128)} %pad_add_fusion.pos, f32[16,4,8,128]{3,2,1,0:T(8,128)} %get-tuple-element.50.refs_0_, f32[1,4,4,8,128]{4,3,2,1,0:T(8,128)} %copy-done.7, f32[1,4,4,8,128]{4,3,2,1,0:T(8,128)} %copy-done.8, f32[1,24,8,128]{3,2,1,0:T(8,128)} %copy-done.9, f32[1,24,8,128]{3,2,1,0:T(8,128)} %copy-done.10), custom_call_target="tpu_custom_call" | custom-call | tf_op jit(solution)/shard_map/next_z/pallas_call | solution.py:30
  117.9 1.7 %collective-permute-start.11 = (f32[1,4,8,128]{3,2,1,0:T(8,128)}, f32[1,4,8,128]{3,2,1,0:T(8,128)S(1)}, u32[]{:S(2)}, u32[]{:S(2)}) collective-permute-start(f32[1,4,8,128]{3,2,1,0:T(8,128)} %next_z.1), channel_id=1, source_target_pairs={{0,1},{1,0},{2,3},{3,2},{4,5},{5,4},{6,7},{7,6},{8,9},{9,8},{10,11... | collective-permute-start | bytes 49160 | tf_op jit(solution)/shard_map/ppermute | solution.py:62
  119.6 2.2 %collective-permute-done.11.refs_5_ = f32[1,4,8,128]{3,2,1,0:T(8,128)S(1)} collective-permute-done((f32[1,4,8,128]{3,2,1,0:T(8,128)}, f32[1,4,8,128]{3,2,1,0:T(8,128)S(1)}, u32[]{:S(2)}, u32[]{:S(2)}) %collective-permute-start.11) | collective-permute-done | bytes 16416 | tf_op jit(solution)/shard_map/ppermute | solution.py:62
  121.8 0.6 copy-done.16
  122.4 2.3 %next_all.1.wide = f32[24,2,40,128]{3,2,1,0:T(8,128)} custom-call(s32[3]{0:T(128)} %pad_add_fusion.pos, f32[16,4,8,128]{3,2,1,0:T(8,128)} %get-tuple-element.50.refs_0_, f32[1,4,4,8,128]{4,3,2,1,0:T(8,128)} %copy-done.7, f32[1,4,4,8,128]{4,3,2,1,0:T(8,128)} %copy-done.8, f32[1,24,8,128]{3,2,1,0:T(8,128)} %copy-done.9, f32[1,24,8,128]{3,2,1,0:T(8,128)} %copy-done.10, ...), custom_call_target="tpu_custom_call" | custom-call | tf_op jit(solution)/shard_map/next_all/pallas_call | solution.py:30
  124.8 0.6 copy-done.13
  125.4 0.0 copy-done.14
  125.4 11.4 %coarse.3 = (f32[16,4,8,128]{3,2,1,0:T(8,128)}, f32[8,5,8,128]{3,2,1,0:T(8,128)}) custom-call(s32[3]{0:T(128)} %pad_add_fusion.pos, s32[8,16]{1,0:T(8,128)} %get-tuple-element.36.table.refs_0_, f32[24,2,40,128]{3,2,1,0:T(8,128)} %next_all.1.wide, f32[24,2,40,128]{3,2,1,0:T(8,128)} %get-tuple-element.42.diag, f32[24,2,40,128]{3,2,1,0:T(8,128)} %get-tuple-element.43.rate, ...), custom_call_target="tpu_custom_call" | custom-call | tf_op jit(solution)/shard_map/coarse/pallas_call | solution.py:30
  136.8 3.4 %all-to-all-start.4 = ((f32[8,5,8,128]{3,2,1,0:T(8,128)}), f32[8,5,8,128]{3,2,1,0:T(8,128)S(1)}, u32[]{:S(2)}, u32[]{:S(2)}) async-start(f32[8,5,8,128]{3,2,1,0:T(8,128)} %get-tuple-element.64), calls=%async_computation.4 | async-start | bytes 327680 | tf_op jit(solution)/shard_map/all_to_all | solution.py:746
  140.2 1.4 slice_reduce_fusion.1
  141.6 3.9 %all-to-all-done.4.got = f32[8,5,8,128]{3,2,1,0:T(8,128)S(1)} async-done(((f32[8,5,8,128]{3,2,1,0:T(8,128)}), f32[8,5,8,128]{3,2,1,0:T(8,128)S(1)}, u32[]{:S(2)}, u32[]{:S(2)}) %all-to-all-start.4) | async-done | bytes 163872 | tf_op jit(solution)/shard_map/all_to_all | solution.py:746
  145.6 0.6 slice_reduce_fusion
  146.2 1.4 pad_maximum_fusion
  147.6 1.1 collective-permute-start.14
  148.7 2.5 %collective-permute-done.14 = f32[8,2]{1,0:T(8,128)S(1)} collective-permute-done((f32[8,2]{1,0:T(8,128)S(1)}, f32[8,2]{1,0:T(8,128)S(1)}, u32[]{:S(2)}, u32[]{:S(2)}) %collective-permute-start.14) | collective-permute-done | bytes 96 | tf_op jit(solution)/shard_map/ppermute | solution.py:869
  151.2 1.6 %collective-permute-start.15 = (f32[8,2]{1,0:T(8,128)S(1)}, f32[8,2]{1,0:T(8,128)S(1)}, u32[]{:S(2)}, u32[]{:S(2)}) collective-permute-start(f32[8,2]{1,0:T(8,128)S(1)} %broadcast_add_fusion), channel_id=1, source_target_pairs={{0,16},{8,24},{16,0},{24,8},{1,17},{9,25},{17,1},{25,9},{2,18},{10... | collective-permute-start | bytes 200 | tf_op jit(solution)/shard_map/ppermute | solution.py:869
  152.7 3.0 %last.1 = f32[1024,128]{1,0:T(8,128)} custom-call(s32[3]{0:T(128)} %pad_add_fusion.pos, s32[8,16]{1,0:T(8,128)} %get-tuple-element.36.table.refs_0_, f32[8,5,8,128]{3,2,1,0:T(8,128)} %copy-done.5, f32[4,34,8,128]{3,2,1,0:T(8,128)} %get-tuple-element.65.state, f32[4,16,8,128]{3,2,1,0:T(8,128)} %get-tuple-element.66.ghosts), custom_call_target="tpu_custom_call" | custom-call | tf_op jit(solution)/shard_map/last/pallas_call | solution.py:30
  155.7 0.5 sqrt_bitcast_fusion
  (39 shorter events, 0.1 us)
Async XLA Ops:
  0.6 0.7 copy-start.17
  4.8 9.2 %collective-permute-start = (f32[3,4,4,8,128]{4,3,2,1,0:T(8,128)}, f32[3,4,4,8,128]{4,3,2,1,0:T(8,128)S(1)}, u32[]{:S(2)}, u32[]{:S(2)}) collective-permute-start(f32[3,4,4,8,128]{4,3,2,1,0:T(8,128)} %get-tuple-element.37), channel_id=1, source_target_pairs={{0,8},{8,0},{16,24},{24,16},{1,9},{9,1},{17,25},{25,17},{2,10},{10... | collective-permute-start | bytes 589832 | tf_op jit(solution)/shard_map/ppermute | solution.py:62
  8.0 11.6 %collective-permute-start.1 = (f32[3,4,4,8,128]{4,3,2,1,0:T(8,128)}, f32[3,4,4,8,128]{4,3,2,1,0:T(8,128)S(1)}, u32[]{:S(2)}, u32[]{:S(2)}) collective-permute-start(f32[3,4,4,8,128]{4,3,2,1,0:T(8,128)} %get-tuple-element.38), channel_id=1, source_target_pairs={{0,24},{8,16},{16,8},{24,0},{1,25},{9,17},{17,9},{25,1},{2,26},{10... | collective-permute-start | bytes 589832 | tf_op jit(solution)/shard_map/ppermute | solution.py:63
  10.3 13.7 %all-to-all-start = ((f32[8,5,8,128]{3,2,1,0:T(8,128)}), f32[8,5,8,128]{3,2,1,0:T(8,128)S(1)}, u32[]{:S(2)}, u32[]{:S(2)}) async-start(f32[8,5,8,128]{3,2,1,0:T(8,128)} %get-tuple-element.35), calls=%async_computation | async-start | bytes 327680 | tf_op jit(solution)/shard_map/all_to_all | solution.py:746
  14.0 5.6 %copy-start = (f32[3,4,4,8,128]{4,3,2,1,0:T(8,128)}, f32[3,4,4,8,128]{4,3,2,1,0:T(8,128)S(1)}, u32[]{:S(2)}) copy-start(f32[3,4,4,8,128]{4,3,2,1,0:T(8,128)S(1)} %collective-permute-done.refs_3_) | copy-start | bytes 589828
  19.6 0.7 copy-start.1
  22.4 28.3 %collective-permute-start.2 = (f32[3,24,8,128]{3,2,1,0:T(8,128)}, f32[3,24,8,128]{3,2,1,0:T(8,128)S(1)}, u32[]{:S(2)}, u32[]{:S(2)}) collective-permute-start(f32[3,24,8,128]{3,2,1,0:T(8,128)} %get-tuple-element.39), channel_id=1, source_target_pairs={{0,2},{2,0},{4,6},{6,4},{1,3},{3,1},{5,7},{7,5},{8,10},{10,8},{12,... | collective-permute-start | bytes 884744 | tf_op jit(solution)/shard_map/ppermute | solution.py:62
  22.4 28.3 %collective-permute-start.3 = (f32[3,24,8,128]{3,2,1,0:T(8,128)}, f32[3,24,8,128]{3,2,1,0:T(8,128)S(1)}, u32[]{:S(2)}, u32[]{:S(2)}) collective-permute-start(f32[3,24,8,128]{3,2,1,0:T(8,128)} %get-tuple-element.40), channel_id=1, source_target_pairs={{0,6},{2,4},{4,2},{6,0},{1,7},{3,5},{5,3},{7,1},{8,14},{10,12},{12... | collective-permute-start | bytes 884744 | tf_op jit(solution)/shard_map/ppermute | solution.py:63
  24.0 0.7 copy-start.6
  48.0 15.5 %collective-permute-start.5 = (f32[16,8,128]{2,1,0:T(8,128)}, f32[16,8,128]{2,1,0:T(8,128)S(1)}, u32[]{:S(2)}, u32[]{:S(2)}) collective-permute-start(f32[16,8,128]{2,1,0:T(8,128)} %get-tuple-element.47), channel_id=1, source_target_pairs={{0,8},{8,0},{16,24},{24,16},{1,9},{9,1},{17,25},{25,17},{2,10},{10... | collective-permute-start | bytes 196616 | tf_op jit(solution)/shard_map/ppermute | solution.py:62
  48.0 15.5 %collective-permute-start.6 = (f32[16,8,128]{2,1,0:T(8,128)}, f32[16,8,128]{2,1,0:T(8,128)S(1)}, u32[]{:S(2)}, u32[]{:S(2)}) collective-permute-start(f32[16,8,128]{2,1,0:T(8,128)} %get-tuple-element.48), channel_id=1, source_target_pairs={{0,24},{8,16},{16,8},{24,0},{1,25},{9,17},{17,9},{25,1},{2,26},{10... | collective-permute-start | bytes 196616 | tf_op jit(solution)/shard_map/ppermute | solution.py:63
  50.7 0.7 copy-start.2
  51.5 0.7 copy-start.3
  54.7 4.3 %collective-permute-start.4 = (f32[3,4,8,128]{3,2,1,0:T(8,128)}, f32[3,4,8,128]{3,2,1,0:T(8,128)S(1)}, u32[]{:S(2)}, u32[]{:S(2)}) collective-permute-start(f32[3,4,8,128]{3,2,1,0:T(8,128)} %fixed_z.1), channel_id=1, source_target_pairs={{0,1},{1,0},{2,3},{3,2},{4,5},{5,4},{6,7},{7,6},{8,9},{9,8},{10,11... | collective-permute-start | bytes 147464 | tf_op jit(solution)/shard_map/ppermute | solution.py:62
  59.0 0.6 copy-start.15
  63.4 0.6 copy-start.11
  63.5 0.6 copy-start.12
  94.1 3.6 %copy-start.19 = (f32[1,4,4,8,128]{4,3,2,1,0:T(8,128)S(1)}, f32[1,4,4,8,128]{4,3,2,1,0:T(8,128)}, u32[]{:S(2)}) copy-start(f32[1,4,4,8,128]{4,3,2,1,0:T(8,128)} %get-tuple-element.51) | copy-start | bytes 196612
  94.1 4.3 %copy-start.18 = (f32[1,4,4,8,128]{4,3,2,1,0:T(8,128)S(1)}, f32[1,4,4,8,128]{4,3,2,1,0:T(8,128)}, u32[]{:S(2)}) copy-start(f32[1,4,4,8,128]{4,3,2,1,0:T(8,128)} %get-tuple-element.52) | copy-start | bytes 196612
  94.1 14.7 %all-to-all-start.3 = ((f32[8,8,8,128]{3,2,1,0:T(8,128)}), f32[8,8,8,128]{3,2,1,0:T(8,128)S(1)}, u32[]{:S(2)}, u32[]{:S(2)}) async-start(f32[8,8,8,128]{3,2,1,0:T(8,128)} %get-tuple-element.58), calls=%async_computation.3 | async-start | bytes 524288 | tf_op jit(solution)/shard_map/all_to_all | solution.py:746
  97.7 4.4 %collective-permute-start.7 = (f32[1,4,4,8,128]{4,3,2,1,0:T(8,128)S(1)}, f32[1,4,4,8,128]{4,3,2,1,0:T(8,128)S(1)}, u32[]{:S(2)}, u32[]{:S(2)}) collective-permute-start(f32[1,4,4,8,128]{4,3,2,1,0:T(8,128)S(1)} %copy-done.19), channel_id=1, source_target_pairs={{0,8},{8,0},{16,24},{24,16},{1,9},{9,1},{17,25},{25,17},{2,10},{10... | collective-permute-start | bytes 196616 | tf_op jit(solution)/shard_map/ppermute | solution.py:62
  98.4 6.1 %collective-permute-start.8 = (f32[1,4,4,8,128]{4,3,2,1,0:T(8,128)S(1)}, f32[1,4,4,8,128]{4,3,2,1,0:T(8,128)S(1)}, u32[]{:S(2)}, u32[]{:S(2)}) collective-permute-start(f32[1,4,4,8,128]{4,3,2,1,0:T(8,128)S(1)} %copy-done.18), channel_id=1, source_target_pairs={{0,24},{8,16},{16,8},{24,0},{1,25},{9,17},{17,9},{25,1},{2,26},{10... | collective-permute-start | bytes 196616 | tf_op jit(solution)/shard_map/ppermute | solution.py:63
  102.1 2.4 %copy-start.7 = (f32[1,4,4,8,128]{4,3,2,1,0:T(8,128)}, f32[1,4,4,8,128]{4,3,2,1,0:T(8,128)S(1)}, u32[]{:S(2)}) copy-start(f32[1,4,4,8,128]{4,3,2,1,0:T(8,128)S(1)} %collective-permute-done.7.refs_1_) | copy-start | bytes 196612
  104.5 0.6 copy-start.8
  106.8 7.9 %collective-permute-start.9 = (f32[1,24,8,128]{3,2,1,0:T(8,128)}, f32[1,24,8,128]{3,2,1,0:T(8,128)S(1)}, u32[]{:S(2)}, u32[]{:S(2)}) collective-permute-start(f32[1,24,8,128]{3,2,1,0:T(8,128)} %get-tuple-element.53), channel_id=1, source_target_pairs={{0,2},{2,0},{4,6},{6,4},{1,3},{3,1},{5,7},{7,5},{8,10},{10,8},{12,... | collective-permute-start | bytes 294920 | tf_op jit(solution)/shard_map/ppermute | solution.py:62
  106.8 7.9 %collective-permute-start.10 = (f32[1,24,8,128]{3,2,1,0:T(8,128)}, f32[1,24,8,128]{3,2,1,0:T(8,128)S(1)}, u32[]{:S(2)}, u32[]{:S(2)}) collective-permute-start(f32[1,24,8,128]{3,2,1,0:T(8,128)} %get-tuple-element.54), channel_id=1, source_target_pairs={{0,6},{2,4},{4,2},{6,0},{1,7},{3,5},{5,3},{7,1},{8,14},{10,12},{12... | collective-permute-start | bytes 294920 | tf_op jit(solution)/shard_map/ppermute | solution.py:63
  108.8 0.7 copy-start.4
  112.8 12.0 %collective-permute-start.12 = (f32[16,8,128]{2,1,0:T(8,128)}, f32[16,8,128]{2,1,0:T(8,128)S(1)}, u32[]{:S(2)}, u32[]{:S(2)}) collective-permute-start(f32[16,8,128]{2,1,0:T(8,128)} %get-tuple-element.60), channel_id=1, source_target_pairs={{0,8},{8,0},{16,24},{24,16},{1,9},{9,1},{17,25},{25,17},{2,10},{10... | collective-permute-start | bytes 196616 | tf_op jit(solution)/shard_map/ppermute | solution.py:62
  113.7 11.0 %collective-permute-start.13 = (f32[16,8,128]{2,1,0:T(8,128)}, f32[16,8,128]{2,1,0:T(8,128)S(1)}, u32[]{:S(2)}, u32[]{:S(2)}) collective-permute-start(f32[16,8,128]{2,1,0:T(8,128)} %get-tuple-element.61), channel_id=1, source_target_pairs={{0,24},{8,16},{16,8},{24,0},{1,25},{9,17},{17,9},{25,1},{2,26},{10... | collective-permute-start | bytes 196616 | tf_op jit(solution)/shard_map/ppermute | solution.py:63
  114.6 0.6 copy-start.9
  115.3 0.6 copy-start.10
  117.9 3.9 %collective-permute-start.11 = (f32[1,4,8,128]{3,2,1,0:T(8,128)}, f32[1,4,8,128]{3,2,1,0:T(8,128)S(1)}, u32[]{:S(2)}, u32[]{:S(2)}) collective-permute-start(f32[1,4,8,128]{3,2,1,0:T(8,128)} %next_z.1), channel_id=1, source_target_pairs={{0,1},{1,0},{2,3},{3,2},{4,5},{5,4},{6,7},{7,6},{8,9},{9,8},{10,11... | collective-permute-start | bytes 49160 | tf_op jit(solution)/shard_map/ppermute | solution.py:62
  121.8 0.6 copy-start.16
  124.7 0.6 copy-start.13
  124.8 0.7 copy-start.14
  136.8 8.7 %all-to-all-start.4 = ((f32[8,5,8,128]{3,2,1,0:T(8,128)}), f32[8,5,8,128]{3,2,1,0:T(8,128)S(1)}, u32[]{:S(2)}, u32[]{:S(2)}) async-start(f32[8,5,8,128]{3,2,1,0:T(8,128)} %get-tuple-element.64), calls=%async_computation.4 | async-start | bytes 327680 | tf_op jit(solution)/shard_map/all_to_all | solution.py:746
  145.6 7.2 %copy-start.5 = (f32[8,5,8,128]{3,2,1,0:T(8,128)}, f32[8,5,8,128]{3,2,1,0:T(8,128)S(1)}, u32[]{:S(2)}) copy-start(f32[8,5,8,128]{3,2,1,0:T(8,128)S(1)} %all-to-all-done.4.got) | copy-start | bytes 491524
  147.6 3.6 %collective-permute-start.14 = (f32[8,2]{1,0:T(8,128)S(1)}, f32[8,2]{1,0:T(8,128)S(1)}, u32[]{:S(2)}, u32[]{:S(2)}) collective-permute-start(f32[8,2]{1,0:T(8,128)S(1)} %broadcast_in_dim.2), channel_id=1, source_target_pairs={{0,8},{8,0},{16,24},{24,16},{1,9},{9,1},{17,25},{25,17},{2,10},{10... | collective-permute-start | bytes 200 | tf_op jit(solution)/shard_map/ppermute | solution.py:869
  151.2 4.6 %collective-permute-start.15 = (f32[8,2]{1,0:T(8,128)S(1)}, f32[8,2]{1,0:T(8,128)S(1)}, u32[]{:S(2)}, u32[]{:S(2)}) collective-permute-start(f32[8,2]{1,0:T(8,128)S(1)} %broadcast_add_fusion), channel_id=1, source_target_pairs={{0,16},{8,24},{16,0},{24,8},{1,17},{9,25},{17,1},{25,9},{2,18},{10... | collective-permute-start | bytes 200 | tf_op jit(solution)/shard_map/ppermute | solution.py:869

commit v2 on v1

--- a/solution.py
+++ b/solution.py
@@ -35,6 +35,7 @@
         out_shape=[shape for _, shape in outs],
         scratch_shapes=list(scratch),
         cost_estimate=pl.CostEstimate(flops=flops, transcendentals=0, bytes_accessed=0),
+        compiler_params=pltpu.CompilerParams(vmem_limit_bytes=16 << 20),
     )(*[value for _, value in ins])
 
 

time: 158 us -> 137 us (0.87)
  Pallas kernels: 68 us -> 48.4 us
  blocking collectives: 19.8 us -> 17 us
  waiting for transfers between devices: 21.8 us -> 24.1 us
    pallas_call x14, Pallas kernels: 68 us -> 48.4 us  [call(): pl.pallas_call(body, name=name, in_specs=[spec for spec, _ in ins], out_s...]
    all_to_all x2, blocking collectives: 19.8 us -> 17 us  [exchange(): lax.all_to_all(value, GROUP_AXES, split_axis=0, concat_axis=0, tiled=True)]
    ppermute x2, waiting for transfers between devices: 2.48 us -> 4.27 us  [local(): lax.ppermute(total, 'gx', [(i, i ^ bit) for i in range(size_x)])]
    unnamed x41 -> x55, local copies, waits for them, and re-layouts: 9.18 us -> 10.5 us
  transfers between devices with their start and end apart: 19 -> 19, of which waited for: 7 -> 8; matrix products, arithmetic and copies ran while one was open for 1% -> 1% of each run, Pallas kernels for 22% -> 15%
where the time goes in v2:
time: 137 us; the launch traced here: 136 us
  Pallas kernels  48.4 us (35%)
  starting transfers between devices  31.9 us (23%)
  waiting for transfers between devices  24.1 us (18%)
  blocking collectives  17 us (12%)
  local copies, waits for them, and re-layouts  10.5 us (8%)
  other arithmetic  3.3 us (2%)
    pallas_call x14, Pallas kernels, call(): pl.pallas_call(body, name=name, in_specs=[spec for spec, _ in ins], out_s...  48.4 us
    all_to_all x2, blocking collectives, exchange(): lax.all_to_all(value, GROUP_AXES, split_axis=0, concat_axis=0, tiled=True)  17 us
    ppermute x6, starting transfers between devices, swap(): got_b = lax.ppermute(second, axis, pairs_b) if count > 2 else got_a  11.4 us
    all_to_all x3, starting transfers between devices, exchange(): lax.all_to_all(value, GROUP_AXES, split_axis=0, concat_axis=0, tiled=True)  10.8 us
    unnamed x55, local copies, waits for them, and re-layouts  10.5 us
    ppermute x8, starting transfers between devices, swap(): got_a = lax.ppermute(first, axis, pairs_a)  8.3 us
    ppermute x8, waiting for transfers between devices, swap(): got_a = lax.ppermute(first, axis, pairs_a)  8.12 us
    ppermute x6, waiting for transfers between devices, swap(): got_b = lax.ppermute(second, axis, pairs_b) if count > 2 else got_a  7.06 us
  transfers between devices with their start and end apart: 19, of which 8 were waited for; matrix products, arithmetic and copies ran while one was open for 1% of the time, Pallas kernels for 15%

profile of v2, /device:TPU:0, one launch (start us, length us, event | category | flops | bytes accessed | tf_op | source)
XLA Modules:
  0.0 136.1 jit_solution(3267006648316091598)
XLA Ops:
  0.6 0.7 copy-done.26
  1.3 0.1 copy.11.corner
  1.4 0.1 pad_add_fusion.pos
  1.5 0.7 copy-done.23
  2.1 0.9 copy-done
  3.1 0.9 copy-done.2
  4.0 0.9 copy-done.4
  5.0 1.6 %send_start.1 = (f32[8,5,8,128]{3,2,1,0:T(8,128)}, f32[3,4,4,8,128]{4,3,2,1,0:T(8,128)S(1)}, f32[3,4,4,8,128]{4,3,2,1,0:T(8,128)S(1)}) custom-call(s32[3]{0:T(128)S(1)} %pad_add_fusion.pos, s32[1,4,3]{2,1,0:T(4,128)S(1)} %copy.11.corner, s32[1,4]{1,0:T(1,128)S(1)} %copy-done.23, f32[16,4,8,128]{3,2,1,0:T(8,128)S(1)} %bitcast.31, ...), custom_call_target="tpu_custom_call" | custom-call | tf_op jit(solution)/shard_map/send_start/pallas_call | solution.py:30
  6.6 3.2 %collective-permute-start = (f32[3,4,4,8,128]{4,3,2,1,0:T(8,128)S(1)}, f32[3,4,4,8,128]{4,3,2,1,0:T(8,128)S(1)}, u32[]{:S(2)}, u32[]{:S(2)}) collective-permute-start(f32[3,4,4,8,128]{4,3,2,1,0:T(8,128)S(1)} %get-tuple-element.37), channel_id=1, source_target_pairs={{0,8},{8,0},{16,24},{24,16},{1,9},{9,1},{17,25},{25,17},{2,10},{10... | collective-permute-start | bytes 589832 | tf_op jit(solution)/shard_map/ppermute | solution.py:63
  9.8 2.5 %collective-permute-start.1 = (f32[3,4,4,8,128]{4,3,2,1,0:T(8,128)S(1)}, f32[3,4,4,8,128]{4,3,2,1,0:T(8,128)S(1)}, u32[]{:S(2)}, u32[]{:S(2)}) collective-permute-start(f32[3,4,4,8,128]{4,3,2,1,0:T(8,128)S(1)} %get-tuple-element.38), channel_id=1, source_target_pairs={{0,24},{8,16},{16,8},{24,0},{1,25},{9,17},{17,9},{25,1},{2,26},{10... | collective-permute-start | bytes 589832 | tf_op jit(solution)/shard_map/ppermute | solution.py:64
  12.3 3.7 %all-to-all-start = ((f32[8,5,8,128]{3,2,1,0:T(8,128)}), f32[8,5,8,128]{3,2,1,0:T(8,128)S(1)}, u32[]{:S(2)}, u32[]{:S(2)}) async-start(f32[8,5,8,128]{3,2,1,0:T(8,128)} %get-tuple-element.35), calls=%async_computation | async-start | bytes 327680 | tf_op jit(solution)/shard_map/all_to_all | solution.py:747
  16.0 0.0 copy-start.9
  16.0 5.1 %collective-permute-done.1.refs_4_ = f32[3,4,4,8,128]{4,3,2,1,0:T(8,128)S(1)} collective-permute-done((f32[3,4,4,8,128]{4,3,2,1,0:T(8,128)S(1)}, f32[3,4,4,8,128]{4,3,2,1,0:T(8,128)S(1)}, u32[]{:S(2)}, u32[]{:S(2)}) %collective-permute-start.1) | collective-permute-done | bytes 196640 | tf_op jit(solution)/shard_map/ppermute | solution.py:64
  21.1 0.0 copy-start.11
  21.1 1.3 fixed_y.1
  22.4 1.6 %collective-permute-start.3 = (f32[3,24,8,128]{3,2,1,0:T(8,128)S(1)}, f32[3,24,8,128]{3,2,1,0:T(8,128)S(1)}, u32[]{:S(2)}, u32[]{:S(2)}) collective-permute-start(f32[3,24,8,128]{3,2,1,0:T(8,128)S(1)} %get-tuple-element.40), channel_id=1, source_target_pairs={{0,6},{2,4},{4,2},{6,0},{1,7},{3,5},{5,3},{7,1},{8,14},{10,12},{12... | collective-permute-start | bytes 884744 | tf_op jit(solution)/shard_map/ppermute | solution.py:64
  24.1 0.0 copy-start.19
  24.1 1.0 copy-done.19
  25.1 8.5 %fine_first.1 = (f32[8,8,8,128]{3,2,1,0:T(8,128)S(1)}, f32[4,34,8,128]{3,2,1,0:T(8,128)S(1)}, f32[4,16,8,128]{3,2,1,0:T(8,128)S(1)}, f32[8,128]{1,0:T(8,128)S(1)}, s32[8,16]{1,0:T(8,128)S(1)}) custom-call(s32[3]{0:T(128)S(1)} %pad_add_fusion.pos, f32[8,5,8,128]{3,2,1,0:T(8,128)S(1)} %all-to-all-done.refs_0_, f32[1024,128]{1,0:T(8,128)S(1)} %bitcast.43, ...), custom_call_target="tpu_custom_call" | custom-call | tf_op jit(solution)/shard_map/fine_first/pallas_call | solution.py:30
  33.7 8.9 %all_to_all.25.got = f32[8,8,8,128]{3,2,1,0:T(8,128)S(1)} all-to-all(f32[8,8,8,128]{3,2,1,0:T(8,128)S(1)} %get-tuple-element.45), channel_id=1, replica_groups=mesh['gx'=4,'gy'=4,'gz'=2] {'gy','gz'}, dimensions={0} | all-to-all | bytes 524288 | tf_op jit(solution)/shard_map/all_to_all | solution.py:747
  42.6 2.1 %place.2 = (f32[16,2,5,8,128]{4,3,2,1,0:T(8,128)S(1)}, f32[16,8,128]{2,1,0:T(8,128)S(1)}, f32[16,8,128]{2,1,0:T(8,128)S(1)}) custom-call(s32[3]{0:T(128)S(1)} %pad_add_fusion.pos, s32[8,16]{1,0:T(8,128)S(1)} %get-tuple-element.36.table.refs_0_, f32[8,8,8,128]{3,2,1,0:T(8,128)S(1)} %all_to_all.25.got), custom_call_target="tpu_custom_call" | custom-call | tf_op jit(solution)/shard_map/place/pallas_call | solution.py:30
  44.7 1.0 collective-permute-start.5
  45.8 2.4 %collective-permute-start.6 = (f32[16,8,128]{2,1,0:T(8,128)S(1)}, f32[16,8,128]{2,1,0:T(8,128)S(1)}, u32[]{:S(2)}, u32[]{:S(2)}) collective-permute-start(f32[16,8,128]{2,1,0:T(8,128)S(1)} %get-tuple-element.48), channel_id=1, source_target_pairs={{0,24},{8,16},{16,8},{24,0},{1,25},{9,17},{17,9},{25,1},{2,26},{10... | collective-permute-start | bytes 196616 | tf_op jit(solution)/shard_map/ppermute | solution.py:64
  48.2 1.0 fixed_z.1
  49.2 1.0 collective-permute-start.4
  50.2 3.2 %collective-permute-done.4.refs_7_ = f32[3,4,8,128]{3,2,1,0:T(8,128)S(1)} collective-permute-done((f32[3,4,8,128]{3,2,1,0:T(8,128)S(1)}, f32[3,4,8,128]{3,2,1,0:T(8,128)S(1)}, u32[]{:S(2)}, u32[]{:S(2)}) %collective-permute-start.4) | collective-permute-done | bytes 49184 | tf_op jit(solution)/shard_map/ppermute | solution.py:63
  53.4 0.9 copy-done.12
  54.3 1.0 copy-done.14
  55.3 1.0 copy-done.16
  56.2 1.0 fixed_all.1
  57.3 0.0 copy-start.10
  57.3 9.0 %coarse.2 = (f32[16,4,8,128]{3,2,1,0:T(8,128)S(1)}, f32[8,5,8,128]{3,2,1,0:T(8,128)S(1)}, f32[1,4,4,8,128]{4,3,2,1,0:T(8,128)S(1)}, f32[1,4,4,8,128]{4,3,2,1,0:T(8,128)S(1)}) custom-call(s32[3]{0:T(128)S(1)} %pad_add_fusion.pos, s32[8,16]{1,0:T(8,128)S(1)} %get-tuple-element.36.table.refs_0_, f32[24,2,40,128]{3,2,1,0:T(8,128)S(1)} %get-tuple-element.41.wide, ...), custom_call_target="tpu_custom_call" | custom-call | tf_op jit(solution)/shard_map/coarse/pallas_call | solution.py:30
  66.4 8.1 %all_to_all.26.refs_1_ = f32[8,5,8,128]{3,2,1,0:T(8,128)S(1)} all-to-all(f32[8,5,8,128]{3,2,1,0:T(8,128)S(1)} %get-tuple-element.55), channel_id=1, replica_groups=mesh['gx'=4,'gy'=4,'gz'=2] {'gy','gz'}, dimensions={0} | all-to-all | bytes 327680 | tf_op jit(solution)/shard_map/all_to_all | solution.py:747
  74.4 7.2 %fine_next.1 = (f32[8,8,8,128]{3,2,1,0:T(8,128)S(1)}, f32[4,34,8,128]{3,2,1,0:T(8,128)S(1)}, f32[4,16,8,128]{3,2,1,0:T(8,128)S(1)}, f32[8,128]{1,0:T(8,128)S(1)}) custom-call(s32[3]{0:T(128)S(1)} %pad_add_fusion.pos, s32[8,16]{1,0:T(8,128)S(1)} %get-tuple-element.36.table.refs_0_, f32[8,5,8,128]{3,2,1,0:T(8,128)S(1)} %all_to_all.26.refs_1_, ...), custom_call_target="tpu_custom_call" | custom-call | tf_op jit(solution)/shard_map/fine_next/pallas_call | solution.py:30
  81.7 0.8 copy-done.17
  82.5 0.7 copy-done.20
  83.2 0.7 copy-done.21
  83.9 3.5 %all-to-all-start.3 = ((f32[8,8,8,128]{3,2,1,0:T(8,128)}), f32[8,8,8,128]{3,2,1,0:T(8,128)S(1)}, u32[]{:S(2)}, u32[]{:S(2)}) async-start(f32[8,8,8,128]{3,2,1,0:T(8,128)} %copy-done.20), calls=%async_computation.3 | async-start | bytes 524288 | tf_op jit(solution)/shard_map/all_to_all | solution.py:747
  87.5 0.1 collective-permute-start.7
  87.6 1.8 %collective-permute-start.8 = (f32[1,4,4,8,128]{4,3,2,1,0:T(8,128)S(1)}, f32[1,4,4,8,128]{4,3,2,1,0:T(8,128)S(1)}, u32[]{:S(2)}, u32[]{:S(2)}) collective-permute-start(f32[1,4,4,8,128]{4,3,2,1,0:T(8,128)S(1)} %get-tuple-element.52), channel_id=1, source_target_pairs={{0,24},{8,16},{16,8},{24,0},{1,25},{9,17},{17,9},{25,1},{2,26},{10... | collective-permute-start | bytes 196616 | tf_op jit(solution)/shard_map/ppermute | solution.py:64
  89.4 2.5 %collective-permute-done.7.refs_1_ = f32[1,4,4,8,128]{4,3,2,1,0:T(8,128)S(1)} collective-permute-done((f32[1,4,4,8,128]{4,3,2,1,0:T(8,128)S(1)}, f32[1,4,4,8,128]{4,3,2,1,0:T(8,128)S(1)}, u32[]{:S(2)}, u32[]{:S(2)}) %collective-permute-start.7) | collective-permute-done | bytes 65568 | tf_op jit(solution)/shard_map/ppermute | solution.py:63
  91.9 2.0 %collective-permute-done.8.refs_2_ = f32[1,4,4,8,128]{4,3,2,1,0:T(8,128)S(1)} collective-permute-done((f32[1,4,4,8,128]{4,3,2,1,0:T(8,128)S(1)}, f32[1,4,4,8,128]{4,3,2,1,0:T(8,128)S(1)}, u32[]{:S(2)}, u32[]{:S(2)}) %collective-permute-start.8) | collective-permute-done | bytes 65568 | tf_op jit(solution)/shard_map/ppermute | solution.py:64
  93.9 0.6 next_y.1
  94.4 0.1 collective-permute-start.9
  94.5 1.8 %collective-permute-start.10 = (f32[1,24,8,128]{3,2,1,0:T(8,128)S(1)}, f32[1,24,8,128]{3,2,1,0:T(8,128)S(1)}, u32[]{:S(2)}, u32[]{:S(2)}) collective-permute-start(f32[1,24,8,128]{3,2,1,0:T(8,128)S(1)} %get-tuple-element.54), channel_id=1, source_target_pairs={{0,6},{2,4},{4,2},{6,0},{1,7},{3,5},{5,3},{7,1},{8,14},{10,12},{12... | collective-permute-start | bytes 294920 | tf_op jit(solution)/shard_map/ppermute | solution.py:64
  96.3 2.1 %place.3 = (f32[16,2,5,8,128]{4,3,2,1,0:T(8,128)S(1)}, f32[16,8,128]{2,1,0:T(8,128)S(1)}, f32[16,8,128]{2,1,0:T(8,128)S(1)}) custom-call(s32[3]{0:T(128)S(1)} %pad_add_fusion.pos, s32[8,16]{1,0:T(8,128)S(1)} %get-tuple-element.36.table.refs_0_, f32[8,8,8,128]{3,2,1,0:T(8,128)S(1)} %all-to-all-done.3.got), custom_call_target="tpu_custom_call" | custom-call | tf_op jit(solution)/shard_map/place/pallas_call | solution.py:30
  98.5 1.6 %collective-permute-start.12 = (f32[16,8,128]{2,1,0:T(8,128)S(1)}, f32[16,8,128]{2,1,0:T(8,128)S(1)}, u32[]{:S(2)}, u32[]{:S(2)}) collective-permute-start(f32[16,8,128]{2,1,0:T(8,128)S(1)} %get-tuple-element.60), channel_id=1, source_target_pairs={{0,8},{8,0},{16,24},{24,16},{1,9},{9,1},{17,25},{25,17},{2,10},{10... | collective-permute-start | bytes 196616 | tf_op jit(solution)/shard_map/ppermute | solution.py:63
  100.1 1.3 collective-permute-start.13
  101.3 0.8 next_z.1
  102.1 1.3 collective-permute-start.11
  103.5 2.5 %collective-permute-done.11.refs_5_ = f32[1,4,8,128]{3,2,1,0:T(8,128)S(1)} collective-permute-done((f32[1,4,8,128]{3,2,1,0:T(8,128)S(1)}, f32[1,4,8,128]{3,2,1,0:T(8,128)S(1)}, u32[]{:S(2)}, u32[]{:S(2)}) %collective-permute-start.11) | collective-permute-done | bytes 16416 | tf_op jit(solution)/shard_map/ppermute | solution.py:63
  105.9 0.8 next_all.1.wide
  106.8 9.8 %coarse.3 = (f32[16,4,8,128]{3,2,1,0:T(8,128)}, f32[8,5,8,128]{3,2,1,0:T(8,128)}) custom-call(s32[3]{0:T(128)S(1)} %pad_add_fusion.pos, s32[8,16]{1,0:T(8,128)S(1)} %get-tuple-element.36.table.refs_0_, f32[24,2,40,128]{3,2,1,0:T(8,128)S(1)} %next_all.1.wide, f32[24,2,40,128]{3,2,1,0:T(8,128)S(1)} %get-tuple-element.42.diag, ...), custom_call_target="tpu_custom_call" | custom-call | tf_op jit(solution)/shard_map/coarse/pallas_call | solution.py:30
  116.5 3.5 %all-to-all-start.4 = ((f32[8,5,8,128]{3,2,1,0:T(8,128)}), f32[8,5,8,128]{3,2,1,0:T(8,128)S(1)}, u32[]{:S(2)}, u32[]{:S(2)}) async-start(f32[8,5,8,128]{3,2,1,0:T(8,128)} %get-tuple-element.64), calls=%async_computation.4 | async-start | bytes 327680 | tf_op jit(solution)/shard_map/all_to_all | solution.py:747
  120.1 0.7 slice_reduce_fusion.1
  120.8 4.7 %all-to-all-done.4.got = f32[8,5,8,128]{3,2,1,0:T(8,128)S(1)} async-done(((f32[8,5,8,128]{3,2,1,0:T(8,128)}), f32[8,5,8,128]{3,2,1,0:T(8,128)S(1)}, u32[]{:S(2)}, u32[]{:S(2)}) %all-to-all-start.4) | async-done | bytes 163872 | tf_op jit(solution)/shard_map/all_to_all | solution.py:747
  125.4 0.6 slice_reduce_fusion
  126.0 1.4 %pad_maximum_fusion = f32[2]{0:T(128)S(1)} fusion(f32[1]{0:T(128)} %bitcast.24, f32[1]{0:T(128)} %bitcast.23), kind=kLoop, calls=%fused_computation.4 | loop fusion | flops 2 | bytes 16 | tf_op jit(solution)/shard_map/stack | solution.py:867
  127.4 0.3 collective-permute-start.14
  127.8 3.3 %collective-permute-done.14 = f32[8,2]{1,0:T(8,128)S(1)} collective-permute-done((f32[8,2]{1,0:T(8,128)S(1)}, f32[8,2]{1,0:T(8,128)S(1)}, u32[]{:S(2)}, u32[]{:S(2)}) %collective-permute-start.14) | collective-permute-done | bytes 96 | tf_op jit(solution)/shard_map/ppermute | solution.py:870
  131.1 1.1 collective-permute-start.15
  132.1 2.4 %last.1 = f32[1024,128]{1,0:T(8,128)} custom-call(s32[3]{0:T(128)S(1)} %pad_add_fusion.pos, s32[8,16]{1,0:T(8,128)S(1)} %get-tuple-element.36.table.refs_0_, f32[8,5,8,128]{3,2,1,0:T(8,128)S(1)} %all-to-all-done.4.got, f32[4,34,8,128]{3,2,1,0:T(8,128)S(1)} %copy-done.18, f32[4,16,8,128]{3,2,1,0:T(8,128)S(1)} %copy-done.22), custom_call_target="tpu_custom_call" | custom-call | tf_op jit(solution)/shard_map/last/pallas_call | solution.py:30
  134.6 1.0 collective-permute-done.15
  135.6 0.5 sqrt_bitcast_fusion
  (53 shorter events, 0.1 us)
Async XLA Ops:
  0.6 0.7 copy-start.26
  1.5 0.7 copy-start.23
  2.1 0.9 copy-start
  3.1 0.9 copy-start.2
  4.0 0.9 copy-start.4
  5.0 16.1 %copy-start.3 = (f32[16,32,128]{2,1,0:T(8,128)S(1)}, f32[16,32,128]{2,1,0:T(8,128)}, u32[]{:S(2)}) copy-start(f32[16,32,128]{2,1,0:T(8,128)} %param.9) | copy-start | bytes 786436
  5.0 16.1 %copy-start.5 = (f32[16,32,128]{2,1,0:T(8,128)S(1)}, f32[16,32,128]{2,1,0:T(8,128)}, u32[]{:S(2)}) copy-start(f32[16,32,128]{2,1,0:T(8,128)} %param.8) | copy-start | bytes 786436
  6.6 14.5 %copy-start.1 = (f32[16,32,128]{2,1,0:T(8,128)S(1)}, f32[16,32,128]{2,1,0:T(8,128)}, u32[]{:S(2)}) copy-start(f32[16,32,128]{2,1,0:T(8,128)} %param.10) | copy-start | bytes 786436
  6.6 9.4 %collective-permute-start = (f32[3,4,4,8,128]{4,3,2,1,0:T(8,128)S(1)}, f32[3,4,4,8,128]{4,3,2,1,0:T(8,128)S(1)}, u32[]{:S(2)}, u32[]{:S(2)}) collective-permute-start(f32[3,4,4,8,128]{4,3,2,1,0:T(8,128)S(1)} %get-tuple-element.37), channel_id=1, source_target_pairs={{0,8},{8,0},{16,24},{24,16},{1,9},{9,1},{17,25},{25,17},{2,10},{10... | collective-permute-start | bytes 589832 | tf_op jit(solution)/shard_map/ppermute | solution.py:63
  9.8 11.3 %collective-permute-start.1 = (f32[3,4,4,8,128]{4,3,2,1,0:T(8,128)S(1)}, f32[3,4,4,8,128]{4,3,2,1,0:T(8,128)S(1)}, u32[]{:S(2)}, u32[]{:S(2)}) collective-permute-start(f32[3,4,4,8,128]{4,3,2,1,0:T(8,128)S(1)} %get-tuple-element.38), channel_id=1, source_target_pairs={{0,24},{8,16},{16,8},{24,0},{1,25},{9,17},{17,9},{25,1},{2,26},{10... | collective-permute-start | bytes 589832 | tf_op jit(solution)/shard_map/ppermute | solution.py:64
  12.3 11.8 %all-to-all-start = ((f32[8,5,8,128]{3,2,1,0:T(8,128)}), f32[8,5,8,128]{3,2,1,0:T(8,128)S(1)}, u32[]{:S(2)}, u32[]{:S(2)}) async-start(f32[8,5,8,128]{3,2,1,0:T(8,128)} %get-tuple-element.35), calls=%async_computation | async-start | bytes 327680 | tf_op jit(solution)/shard_map/all_to_all | solution.py:747
  16.0 8.1 %copy-start.8 = (f32[4,32768]{1,0:T(4,128)S(1)}, f32[4,32768]{1,0:T(4,128)}, u32[]{:S(2)}) copy-start(f32[4,32768]{1,0:T(4,128)} %param.11) | copy-start | bytes 1572868
  16.0 8.1 %copy-start.9 = (f32[4,32768]{1,0:T(4,128)S(1)}, f32[4,32768]{1,0:T(4,128)}, u32[]{:S(2)}) copy-start(f32[4,32768]{1,0:T(4,128)} %param.12) | copy-start | bytes 1572868
  21.1 27.0 %copy-start.11 = (f32[3,4,4,8,128]{4,3,2,1,0:T(8,128)}, f32[3,4,4,8,128]{4,3,2,1,0:T(8,128)S(1)}, u32[]{:S(2)}) copy-start(f32[3,4,4,8,128]{4,3,2,1,0:T(8,128)S(1)} %collective-permute-done.1.refs_4_) | copy-start | bytes 589828
  22.4 25.7 %collective-permute-start.2 = (f32[3,24,8,128]{3,2,1,0:T(8,128)}, f32[3,24,8,128]{3,2,1,0:T(8,128)S(1)}, u32[]{:S(2)}, u32[]{:S(2)}) collective-permute-start(f32[3,24,8,128]{3,2,1,0:T(8,128)} %get-tuple-element.39), channel_id=1, source_target_pairs={{0,2},{2,0},{4,6},{6,4},{1,3},{3,1},{5,7},{7,5},{8,10},{10,8},{12,... | collective-permute-start | bytes 884744 | tf_op jit(solution)/shard_map/ppermute | solution.py:63
  22.4 25.7 %collective-permute-start.3 = (f32[3,24,8,128]{3,2,1,0:T(8,128)S(1)}, f32[3,24,8,128]{3,2,1,0:T(8,128)S(1)}, u32[]{:S(2)}, u32[]{:S(2)}) collective-permute-start(f32[3,24,8,128]{3,2,1,0:T(8,128)S(1)} %get-tuple-element.40), channel_id=1, source_target_pairs={{0,6},{2,4},{4,2},{6,0},{1,7},{3,5},{5,3},{7,1},{8,14},{10,12},{12... | collective-permute-start | bytes 884744 | tf_op jit(solution)/shard_map/ppermute | solution.py:64
  24.1 1.0 copy-start.19
  44.7 12.6 %collective-permute-start.5 = (f32[16,8,128]{2,1,0:T(8,128)S(1)}, f32[16,8,128]{2,1,0:T(8,128)S(1)}, u32[]{:S(2)}, u32[]{:S(2)}) collective-permute-start(f32[16,8,128]{2,1,0:T(8,128)S(1)} %get-tuple-element.47), channel_id=1, source_target_pairs={{0,8},{8,0},{16,24},{24,16},{1,9},{9,1},{17,25},{25,17},{2,10},{10... | collective-permute-start | bytes 196616 | tf_op jit(solution)/shard_map/ppermute | solution.py:63
  45.8 11.5 %collective-permute-start.6 = (f32[16,8,128]{2,1,0:T(8,128)S(1)}, f32[16,8,128]{2,1,0:T(8,128)S(1)}, u32[]{:S(2)}, u32[]{:S(2)}) collective-permute-start(f32[16,8,128]{2,1,0:T(8,128)S(1)} %get-tuple-element.48), channel_id=1, source_target_pairs={{0,24},{8,16},{16,8},{24,0},{1,25},{9,17},{17,9},{25,1},{2,26},{10... | collective-permute-start | bytes 196616 | tf_op jit(solution)/shard_map/ppermute | solution.py:64
  48.1 1.1 copy-start.13
  48.2 1.1 copy-start.15
  49.2 4.2 %collective-permute-start.4 = (f32[3,4,8,128]{3,2,1,0:T(8,128)S(1)}, f32[3,4,8,128]{3,2,1,0:T(8,128)S(1)}, u32[]{:S(2)}, u32[]{:S(2)}) collective-permute-start(f32[3,4,8,128]{3,2,1,0:T(8,128)S(1)} %fixed_z.1), channel_id=1, source_target_pairs={{0,1},{1,0},{2,3},{3,2},{4,5},{5,4},{6,7},{7,6},{8,9},{9,8},{10,11... | collective-permute-start | bytes 147464 | tf_op jit(solution)/shard_map/ppermute | solution.py:63
  53.4 0.9 copy-start.12
  54.3 1.0 copy-start.14
  55.3 1.0 copy-start.16
  57.3 9.1 %copy-start.6 = (f32[24,2,40,128]{3,2,1,0:T(8,128)}, f32[24,2,40,128]{3,2,1,0:T(8,128)S(1)}, u32[]{:S(2)}) copy-start(f32[24,2,40,128]{3,2,1,0:T(8,128)S(1)} %get-tuple-element.44.source) | copy-start | bytes 2949124
  57.3 17.1 %copy-start.10 = (f32[4,32768]{1,0:T(4,128)S(1)}, f32[4,32768]{1,0:T(4,128)}, u32[]{:S(2)}) copy-start(f32[4,32768]{1,0:T(4,128)} %param.12) | copy-start | bytes 1572868
  66.4 8.1 %copy-start.24 = (f32[1,4,4,8,128]{4,3,2,1,0:T(8,128)}, f32[1,4,4,8,128]{4,3,2,1,0:T(8,128)S(1)}, u32[]{:S(2)}) copy-start(f32[1,4,4,8,128]{4,3,2,1,0:T(8,128)S(1)} %get-tuple-element.51) | copy-start | bytes 196612
  81.7 0.8 copy-start.17
  82.5 0.7 copy-start.20
  83.2 0.7 copy-start.21
  83.9 3.6 %copy-start.25 = (f32[1,4,4,8,128]{4,3,2,1,0:T(8,128)S(1)}, f32[1,4,4,8,128]{4,3,2,1,0:T(8,128)}, u32[]{:S(2)}) copy-start(f32[1,4,4,8,128]{4,3,2,1,0:T(8,128)} %copy-done.24) | copy-start | bytes 196612
  83.9 12.4 %all-to-all-start.3 = ((f32[8,8,8,128]{3,2,1,0:T(8,128)}), f32[8,8,8,128]{3,2,1,0:T(8,128)S(1)}, u32[]{:S(2)}, u32[]{:S(2)}) async-start(f32[8,8,8,128]{3,2,1,0:T(8,128)} %copy-done.20), calls=%async_computation.3 | async-start | bytes 524288 | tf_op jit(solution)/shard_map/all_to_all | solution.py:747
  87.5 4.4 %collective-permute-start.7 = (f32[1,4,4,8,128]{4,3,2,1,0:T(8,128)S(1)}, f32[1,4,4,8,128]{4,3,2,1,0:T(8,128)S(1)}, u32[]{:S(2)}, u32[]{:S(2)}) collective-permute-start(f32[1,4,4,8,128]{4,3,2,1,0:T(8,128)S(1)} %copy-done.25), channel_id=1, source_target_pairs={{0,8},{8,0},{16,24},{24,16},{1,9},{9,1},{17,25},{25,17},{2,10},{10... | collective-permute-start | bytes 196616 | tf_op jit(solution)/shard_map/ppermute | solution.py:63
  87.6 6.3 %collective-permute-start.8 = (f32[1,4,4,8,128]{4,3,2,1,0:T(8,128)S(1)}, f32[1,4,4,8,128]{4,3,2,1,0:T(8,128)S(1)}, u32[]{:S(2)}, u32[]{:S(2)}) collective-permute-start(f32[1,4,4,8,128]{4,3,2,1,0:T(8,128)S(1)} %get-tuple-element.52), channel_id=1, source_target_pairs={{0,24},{8,16},{16,8},{24,0},{1,25},{9,17},{17,9},{25,1},{2,26},{10... | collective-permute-start | bytes 196616 | tf_op jit(solution)/shard_map/ppermute | solution.py:64
  94.4 6.9 %collective-permute-start.9 = (f32[1,24,8,128]{3,2,1,0:T(8,128)S(1)}, f32[1,24,8,128]{3,2,1,0:T(8,128)S(1)}, u32[]{:S(2)}, u32[]{:S(2)}) collective-permute-start(f32[1,24,8,128]{3,2,1,0:T(8,128)S(1)} %get-tuple-element.53), channel_id=1, source_target_pairs={{0,2},{2,0},{4,6},{6,4},{1,3},{3,1},{5,7},{7,5},{8,10},{10,8},{12,... | collective-permute-start | bytes 294920 | tf_op jit(solution)/shard_map/ppermute | solution.py:63
  94.5 6.8 %collective-permute-start.10 = (f32[1,24,8,128]{3,2,1,0:T(8,128)S(1)}, f32[1,24,8,128]{3,2,1,0:T(8,128)S(1)}, u32[]{:S(2)}, u32[]{:S(2)}) collective-permute-start(f32[1,24,8,128]{3,2,1,0:T(8,128)S(1)} %get-tuple-element.54), channel_id=1, source_target_pairs={{0,6},{2,4},{4,2},{6,0},{1,7},{3,5},{5,3},{7,1},{8,14},{10,12},{12... | collective-permute-start | bytes 294920 | tf_op jit(solution)/shard_map/ppermute | solution.py:64
  98.5 8.3 %collective-permute-start.12 = (f32[16,8,128]{2,1,0:T(8,128)S(1)}, f32[16,8,128]{2,1,0:T(8,128)S(1)}, u32[]{:S(2)}, u32[]{:S(2)}) collective-permute-start(f32[16,8,128]{2,1,0:T(8,128)S(1)} %get-tuple-element.60), channel_id=1, source_target_pairs={{0,8},{8,0},{16,24},{24,16},{1,9},{9,1},{17,25},{25,17},{2,10},{10... | collective-permute-start | bytes 196616 | tf_op jit(solution)/shard_map/ppermute | solution.py:63
  100.1 6.7 %copy-start.7 = (f32[24,2,40,128]{3,2,1,0:T(8,128)S(1)}, f32[24,2,40,128]{3,2,1,0:T(8,128)}, u32[]{:S(2)}) copy-start(f32[24,2,40,128]{3,2,1,0:T(8,128)} %copy-done.6) | copy-start | bytes 2949124
  100.1 6.7 %collective-permute-start.13 = (f32[16,8,128]{2,1,0:T(8,128)S(1)}, f32[16,8,128]{2,1,0:T(8,128)S(1)}, u32[]{:S(2)}, u32[]{:S(2)}) collective-permute-start(f32[16,8,128]{2,1,0:T(8,128)S(1)} %get-tuple-element.61), channel_id=1, source_target_pairs={{0,24},{8,16},{16,8},{24,0},{1,25},{9,17},{17,9},{25,1},{2,26},{10... | collective-permute-start | bytes 196616 | tf_op jit(solution)/shard_map/ppermute | solution.py:64
  102.1 3.8 %collective-permute-start.11 = (f32[1,4,8,128]{3,2,1,0:T(8,128)S(1)}, f32[1,4,8,128]{3,2,1,0:T(8,128)S(1)}, u32[]{:S(2)}, u32[]{:S(2)}) collective-permute-start(f32[1,4,8,128]{3,2,1,0:T(8,128)S(1)} %next_z.1), channel_id=1, source_target_pairs={{0,1},{1,0},{2,3},{3,2},{4,5},{5,4},{6,7},{7,6},{8,9},{9,8},{10,11... | collective-permute-start | bytes 49160 | tf_op jit(solution)/shard_map/ppermute | solution.py:63
  106.8 25.4 %copy-start.18 = (f32[4,34,8,128]{3,2,1,0:T(8,128)S(1)}, f32[4,34,8,128]{3,2,1,0:T(8,128)}, u32[]{:S(2)}) copy-start(f32[4,34,8,128]{3,2,1,0:T(8,128)} %copy-done.17) | copy-start | bytes 1671172
  116.5 15.6 %copy-start.22 = (f32[4,16,8,128]{3,2,1,0:T(8,128)S(1)}, f32[4,16,8,128]{3,2,1,0:T(8,128)}, u32[]{:S(2)}) copy-start(f32[4,16,8,128]{3,2,1,0:T(8,128)} %copy-done.21) | copy-start | bytes 786436
  116.5 8.9 %all-to-all-start.4 = ((f32[8,5,8,128]{3,2,1,0:T(8,128)}), f32[8,5,8,128]{3,2,1,0:T(8,128)S(1)}, u32[]{:S(2)}, u32[]{:S(2)}) async-start(f32[8,5,8,128]{3,2,1,0:T(8,128)} %get-tuple-element.64), calls=%async_computation.4 | async-start | bytes 327680 | tf_op jit(solution)/shard_map/all_to_all | solution.py:747
  127.4 3.6 %collective-permute-start.14 = (f32[8,2]{1,0:T(8,128)S(1)}, f32[8,2]{1,0:T(8,128)S(1)}, u32[]{:S(2)}, u32[]{:S(2)}) collective-permute-start(f32[8,2]{1,0:T(8,128)S(1)} %broadcast_in_dim.2), channel_id=1, source_target_pairs={{0,8},{8,0},{16,24},{24,16},{1,9},{9,1},{17,25},{25,17},{2,10},{10... | collective-permute-start | bytes 200 | tf_op jit(solution)/shard_map/ppermute | solution.py:870
  131.1 4.5 %collective-permute-start.15 = (f32[8,2]{1,0:T(8,128)S(1)}, f32[8,2]{1,0:T(8,128)S(1)}, u32[]{:S(2)}, u32[]{:S(2)}) collective-permute-start(f32[8,2]{1,0:T(8,128)S(1)} %broadcast_add_fusion), channel_id=1, source_target_pairs={{0,16},{8,24},{16,0},{24,8},{1,17},{9,25},{17,1},{25,9},{2,18},{10... | collective-permute-start | bytes 200 | tf_op jit(solution)/shard_map/ppermute | solution.py:870

commit v3 on v2

--- a/solution.py
+++ b/solution.py
@@ -5,6 +5,7 @@
 from jax.experimental.pallas import tpu as pltpu
 from jax.sharding import PartitionSpec as P
 
+
 FOOT = 16
 CYCLES = 2
 CSWEEPS = 4
@@ -15,10 +16,12 @@
 LANES = 128
 SIDE = 2 * FOOT
 WIDE = 4
+COLS = 8
 GROUP_AXES = ("gy", "gz")
 
 VMEM = pl.BlockSpec(memory_space=pltpu.VMEM)
 SMEM = pl.BlockSpec(memory_space=pltpu.SMEM)
+HBM = pl.BlockSpec(memory_space=pltpu.HBM)
 F32 = jnp.float32
 
 
@@ -26,17 +29,35 @@
     return jax.ShapeDtypeStruct(shape, dtype)
 
 
-def call(body, name, ins, outs, scratch=(), flops=0):
+def call(body, ins, outs, scratch=()):
+    values = [
+        pltpu.with_memory_space_constraint(value, pltpu.HBM) if spec is HBM else value
+        for spec, value in ins
+    ]
+    shapes = [pltpu.HBM(shape.shape, shape.dtype) if spec is HBM else shape for spec, shape in outs]
     return pl.pallas_call(
         body,
-        name=name,
         in_specs=[spec for spec, _ in ins],
         out_specs=[spec for spec, _ in outs],
-        out_shape=[shape for _, shape in outs],
+        out_shape=shapes,
         scratch_shapes=list(scratch),
-        cost_estimate=pl.CostEstimate(flops=flops, transcendentals=0, bytes_accessed=0),
         compiler_params=pltpu.CompilerParams(vmem_limit_bytes=16 << 20),
-    )(*[value for _, value in ins])
+    )(*values)
+
+
+def place_of():
+    return [lax.axis_index(axis) for axis in ("gx", "gy", "gz")]
+
+
+def fetch(copies):
+    for copy in copies:
+        copy.start()
+    return copies
+
+
+def arrive(copies):
+    for copy in copies:
+        copy.wait()
 
 
 def lane_id():
@@ -87,23 +108,20 @@
 
 
 def send_start_body(dims):
-    ex, nt, group, slots, nbx, nby, nbz = dims
-
-    def body(pos, corner, owner, start, shift, source, send, side_a, side_b):
-        odd = pos[0] % 2 == 1
-        for index, field in enumerate((start, shift, source)):
-            low = field[0:WIDE]
-            high = field[ex - WIDE : ex]
-            side_a[index] = jnp.where(odd, low, high)
-            side_b[index] = jnp.where(odd, high, low)
+    group, slots, nbx, nby, nbz = dims
+
+    def body(corner, owner, field, send, start, sem):
+        copy = pltpu.make_async_copy(field, start, sem)
+        copy.start()
+        pos = place_of()
         lanes = lane_id()
         note = jnp.zeros((SUB, LANES), F32)
         blocks = []
         for slot in range(slots):
             block = (
-                corner[0, slot, 0] // SIDE - pos[0] * nbx,
-                corner[0, slot, 1] // SIDE - pos[1] * nby,
-                corner[0, slot, 2] // SIDE - pos[2] * nbz,
+                corner[0, 0, slot] // SIDE - pos[0] * nbx,
+                corner[1, 0, slot] // SIDE - pos[1] * nby,
+                corner[2, 0, slot] // SIDE - pos[2] * nbz,
             )
             blocks.append(block)
             for index, value in enumerate((owner[0, slot],) + block):
@@ -111,6 +129,7 @@
         for target in range(group):
             send[target, 0:4] = jnp.zeros((4, SUB, LANES), F32)
             send[target, 4] = note
+        copy.wait()
         for slot in range(slots):
             target = owner[0, slot]
 
@@ -120,6 +139,24 @@
                     send[target, quad] = packed
 
                 extract(start, write, *blocks[slot])
+
+    return body
+
+
+def sides_body(ex):
+    def body(start, shift, source, side_a, side_b, sems):
+        pos = place_of()
+        odd = pos[0] % 2
+        copies = []
+        for index, field in enumerate((start, shift, source)):
+            for side, goal in enumerate((side_a, side_b)):
+                high = 1 - odd if side == 0 else odd
+                planes = field.at[pl.ds(high * (ex - WIDE), WIDE)]
+                copies.append(pltpu.make_async_copy(planes, goal.at[index], sems.at[index, side]))
+        for copy in copies:
+            copy.start()
+        for copy in copies:
+            copy.wait()
 
     return body
 
@@ -133,31 +170,69 @@
 
 
 def y_send_body(count, ex, nt):
-    def body(pos, *refs):
-        fields, (xa, xb, ya, yb) = refs[:count], refs[count:]
+    def body(*refs):
+        fields, (xa, xb, ya, yb) = refs[:count], refs[count : count + 4]
+        planes, sems = refs[count + 4 :]
+        pos = place_of()
         odd_x = pos[0] % 2 == 1
         odd_y = pos[1] % 2 == 1
+        copies = []
         for index in range(count):
-            for xi in range(ex + 2 * WIDE):
-                plane = x_plane(fields[index], xa.at[index], xb.at[index], odd_x, ex, xi)
-                low, high = plane[0], plane[nt - 1]
-                ya[index, xi] = jnp.where(odd_y, low, high)
-                yb[index, xi] = jnp.where(odd_y, high, low)
+            for side in range(2):
+                tile = fields[index].at[:, side * (nt - 1)]
+                copies.append(
+                    pltpu.make_async_copy(tile, planes.at[index, side], sems.at[index, side])
+                )
+        fetch(copies)
+        rows = sub_id()
+
+        def pair(index, xi):
+            found = []
+            for at in (xi, xi + 1):
+                if WIDE <= at < WIDE + ex:
+                    found.append((planes[index, 0, at - WIDE], planes[index, 1, at - WIDE]))
+                else:
+                    plane = x_plane(None, xa.at[index], xb.at[index], odd_x, ex, at)
+                    found.append((plane[0], plane[nt - 1]))
+            (low, high), (low_next, high_next) = found
+            low = jnp.where(rows < WIDE, low, pltpu.roll(low_next, WIDE, 0))
+            high = jnp.where(rows < WIDE, pltpu.roll(high, WIDE, 0), high_next)
+            ya[index, xi // 2] = jnp.where(odd_y, low, high)
+            yb[index, xi // 2] = jnp.where(odd_y, high, low)
+
+        edges = [*range(0, WIDE, 2), *range(WIDE + ex, 2 * WIDE + ex, 2)]
+        for index in range(count):
+            for xi in edges:
+                pair(index, xi)
+        arrive(copies)
+        for index in range(count):
+            for xi in range(WIDE, WIDE + ex, 2):
+                pair(index, xi)
 
     return body
 
 
 def seam_tile(ya, yb, odd_y, xi):
-    low = pick_low(odd_y, ya[xi], yb[xi])
-    high = pick_high(odd_y, ya[xi], yb[xi])
+    low = pick_low(odd_y, ya[xi // 2], yb[xi // 2])
+    high = pick_high(odd_y, ya[xi // 2], yb[xi // 2])
+    if xi % 2 == 0:
+        low = pltpu.roll(low, WIDE, 0)
+    else:
+        high = pltpu.roll(high, WIDE, 0)
     return jnp.where(sub_id() < WIDE, high, low)
 
 
-def z_send_body(count, ex, nt, both):
-    def body(pos, *refs):
-        fields, refs = refs[:count], refs[count:]
-        xa, xb, ya, yb = refs[:4]
-        outs = refs[4:]
+def z_send_body(count, ex, nt):
+    def body(*refs):
+        raw, (xa, xb, ya, yb) = refs[:count], refs[count : count + 4]
+        outs = refs[count + 4 : -2]
+        fields, sems = refs[-2:]
+        copies = [
+            pltpu.make_async_copy(raw[index], fields.at[index], sems.at[index])
+            for index in range(count)
+        ]
+        arrive(fetch(copies))
+        pos = place_of()
         odd_x = pos[0] % 2 == 1
         odd_y = pos[1] % 2 == 1
         odd_z = pos[2] % 2
@@ -168,7 +243,7 @@
             packed = [None] * len(outs)
             total = (ex + 2 * WIDE) * (nt + 1)
             for xi in range(ex + 2 * WIDE):
-                plane = x_plane(fields[index], xa.at[index], xb.at[index], odd_x, ex, xi)
+                plane = x_plane(fields.at[index], xa.at[index], xb.at[index], odd_x, ex, xi)
                 for tile in range(nt + 1):
                     if tile < nt:
                         value = plane[tile]
@@ -189,7 +264,7 @@
     return body
 
 
-def halo_body(count, ex, nt, both, sizes, first):
+def halo_body(count, ex, nt, both, sizes):
     ny_rows = SUB * nt
 
     def inside_xy(pos, xi, tile):
@@ -201,11 +276,17 @@
         y = pos[1] * ny_rows + jnp.where(row < WIDE, ny_rows + row, row - SUB)
         return ok, (y >= 0) & (y < sizes[1] * ny_rows)
 
-    def body(pos, *refs):
-        fields, refs = refs[:count], refs[count:]
-        xa, xb, ya, yb = refs[:4]
-        zs = refs[4 : 6 if both else 5]
-        outs = refs[6 if both else 5 :]
+    def body(*refs):
+        raw, (xa, xb, ya, yb) = refs[:count], refs[count : count + 4]
+        rest = refs[count + 4 : -2]
+        zs, outs = (rest[:2], rest[2:]) if both else (rest[:1], rest[1:])
+        fields, sems = refs[-2:]
+        copies = [
+            pltpu.make_async_copy(raw[index], fields.at[index], sems.at[index])
+            for index in range(count)
+        ]
+        arrive(fetch(copies))
+        pos = place_of()
         odd_x = pos[0] % 2 == 1
         odd_y = pos[1] % 2 == 1
         odd_z = pos[2] % 2
@@ -217,7 +298,7 @@
         unit = 0
         for xi in range(ex + 2 * WIDE):
             planes = [
-                x_plane(fields[index], xa.at[index], xb.at[index], odd_x, ex, xi)
+                x_plane(fields.at[index], xa.at[index], xb.at[index], odd_x, ex, xi)
                 for index in range(count)
             ]
             for tile in range(nt + 1):
@@ -251,15 +332,12 @@
                         outs[0][where_main] = jnp.where(good, main, 0.0)
                         outs[0][where_halo] = jnp.where(good & z_mask, halo, 0.0)
                     elif index == 1:
-                        diag = 6.0 + main
-                        outs[1][where_main] = diag
-                        outs[2][where_main] = jnp.where(good, OMEGA / diag, 0.0)
+                        outs[1][where_main] = jnp.where(good, OMEGA / (6.0 + main), 0.0)
                         diag = 6.0 + jnp.where(z_mask, halo, 0.0)
-                        outs[1][where_halo] = diag
-                        outs[2][where_halo] = jnp.where(good & z_mask, OMEGA / diag, 0.0)
+                        outs[1][where_halo] = jnp.where(good & z_mask, OMEGA / diag, 0.0)
                     else:
-                        outs[3][where_main] = main
-                        outs[3][where_halo] = jnp.where(z_mask, halo, 0.0)
+                        outs[2][where_main] = main
+                        outs[2][where_halo] = jnp.where(z_mask, halo, 0.0)
                 unit += 1
 
     return body
@@ -295,7 +373,7 @@
     count = jnp.int32(0)
     for home in range(group):
         for slot in range(slots):
-            hit = table[home, 4 * slot] == rank
+            hit = table[home, COLS * slot] == rank
 
             @pl.when(hit)
             def _():
@@ -324,48 +402,83 @@
     lax.fori_loop(0, slots, box, 0)
 
 
+def prepare_body(slots):
+    def body(source, shift, start, kept, rate, state, *scratch):
+        ins, outs, sems = scratch[:3], scratch[3:6], scratch[6]
+        arrive(
+            fetch(
+                [
+                    pltpu.make_async_copy(raw, local, sems.at[index])
+                    for index, (raw, local) in enumerate(zip((source, shift, start), ins))
+                ]
+            )
+        )
+
+        def load(index, carry):
+            for x in range(SIDE):
+                at = pl.ds(SIDE * x + index, SUB, stride=slots)
+                outs[0][index, x] = ins[0][at, :]
+                outs[1][index, x] = OMEGA / (6.0 + ins[1][at, :])
+                outs[2][index, x] = ins[2][at, :]
+            return carry
+
+        lax.fori_loop(0, slots, load, 0)
+        arrive(
+            fetch(
+                [
+                    pltpu.make_async_copy(local, goal, sems.at[3 + index])
+                    for index, (local, goal) in enumerate(zip(outs, (kept, rate, state)))
+                ]
+            )
+        )
+
+    return body
+
+
 def fine_body(dims, first):
-    group, slots, nby, nbz, size_z = dims
-
-    def body(pos, *refs):
+    group, slots, _, _, size_z = dims
+
+    def body(*refs):
         if first:
-            got, source, shift, start = refs[:4]
-            ret, state, ghosts, squares, table = refs[4:9]
-            (packed, other, diag, rate, kept, homes, copied, sems) = refs[9:]
+            got, *stored = refs[:4]
+            ret, state_out, ghosts_out, squares, table = refs[4:9]
+            packed, other, state, ghosts, kept, rate, homes, moved, copied, counts, sems = refs[9:]
+            old = (kept, rate, other)
         else:
-            table, got, source, shift, old_state, old_ghosts = refs[:6]
-            ret, state, ghosts, squares = refs[6:10]
-            (packed, other, diag, rate, kept, homes) = refs[10:]
-        rank = pos[1] * size_z + pos[2]
+            table, got, *stored = refs[:6]
+            ret, state_out, ghosts_out, squares = refs[6:10]
+            packed, other, state, ghosts, kept, rate, homes, moved, old_ghosts = refs[10:]
+            old = (kept, rate, other, old_ghosts)
+        loads = [
+            pltpu.make_async_copy(source, goal, moved.at[index])
+            for index, (source, goal) in enumerate(zip(stored, old))
+        ]
+        rank = lax.axis_index("gy") * size_z + lax.axis_index("gz")
         if first:
             for home in range(group):
                 pltpu.make_async_copy(got.at[home, 4, 0], copied.at[home], sems.at[home]).start()
+        fetch(loads)
         packed[...] = jnp.zeros(packed.shape, F32)
-
-        def load(index, carry):
-            for x in range(SIDE):
-                at = pl.ds(SIDE * x + index, SUB, stride=slots)
-                six = 6.0 + shift[at, :]
-                diag[index, x] = six
-                rate[index, x] = OMEGA / six
-                kept[index, x] = source[at, :]
-                if first:
-                    other[index, 1 + x] = start[at, :]
-            return carry
-
-        lax.fori_loop(0, slots, load, 0)
         if first:
             for home in range(group):
                 pltpu.make_async_copy(got.at[home, 4, 0], copied.at[home], sems.at[home]).wait()
+            for owner in range(group):
+                counts[owner] = jnp.int32(0)
             for home in range(group):
-                for index in range(4 * slots):
-                    table[home, index] = copied[home, index].astype(jnp.int32)
+                for slot in range(slots):
+                    for index in range(4):
+                        value = copied[home, 4 * slot + index].astype(jnp.int32)
+                        table[home, COLS * slot + index] = value
+                    owner = jnp.minimum(table[home, COLS * slot], group)
+                    place = counts[owner]
+                    table[home, COLS * slot + 4] = place
+                    counts[owner] = place + 1
 
         def found(count, home, slot):
             packed[count] = got[home, 0:4]
             homes[count, 0] = jnp.int32(home)
-            homes[count, 1] = table[home, 4 * slot + 2]
-            homes[count, 2] = table[home, 4 * slot + 3]
+            homes[count, 1] = table[home, COLS * slot + 2]
+            homes[count, 2] = table[home, COLS * slot + 3]
 
         for slot in range(slots):
             homes[slot, 0] = jnp.int32(0)
@@ -373,42 +486,48 @@
             homes[slot, 2] = jnp.int32(0)
         live = assign(rank, table, group, slots, found)
         unpack(packed, ghosts, slots)
+        saves = [pltpu.make_async_copy(ghosts, ghosts_out, moved.at[4])]
+        fetch(saves)
+        arrive(loads)
         masks = fine_masks()
         lanes, rows = lane_id(), sub_id()
 
         def begin(index, carry):
-            if not first:
-                for x in range(SIDE):
-                    change = ghosts[index, x // 2] - old_ghosts[index, x // 2]
-                    other[index, 1 + x] = old_state[index, 1 + x] + change
-            for buffer in (other, state):
-                buffer[index, 0] = ghosts[index, 0]
-                buffer[index, SIDE + 1] = ghosts[index, FOOT - 1]
+            for x in range(SIDE):
+                change = ghosts[index, x // 2] - old_ghosts[index, x // 2]
+                other[index, x] = other[index, x] + change
             return carry
 
-        lax.fori_loop(0, slots, begin, 0)
+        if not first:
+            lax.fori_loop(0, slots, begin, 0)
 
         def residual(buffer, index, x):
-            value = buffer[index, 1 + x]
-            near = around(value, ghosts[index, x // 2], masks)
-            near = near + buffer[index, x] + buffer[index, 2 + x]
-            return value, kept[index, x] - diag[index, x] * value + near
-
-        buffers = [other, state]
+            value = buffer[index, x]
+            ghost = ghosts[index, x // 2]
+            near = around(value, ghost, masks)
+            near = near + (buffer[index, x - 1] if x > 0 else ghost)
+            near = near + (buffer[index, x + 1] if x < SIDE - 1 else ghost)
+            return value, kept[index, x] + near
+
+        buffers = [other, state, other, state]
         for sweep in range(FSWEEPS):
-            here, there = buffers[sweep % 2], buffers[1 - sweep % 2]
+            here, there = buffers[sweep], buffers[sweep + 1]
 
             def step(index, carry):
                 for x in range(SIDE):
                     value, rest = residual(here, index, x)
-                    there[index, 1 + x] = value + rate[index, x] * rest
+                    there[index, x] = (1.0 - OMEGA) * value + rate[index, x] * rest
                 return carry
 
             lax.fori_loop(0, slots, step, 0)
-        final = buffers[FSWEEPS % 2]
-        assert final is state
-
-        ret_rows = [[None] * slots for _ in range(group)]
+        final = state
+        saves.append(pltpu.make_async_copy(state, state_out, moved.at[5]))
+        fetch(saves[1:])
+
+        def remainder(index, x):
+            value, rest = residual(final, index, x)
+            return rest - (OMEGA / rate[index, x]) * value
+
 
         def finish(index, total):
             zone_y = jnp.where(homes[index, 1] == 0, 0, SUB - 2)
@@ -424,9 +543,9 @@
             z_slab = jnp.zeros((SUB, LANES), F32)
             whole = None
             for xp in range(FOOT):
-                value, left = residual(final, index, 2 * xp)
+                left = remainder(index, 2 * xp)
                 mine = mine + left * left
-                value, right = residual(final, index, 2 * xp + 1)
+                right = remainder(index, 2 * xp + 1)
                 mine = mine + right * right
                 both = left + right
                 both = both + pltpu.roll(both, LANES - 1, 1)
@@ -456,14 +575,21 @@
             def _():
                 ret[homes[index, 0], 0:4] = packed[index]
 
+        arrive(saves)
+
     return body
 
 
 def last_body(dims):
     group, slots, size_z = dims
 
-    def body(pos, table, got, state, ghosts, result, packed, fresh):
-        rank = pos[1] * size_z + pos[2]
+    def body(table, got, old_state, old_ghosts, goal, packed, fresh, state, ghosts, result, sems):
+        loads = [
+            pltpu.make_async_copy(old_ghosts, ghosts, sems.at[0]),
+            pltpu.make_async_copy(old_state, state, sems.at[1]),
+        ]
+        fetch(loads)
+        rank = lax.axis_index("gy") * size_z + lax.axis_index("gz")
         packed[...] = jnp.zeros(packed.shape, F32)
 
         def found(count, home, slot):
@@ -471,15 +597,27 @@
 
         live = assign(rank, table, group, slots, found)
         unpack(packed, fresh, slots)
+        arrive(loads)
 
         def box(index, carry):
             for x in range(SIDE):
-                value = state[index, 1 + x] + (fresh[index, x // 2] - ghosts[index, x // 2])
+                value = state[index, x] + (fresh[index, x // 2] - ghosts[index, x // 2])
                 value = jnp.where(index < live, value, 0.0)
                 result[pl.ds(SIDE * x + index, SUB, stride=slots), :] = value
             return carry
 
         lax.fori_loop(0, slots, box, 0)
+        arrive(fetch([pltpu.make_async_copy(result, goal, sems.at[2])]))
+
+    return body
+
+
+def norm_body(group):
+    def body(got, total):
+        result = got[0, 4]
+        for peer in range(1, group):
+            result = result + got[peer, 4]
+        total[...] = result
 
     return body
 
@@ -488,29 +626,21 @@
     ex, nt, group, slots, size_y, size_z, nby, nbz = dims
     tiles = FOOT // SUB
 
-    def body(pos, table, got, added, side_a, side_b):
+    def body(table, got, added, side_a, side_b):
+        pos = place_of()
         odd = pos[0] % 2 == 1
         rank = pos[1] * size_z + pos[2]
         lanes, rows = lane_id(), sub_id()
         added[...] = jnp.zeros(added.shape, F32)
 
-        def slot_of(home, slot):
-            owner = table[home, 4 * slot]
-            count = jnp.int32(0)
-            for lower in range(group):
-                for index in range(slots):
-                    hit = (table[lower, 4 * index] == owner) & (lower < home)
-                    count = count + hit.astype(jnp.int32)
-            return count
-
         def own(slot, carry):
-            owner = table[rank, 4 * slot]
+            owner = table[rank, COLS * slot]
 
             @pl.when(owner < group)
             def _():
-                base_x = FOOT * table[rank, 4 * slot + 1]
-                base_y = tiles * table[rank, 4 * slot + 2]
-                base_z = FOOT * table[rank, 4 * slot + 3]
+                base_x = FOOT * table[rank, COLS * slot + 1]
+                base_y = tiles * table[rank, COLS * slot + 2]
+                base_z = FOOT * table[rank, COLS * slot + 3]
                 keep = (lanes >= base_z) & (lanes < base_z + FOOT)
                 for quad in range(4):
                     value = got[owner, quad]
@@ -535,9 +665,9 @@
                 home = jnp.where(exists, home_y * size_z + home_z, 0)
 
                 def near(slot, carry):
-                    owner = table[home, 4 * slot]
-                    block_y = table[home, 4 * slot + 2]
-                    block_z = table[home, 4 * slot + 3]
+                    owner = table[home, COLS * slot]
+                    block_y = table[home, COLS * slot + 2]
+                    block_z = table[home, COLS * slot + 3]
                     wanted = exists & (owner < group)
                     if dy != 0:
                         wanted = wanted & (block_y == (nby - 1 if dy < 0 else 0))
@@ -546,8 +676,8 @@
 
                     @pl.when(wanted)
                     def _():
-                        value = got[owner, 4 + slot_of(home, slot)]
-                        base_x = FOOT * table[home, 4 * slot + 1]
+                        value = got[owner, 4 + table[home, COLS * slot + 4]]
+                        base_x = FOOT * table[home, COLS * slot + 1]
                         goal = 0 if dy > 0 else 1
                         if dz == 0:
                             base_z = FOOT * block_z
@@ -614,11 +744,13 @@
     span = ex + 2 * WIDE
     rows_all = SUB * (nt + 1)
 
-    def body(pos, table, wide, diag, rate, source, added, xa, xb, fine_sq, *refs):
+    def body(table, wide, rate, source, added, xa, xb, *refs):
+        pos = place_of()
+        sq_in, refs = refs[: 1 if more else 2], refs[1 if more else 2 :]
         if more:
-            potential, send, side_a, side_b = refs[:4]
+            potential, send, squares, side_a, side_b = refs[:5]
         else:
-            potential, send = refs[:2]
+            potential, send, squares = refs[:3]
         comp, one, two = refs[-3:]
         odd = pos[0] % 2 == 1
         rank = pos[1] * size_z + pos[2]
@@ -633,7 +765,7 @@
                     comp[at] = source[at] + added[x, zone, tile]
             return carry
 
-        lax.fori_loop(0, ex, fill, 0)
+        lax.fori_loop(0, ex, fill, 0, unroll=True)
         low_tail = pick_low(odd, xa[units], xb[units])
         high_tail = pick_high(odd, xa[units], xb[units])
         for index in range(WIDE - 1):
@@ -665,7 +797,7 @@
                     near = jnp.where(at_low, main_up, halo_up) + jnp.where(at_high, main_dn, halo_dn)
                 near = near + pltpu.roll(value, 1, 0) + pltpu.roll(value, rows_all - 1, 0)
                 near = near + here[xi - 1, zone] + here[xi + 1, zone]
-                rest = comp[xi, zone] - diag[xi, zone] * value + near
+                rest = comp[xi, zone] + near
                 result.append((value, rest))
             return result
 
@@ -675,34 +807,43 @@
 
             def step(xi, carry):
                 for zone, (value, rest) in enumerate(update(here, xi)):
-                    there[xi, zone] = value + rate[xi, zone] * rest
+                    there[xi, zone] = (1.0 - OMEGA) * value + rate[xi, zone] * rest
                 return carry
 
-            lax.fori_loop(1 + sweep, span - 1 - sweep, step, 0)
+            lax.fori_loop(1 + sweep, span - 1 - sweep, step, 0, unroll=True)
         here = buffers[CSWEEPS - 1]
 
         def step(x, total):
             value, rest = update(here, WIDE + x)[0]
-            value = value + rate[WIDE + x, 0] * rest
+            weight = rate[WIDE + x, 0]
+            rest = rest - (OMEGA / weight) * value
+            value = value + weight * rest
             for tile in range(nt):
                 rows = slice(SUB * tile, SUB * tile + SUB)
                 potential[x, tile] = value[rows]
                 total = total + rest[rows] * rest[rows]
             return total
 
-        total = lax.fori_loop(0, ex, step, fine_sq[...])
+        total = lax.fori_loop(0, ex, step, sq_in[0][...], unroll=True)
+        if more:
+            squares[...] = total
+        else:
+            first_sum = jnp.sum(sq_in[1][...], axis=0, keepdims=True)
+            second_sum = jnp.sum(total, axis=0, keepdims=True)
+            squares[...] = jnp.where(sub_id() == 0, first_sum, second_sum)
         for target in range(group):
             send[target, 0:4] = jnp.zeros((4, SUB, LANES), F32)
-            send[target, 4] = total
+            if not more:
+                send[target, 4] = squares[...]
         for slot in range(slots):
-            target = table[rank, 4 * slot]
+            target = table[rank, COLS * slot]
 
             @pl.when(target < group)
             def _():
                 def write(quad, packed):
                     send[target, quad] = packed
 
-                block = [table[rank, 4 * slot + 1 + index] for index in range(3)]
+                block = [table[rank, COLS * slot + 1 + index] for index in range(3)]
                 extract(potential, write, *block)
 
         if more:
@@ -714,7 +855,7 @@
     return body
 
 
-def local(
+def work(
     coarse_source,
     coarse_shift,
     coarse_start,
@@ -734,7 +875,7 @@
     both = size_z > 2
     span = ex + 2 * WIDE
     sizes = (size_x, size_y, size_z)
-    pos = jnp.stack([lax.axis_index(axis) for axis in ("gx", "gy", "gz")]).astype(jnp.int32)
+    corner = jnp.transpose(box_corner, (2, 0, 1))
 
     def tiled(field):
         return field.reshape(ex, nt, SUB, LANES)
@@ -749,60 +890,78 @@
     start, shift, source = tiled(coarse_start), tiled(coarse_shift), tiled(coarse_source)
     f_source, f_shift, f_start = rows(fine_source), rows(fine_shift), rows(fine_start)
 
-    def halos(fields, side_a, side_b, outs, label):
+    def halos(fields, side_a, side_b, outs):
         count = len(fields)
         xa, xb = swap("gx", side_a, side_b)
-        ins = [(SMEM, pos)] + [(VMEM, field) for field in fields]
+        place = HBM if count > 1 else VMEM
+        ins = [(place, field) for field in fields]
         ya, yb = call(
             y_send_body(count, ex, nt),
-            label + "_y",
             ins + [(VMEM, xa), (VMEM, xb)],
-            [(VMEM, out(count, span, SUB, LANES))] * 2,
+            [(VMEM, out(count, span // 2, SUB, LANES))] * 2,
+            [
+                pltpu.VMEM((count, 2, ex, SUB, LANES), F32),
+                pltpu.SemaphoreType.DMA((count, 2)),
+            ],
         )
         ya, yb = swap("gy", ya, yb)
         units = -(-span * (nt + 1) // (LANES // WIDE))
         zs = call(
-            z_send_body(count, ex, nt, both),
-            label + "_z",
+            z_send_body(count, ex, nt),
             ins + [(VMEM, value) for value in (xa, xb, ya, yb)],
             [(VMEM, out(count, units, SUB, LANES))] * (2 if both else 1),
+            [
+                pltpu.VMEM((count, ex, nt, SUB, LANES), F32),
+                pltpu.SemaphoreType.DMA((count,)),
+            ],
         )
         if both:
             zs = list(swap("gz", *zs))
         else:
             zs = [swap("gz", zs[0], zs[0])[0]]
         return call(
-            halo_body(count, ex, nt, both, sizes, count > 1),
-            label + "_all",
+            halo_body(count, ex, nt, both, sizes),
             ins + [(VMEM, value) for value in (xa, xb, ya, yb, *zs)],
             [(VMEM, out(span, 2, SUB * (nt + 1), LANES))] * outs,
+            [
+                pltpu.VMEM((count, ex, nt, SUB, LANES), F32),
+                pltpu.SemaphoreType.DMA((count,)),
+            ],
         )
 
-    chunk = out(group, 5, SUB, LANES)
-    send, side_a, side_b = call(
-        send_start_body((ex, nt, group, slots, nbx, nby, nbz)),
-        "send_start",
-        [(SMEM, pos), (SMEM, box_corner), (SMEM, box_owner)]
-        + [(VMEM, value) for value in (start, shift, source)],
-        [(VMEM, chunk)] + [(VMEM, out(3, WIDE, nt, SUB, LANES))] * 2,
+    (send,) = call(
+        send_start_body((group, slots, nbx, nby, nbz)),
+        [(SMEM, corner), (SMEM, box_owner), (HBM, start)],
+        [(VMEM, out(group, 5, SUB, LANES))],
+        [pltpu.VMEM((ex, nt, SUB, LANES), F32), pltpu.SemaphoreType.DMA],
     )
     got = exchange(send)
-    wide, diag, rate, source_wide = halos([start, shift, source], side_a, side_b, 4, "fixed")
+    fields = [start, shift, source]
+    side_a, side_b = call(
+        sides_body(ex),
+        [(HBM, field) for field in fields],
+        [(VMEM, out(3, WIDE, nt, SUB, LANES))] * 2,
+        [pltpu.SemaphoreType.DMA((3, 2))],
+    )
+    wide, rate, source_wide = halos(fields, side_a, side_b, 3)
 
     box_shape = (slots, SIDE, SUB, LANES)
-    state_shape = (slots, SIDE + 2, SUB, LANES)
-    box_scratch = [
-        pltpu.VMEM((slots, 4, SUB, LANES), F32),
-        pltpu.VMEM(state_shape, F32),
-        pltpu.VMEM(box_shape, F32),
-        pltpu.VMEM(box_shape, F32),
-        pltpu.VMEM(box_shape, F32),
-        pltpu.SMEM((slots, 3), jnp.int32),
-    ]
+    flat = pltpu.VMEM((slots * fine // LANES, LANES), F32)
+    whole = pltpu.VMEM(box_shape, F32)
+    ghost = pltpu.VMEM((slots, FOOT, SUB, LANES), F32)
+    packs = pltpu.VMEM((slots, 4, SUB, LANES), F32)
+    kept, f_rate, state = call(
+        prepare_body(slots),
+        [(HBM, value) for value in (f_source, f_shift, f_start)],
+        [(HBM, out(*box_shape))] * 3,
+        [flat] * 3 + [whole] * 3 + [pltpu.SemaphoreType.DMA((6,))],
+    )
+    box_scratch = [packs, whole, whole, ghost, whole, whole]
+    box_scratch += [pltpu.SMEM((slots, 3), jnp.int32), pltpu.SemaphoreType.DMA((6,))]
     box_outs = [
         (VMEM, out(group, 4 + slots, SUB, LANES)),
-        (VMEM, out(*state_shape)),
-        (VMEM, out(slots, FOOT, SUB, LANES)),
+        (HBM, out(*box_shape)),
+        (HBM, out(slots, FOOT, SUB, LANES)),
         (VMEM, out(SUB, LANES)),
     ]
     norms = []
@@ -813,28 +972,28 @@
         if first:
             ret, state, ghosts, squares, table = call(
                 body,
-                "fine_first",
-                [(SMEM, pos)] + [(VMEM, value) for value in (got, f_source, f_shift, f_start)],
-                box_outs + [(SMEM, out(group, 4 * slots, dtype=jnp.int32))],
+                [(VMEM, got)] + [(HBM, value) for value in (kept, f_rate, state)],
+                box_outs + [(SMEM, out(group, COLS * slots, dtype=jnp.int32))],
                 box_scratch
-                + [pltpu.SMEM((group, LANES), F32), pltpu.SemaphoreType.DMA((group,))],
+                + [
+                    pltpu.SMEM((group, LANES), F32),
+                    pltpu.SMEM((group + 1,), jnp.int32),
+                    pltpu.SemaphoreType.DMA((group,)),
+                ],
             )
         else:
-            norms.append(jnp.sum(got[:, 4]))
             ret, state, ghosts, squares = call(
                 body,
-                "fine_next",
-                [(SMEM, pos), (SMEM, table)]
-                + [(VMEM, value) for value in (got, f_source, f_shift, state, ghosts)],
+                [(SMEM, table), (VMEM, got)]
+                + [(HBM, value) for value in (kept, f_rate, state, ghosts)],
                 box_outs,
-                box_scratch,
+                box_scratch + [ghost],
             )
         back = exchange(ret)
         units = (WIDE - 1) * (nt + 1) + 1
         added, side_a, side_b = call(
             place_body((ex, nt, group, slots, size_y, size_z, nby, nbz)),
-            "place",
-            [(SMEM, pos), (SMEM, table), (VMEM, back)],
+            [(SMEM, table), (VMEM, back)],
             [(VMEM, out(ex, 2, nt + 1, SUB, LANES))] + [(VMEM, out(units, SUB, LANES))] * 2,
         )
         xa, xb = swap("gx", side_a, side_b)
@@ -842,36 +1001,37 @@
         wide_shape = (span, 2, SUB * (nt + 1), LANES)
         result = call(
             coarse_body((ex, nt, group, slots, size_z), more),
-            "coarse",
-            [(SMEM, pos), (SMEM, table)]
-            + [(VMEM, v) for v in (wide, diag, rate, source_wide, added, xa, xb, squares)],
-            [(VMEM, out(ex, nt, SUB, LANES)), (VMEM, chunk)]
+            [(SMEM, table)]
+            + [(VMEM, v) for v in (wide, rate, source_wide, added, xa, xb, squares, *norms)],
+            [
+                (VMEM, out(ex, nt, SUB, LANES)),
+                (VMEM, out(group, 4 if more else 5, SUB, LANES)),
+                (VMEM, out(SUB, LANES)),
+            ]
             + [(VMEM, out(1, WIDE, nt, SUB, LANES))] * (2 if more else 0),
             [pltpu.VMEM(wide_shape, F32)] * 3,
         )
         potential, send = result[:2]
+        norms.append(result[2])
         got = exchange(send)
         if more:
-            (wide,) = halos([potential], result[2], result[3], 1, "next")
+            (wide,) = halos([potential], result[3], result[4], 1)
+    (total,) = call(norm_body(group), [(VMEM, got)], [(VMEM, out(SUB, LANES))])
     (values,) = call(
         last_body((group, slots, size_z)),
-        "last",
-        [(SMEM, pos), (SMEM, table)] + [(VMEM, value) for value in (got, state, ghosts)],
-        [(VMEM, out(slots * fine // LANES, LANES))],
-        [
-            pltpu.VMEM((slots, 4, SUB, LANES), F32),
-            pltpu.VMEM((slots, FOOT, SUB, LANES), F32),
-        ],
+        [(SMEM, table), (VMEM, got), (HBM, state), (HBM, ghosts)],
+        [(HBM, out(slots * fine // LANES, LANES))],
+        [packs, ghost, whole, ghost, flat, pltpu.SemaphoreType.DMA((3,))],
     )
-    norms.append(jnp.sum(got[:, 4]))
-    total = jnp.broadcast_to(jnp.stack(norms)[None, :], (SUB, CYCLES))
+    cells = float(ex * ey * ez * size_x * size_y * size_z)
     bit = 1
     while bit < size_x:
-        total = total + lax.ppermute(total, "gx", [(i, i ^ bit) for i in range(size_x)])
+        pairs = [(i, i ^ bit) for i in range(size_x)]
+        total = total + lax.ppermute(total, "gx", pairs)
         bit *= 2
-    cells = float(ex * ey * ez * size_x * size_y * size_z)
+    total = jnp.sum(total[:CYCLES], axis=1)
     values = values.reshape(fine // LANES, slots, LANES).transpose(1, 0, 2).reshape(slots, fine)
-    return potential.reshape(ex, ey, ez), values, jnp.sqrt(total[0] / cells)
+    return potential.reshape(ex, ey, ez), values, jnp.sqrt(total / cells)
 
 
 def solution(mesh):
@@ -886,4 +1046,4 @@
         P(("gx", "gy", "gz"), None),
     )
     out_specs = (P("gx", "gy", "gz"), P(("gx", "gy", "gz"), None), P())
-    return jax.shard_map(local, mesh=mesh, in_specs=in_specs, out_specs=out_specs, check_vma=False)
+    return jax.shard_map(work, mesh=mesh, in_specs=in_specs, out_specs=out_specs, check_vma=False)

time: 137 us -> 110 us (0.80)
  local copies, waits for them, and re-layouts: 10.5 us -> 0.67 us
  Pallas kernels: 48.4 us -> 41.7 us
  waiting for transfers between devices: 24.1 us -> 17.8 us
  other arithmetic: 3.3 us -> 0.65 us
  blocking collectives: 17 us -> 15.3 us
    unnamed x55 -> x4, local copies, waits for them, and re-layouts: 10.5 us -> 0.67 us
    pallas_call x14 -> x17, Pallas kernels: 48.4 us -> 41.7 us  [call(): pl.pallas_call(body, in_specs=[spec for spec, _ in ins], out_specs=[spec...]
    ppermute x6, waiting for transfers between devices: 7.06 us -> 2.78 us  [swap(): got_b = lax.ppermute(second, axis, pairs_b) if count > 2 else got_a]
    all_to_all x3, starting transfers between devices: 10.8 us -> 12.8 us  [exchange(): lax.all_to_all(value, GROUP_AXES, split_axis=0, concat_axis=0, tiled=True)]
    all_to_all x2, blocking collectives: 17 us -> 15.3 us  [exchange(): lax.all_to_all(value, GROUP_AXES, split_axis=0, concat_axis=0, tiled=True)]
    all_to_all x3, waiting for transfers between devices: 4.67 us -> 3.13 us  [exchange(): lax.all_to_all(value, GROUP_AXES, split_axis=0, concat_axis=0, tiled=True)]
    another operation x2 -> x0, other arithmetic: 1.48 us -> none  [the longest x1 1.41 us: local(): total = jnp.broadcast_to(jnp.stack(norms)[None, :], (SUB, CYCLES))]
  transfers between devices with their start and end apart: 19 -> 19, of which waited for: 8 -> 7; matrix products, arithmetic and copies ran while one was open for 1% -> 0% of each run, Pallas kernels for 15% -> 22%
where the time goes in v3:
time: 110 us; the launch traced here: 109 us
  Pallas kernels  41.7 us (38%)
  starting transfers between devices  32.5 us (30%)
  waiting for transfers between devices  17.8 us (16%)
  blocking collectives  15.3 us (14%)
    pallas_call x17, Pallas kernels, call(): pl.pallas_call(body, in_specs=[spec for spec, _ in ins], out_specs=[spec...  41.7 us
    all_to_all x2, blocking collectives, exchange(): lax.all_to_all(value, GROUP_AXES, split_axis=0, concat_axis=0, tiled=True)  15.3 us
    all_to_all x3, starting transfers between devices, exchange(): lax.all_to_all(value, GROUP_AXES, split_axis=0, concat_axis=0, tiled=True)  12.8 us
    ppermute x6, starting transfers between devices, swap(): got_b = lax.ppermute(second, axis, pairs_b) if count > 2 else got_a  10 us
    ppermute x8, starting transfers between devices, swap(): got_a = lax.ppermute(first, axis, pairs_a)  9.19 us
    ppermute x8, waiting for transfers between devices, swap(): got_a = lax.ppermute(first, axis, pairs_a)  6.83 us
    ppermute x2, waiting for transfers between devices, work(): total = total + lax.ppermute(total, 'gx', pairs)  5.02 us
    all_to_all x3, waiting for transfers between devices, exchange(): lax.all_to_all(value, GROUP_AXES, split_axis=0, concat_axis=0, tiled=True)  3.13 us
  transfers between devices with their start and end apart: 19, of which 7 were waited for; matrix products, arithmetic and copies ran while one was open for 0% of the time, Pallas kernels for 22%

profile of v3, /device:TPU:0, one launch (start us, length us, event | category | flops | bytes accessed | tf_op | source)
XLA Modules:
  0.0 109.4 jit_solution(12901308894602636440)
XLA Ops:
  0.6 0.0 copy-start
  0.6 0.0 copy-start.1
  0.7 0.7 copy-done
  1.3 0.0 copy-done.1
  1.3 2.6 %shard_map.103 = f32[8,5,8,128]{3,2,1,0:T(8,128)} custom-call(s32[3,1,4]{2,1,0:T(1,128)S(1)} %bitcast.25, s32[1,4]{1,0:T(1,128)S(1)} %copy-done.1, f32[16,4,8,128]{3,2,1,0:T(8,128)} %bitcast.26), custom_call_target="tpu_custom_call" | custom-call | tf_op jit(solution)/shard_map/pallas_call | solution.py:38
  3.9 5.0 %all-to-all-start = ((f32[8,5,8,128]{3,2,1,0:T(8,128)}), f32[8,5,8,128]{3,2,1,0:T(8,128)S(1)}, u32[]{:S(2)}, u32[]{:S(2)}) async-start(f32[8,5,8,128]{3,2,1,0:T(8,128)} %shard_map.103), calls=%async_computation | async-start | bytes 327680 | tf_op jit(solution)/shard_map/all_to_all | solution.py:888
  8.9 1.0 shard_map.106
  10.0 1.8 %collective-permute-start = (f32[3,4,4,8,128]{4,3,2,1,0:T(8,128)S(1)}, f32[3,4,4,8,128]{4,3,2,1,0:T(8,128)S(1)}, u32[]{:S(2)}, u32[]{:S(2)}) collective-permute-start(f32[3,4,4,8,128]{4,3,2,1,0:T(8,128)S(1)} %get-tuple-element.41), channel_id=1, source_target_pairs={{0,8},{8,0},{16,24},{24,16},{1,9},{9,1},{17,25},{25,17},{2,10},{10... | collective-permute-start | bytes 589832 | tf_op jit(solution)/shard_map/ppermute | solution.py:84
  11.8 2.3 %collective-permute-start.1 = (f32[3,4,4,8,128]{4,3,2,1,0:T(8,128)S(1)}, f32[3,4,4,8,128]{4,3,2,1,0:T(8,128)S(1)}, u32[]{:S(2)}, u32[]{:S(2)}) collective-permute-start(f32[3,4,4,8,128]{4,3,2,1,0:T(8,128)S(1)} %get-tuple-element.42), channel_id=1, source_target_pairs={{0,24},{8,16},{16,8},{24,0},{1,25},{9,17},{17,9},{25,1},{2,26},{10... | collective-permute-start | bytes 589832 | tf_op jit(solution)/shard_map/ppermute | solution.py:85
  14.1 2.8 %shard_map.104 = (f32[4,32,8,128]{3,2,1,0:T(8,128)}, f32[4,32,8,128]{3,2,1,0:T(8,128)}, f32[4,32,8,128]{3,2,1,0:T(8,128)}) custom-call(f32[1024,128]{1,0:T(8,128)} %bitcast.39, f32[1024,128]{1,0:T(8,128)} %bitcast.40, f32[1024,128]{1,0:T(8,128)} %bitcast.41), custom_call_target="tpu_custom_call" | custom-call | tf_op jit(solution)/shard_map/pallas_call | solution.py:38
  16.9 0.0 all-to-all-done.refs_0_
  16.9 8.2 %shard_map.105 = (f32[8,8,8,128]{3,2,1,0:T(8,128)}, f32[4,32,8,128]{3,2,1,0:T(8,128)}, f32[4,16,8,128]{3,2,1,0:T(8,128)}, f32[8,128]{1,0:T(8,128)S(1)}, s32[8,32]{1,0:T(8,128)S(1)}) custom-call(f32[8,5,8,128]{3,2,1,0:T(8,128)S(1)} %all-to-all-done.refs_0_, f32[4,32,8,128]{3,2,1,0:T(8,128)} %get-tuple-element.37.refs_1_.refs_2_, ...), custom_call_target="tpu_custom_call" | custom-call | tf_op jit(solution)/shard_map/pallas_call | solution.py:38
  25.2 4.2 %all-to-all-start.1 = ((f32[8,8,8,128]{3,2,1,0:T(8,128)}), f32[8,8,8,128]{3,2,1,0:T(8,128)S(1)}, u32[]{:S(2)}, u32[]{:S(2)}) async-start(f32[8,8,8,128]{3,2,1,0:T(8,128)} %get-tuple-element.48), calls=%async_computation.1 | async-start | bytes 524288 | tf_op jit(solution)/shard_map/all_to_all | solution.py:888
  29.4 0.0 collective-permute-done.refs_3_
  29.4 0.0 collective-permute-done.1.refs_4_
  29.4 1.1 shard_map.107
  30.5 0.6 collective-permute-start.2
  31.0 1.6 %collective-permute-start.3 = (f32[3,12,8,128]{3,2,1,0:T(8,128)S(1)}, f32[3,12,8,128]{3,2,1,0:T(8,128)S(1)}, u32[]{:S(2)}, u32[]{:S(2)}) collective-permute-start(f32[3,12,8,128]{3,2,1,0:T(8,128)S(1)} %get-tuple-element.44), channel_id=1, source_target_pairs={{0,6},{2,4},{4,2},{6,0},{1,7},{3,5},{5,3},{7,1},{8,14},{10,12},{12... | collective-permute-start | bytes 442376 | tf_op jit(solution)/shard_map/ppermute | solution.py:85
  32.7 3.1 %all-to-all-done.1.got = f32[8,8,8,128]{3,2,1,0:T(8,128)S(1)} async-done(((f32[8,8,8,128]{3,2,1,0:T(8,128)}), f32[8,8,8,128]{3,2,1,0:T(8,128)S(1)}, u32[]{:S(2)}, u32[]{:S(2)}) %all-to-all-start.1) | async-done | bytes 262176 | tf_op jit(solution)/shard_map/all_to_all | solution.py:888
  35.8 2.1 %shard_map.110 = (f32[16,2,5,8,128]{4,3,2,1,0:T(8,128)S(1)}, f32[16,8,128]{2,1,0:T(8,128)S(1)}, f32[16,8,128]{2,1,0:T(8,128)S(1)}) custom-call(s32[8,32]{1,0:T(8,128)S(1)} %get-tuple-element.40.table.refs_0_, f32[8,8,8,128]{3,2,1,0:T(8,128)S(1)} %all-to-all-done.1.got), custom_call_target="tpu_custom_call" | custom-call | tf_op jit(solution)/shard_map/pallas_call | solution.py:38
  37.9 0.9 collective-permute-start.5
  38.8 1.3 %collective-permute-start.6 = (f32[16,8,128]{2,1,0:T(8,128)S(1)}, f32[16,8,128]{2,1,0:T(8,128)S(1)}, u32[]{:S(2)}, u32[]{:S(2)}) collective-permute-start(f32[16,8,128]{2,1,0:T(8,128)S(1)} %get-tuple-element.51), channel_id=1, source_target_pairs={{0,24},{8,16},{16,8},{24,0},{1,25},{9,17},{17,9},{25,1},{2,26},{10... | collective-permute-start | bytes 196616 | tf_op jit(solution)/shard_map/ppermute | solution.py:85
  40.0 0.0 collective-permute-done.2.refs_5_
  40.0 0.0 collective-permute-done.3.refs_6_
  40.0 1.6 %shard_map.108 = f32[3,4,8,128]{3,2,1,0:T(8,128)S(1)} custom-call(f32[16,4,8,128]{3,2,1,0:T(8,128)} %bitcast.29, f32[16,4,8,128]{3,2,1,0:T(8,128)} %bitcast.33, f32[16,4,8,128]{3,2,1,0:T(8,128)} %bitcast.37, f32[3,4,4,8,128]{4,3,2,1,0:T(8,128)S(1)} %collective-permute-done.refs_3_, f32[3,4,4,8,128]{4,3,2,1,0:T(8,128)S(1)} %collective-permute-done.1.refs_4_, ...), custom_call_target="tpu_custom_call" | custom-call | tf_op jit(solution)/shard_map/pallas_call | solution.py:38
  41.7 1.3 %collective-permute-start.4 = (f32[3,4,8,128]{3,2,1,0:T(8,128)S(1)}, f32[3,4,8,128]{3,2,1,0:T(8,128)S(1)}, u32[]{:S(2)}, u32[]{:S(2)}) collective-permute-start(f32[3,4,8,128]{3,2,1,0:T(8,128)S(1)} %shard_map.108), channel_id=1, source_target_pairs={{0,1},{1,0},{2,3},{3,2},{4,5},{5,4},{6,7},{7,6},{8,9},{9,8},{10,11... | collective-permute-start | bytes 147464 | tf_op jit(solution)/shard_map/ppermute | solution.py:84
  42.9 2.9 %collective-permute-done.4.refs_7_ = f32[3,4,8,128]{3,2,1,0:T(8,128)S(1)} collective-permute-done((f32[3,4,8,128]{3,2,1,0:T(8,128)S(1)}, f32[3,4,8,128]{3,2,1,0:T(8,128)S(1)}, u32[]{:S(2)}, u32[]{:S(2)}) %collective-permute-start.4) | collective-permute-done | bytes 49184 | tf_op jit(solution)/shard_map/ppermute | solution.py:84
  45.8 1.6 %shard_map.109 = (f32[24,2,40,128]{3,2,1,0:T(8,128)S(1)}, f32[24,2,40,128]{3,2,1,0:T(8,128)S(1)}, f32[24,2,40,128]{3,2,1,0:T(8,128)S(1)}) custom-call(f32[16,4,8,128]{3,2,1,0:T(8,128)} %bitcast.30, f32[16,4,8,128]{3,2,1,0:T(8,128)} %bitcast.34, f32[16,4,8,128]{3,2,1,0:T(8,128)} %bitcast.38, f32[3,4,4,8,128]{4,3,2,1,0:T(8,128)S(1)} %collective-permute-done.refs_3_, ...), custom_call_target="tpu_custom_call" | custom-call | tf_op jit(solution)/shard_map/pallas_call | solution.py:38
  47.5 0.0 collective-permute-done.5.xa
  47.5 0.0 collective-permute-done.6.xb
  47.5 3.0 %shard_map.111 = (f32[16,4,8,128]{3,2,1,0:T(8,128)S(1)}, f32[8,4,8,128]{3,2,1,0:T(8,128)S(1)}, f32[8,128]{1,0:T(8,128)S(1)}, f32[1,4,4,8,128]{4,3,2,1,0:T(8,128)S(1)}, f32[1,4,4,8,128]{4,3,2,1,0:T(8,128)S(1)}) custom-call(s32[8,32]{1,0:T(8,128)S(1)} %get-tuple-element.40.table.refs_0_, f32[24,2,40,128]{3,2,1,0:T(8,128)S(1)} %get-tuple-element.45.wide, ...), custom_call_target="tpu_custom_call" | custom-call | tf_op jit(solution)/shard_map/pallas_call | solution.py:38
  50.5 7.5 %all_to_all.25.refs_1_ = f32[8,4,8,128]{3,2,1,0:T(8,128)S(1)} all-to-all(f32[8,4,8,128]{3,2,1,0:T(8,128)S(1)} %get-tuple-element.58), channel_id=1, replica_groups=mesh['gx'=4,'gy'=4,'gz'=2] {'gy','gz'}, dimensions={0} | all-to-all | bytes 262144 | tf_op jit(solution)/shard_map/all_to_all | solution.py:888
  58.0 8.4 %shard_map.115 = (f32[8,8,8,128]{3,2,1,0:T(8,128)}, f32[4,32,8,128]{3,2,1,0:T(8,128)}, f32[4,16,8,128]{3,2,1,0:T(8,128)}, f32[8,128]{1,0:T(8,128)S(1)}) custom-call(s32[8,32]{1,0:T(8,128)S(1)} %get-tuple-element.40.table.refs_0_, f32[8,4,8,128]{3,2,1,0:T(8,128)S(1)} %all_to_all.25.refs_1_, f32[4,32,8,128]{3,2,1,0:T(8,128)} %get-tuple-element.37.refs_1_.refs_2_, ...), custom_call_target="tpu_custom_call" | custom-call | tf_op jit(solution)/shard_map/pallas_call | solution.py:38
  66.4 3.6 %all-to-all-start.3 = ((f32[8,8,8,128]{3,2,1,0:T(8,128)}), f32[8,8,8,128]{3,2,1,0:T(8,128)S(1)}, u32[]{:S(2)}, u32[]{:S(2)}) async-start(f32[8,8,8,128]{3,2,1,0:T(8,128)} %get-tuple-element.61), calls=%async_computation.3 | async-start | bytes 524288 | tf_op jit(solution)/shard_map/all_to_all | solution.py:888
  70.0 1.0 collective-permute-start.7
  71.1 1.9 %collective-permute-start.8 = (f32[1,4,4,8,128]{4,3,2,1,0:T(8,128)S(1)}, f32[1,4,4,8,128]{4,3,2,1,0:T(8,128)S(1)}, u32[]{:S(2)}, u32[]{:S(2)}) collective-permute-start(f32[1,4,4,8,128]{4,3,2,1,0:T(8,128)S(1)} %get-tuple-element.55), channel_id=1, source_target_pairs={{0,24},{8,16},{16,8},{24,0},{1,25},{9,17},{17,9},{25,1},{2,26},{10... | collective-permute-start | bytes 196616 | tf_op jit(solution)/shard_map/ppermute | solution.py:85
  73.0 1.4 %collective-permute-done.7.refs_1_ = f32[1,4,4,8,128]{4,3,2,1,0:T(8,128)S(1)} collective-permute-done((f32[1,4,4,8,128]{4,3,2,1,0:T(8,128)S(1)}, f32[1,4,4,8,128]{4,3,2,1,0:T(8,128)S(1)}, u32[]{:S(2)}, u32[]{:S(2)}) %collective-permute-start.7) | collective-permute-done | bytes 65568 | tf_op jit(solution)/shard_map/ppermute | solution.py:84
  74.4 2.8 %collective-permute-done.8.refs_2_ = f32[1,4,4,8,128]{4,3,2,1,0:T(8,128)S(1)} collective-permute-done((f32[1,4,4,8,128]{4,3,2,1,0:T(8,128)S(1)}, f32[1,4,4,8,128]{4,3,2,1,0:T(8,128)S(1)}, u32[]{:S(2)}, u32[]{:S(2)}) %collective-permute-start.8) | collective-permute-done | bytes 65568 | tf_op jit(solution)/shard_map/ppermute | solution.py:85
  77.1 0.1 shard_map.112
  77.2 0.2 collective-permute-start.10
  77.4 1.7 %collective-permute-start.9 = (f32[1,12,8,128]{3,2,1,0:T(8,128)S(1)}, f32[1,12,8,128]{3,2,1,0:T(8,128)S(1)}, u32[]{:S(2)}, u32[]{:S(2)}) collective-permute-start(f32[1,12,8,128]{3,2,1,0:T(8,128)S(1)} %get-tuple-element.56), channel_id=1, source_target_pairs={{0,2},{2,0},{4,6},{6,4},{1,3},{3,1},{5,7},{7,5},{8,10},{10,8},{12,... | collective-permute-start | bytes 147464 | tf_op jit(solution)/shard_map/ppermute | solution.py:84
  79.1 0.0 all-to-all-done.3.got
  79.1 2.1 %shard_map.116 = (f32[16,2,5,8,128]{4,3,2,1,0:T(8,128)S(1)}, f32[16,8,128]{2,1,0:T(8,128)S(1)}, f32[16,8,128]{2,1,0:T(8,128)S(1)}) custom-call(s32[8,32]{1,0:T(8,128)S(1)} %get-tuple-element.40.table.refs_0_, f32[8,8,8,128]{3,2,1,0:T(8,128)S(1)} %all-to-all-done.3.got), custom_call_target="tpu_custom_call" | custom-call | tf_op jit(solution)/shard_map/pallas_call | solution.py:38
  81.2 0.6 collective-permute-start.12
  81.8 2.8 %collective-permute-start.13 = (f32[16,8,128]{2,1,0:T(8,128)S(1)}, f32[16,8,128]{2,1,0:T(8,128)S(1)}, u32[]{:S(2)}, u32[]{:S(2)}) collective-permute-start(f32[16,8,128]{2,1,0:T(8,128)S(1)} %get-tuple-element.64), channel_id=1, source_target_pairs={{0,24},{8,16},{16,8},{24,0},{1,25},{9,17},{17,9},{25,1},{2,26},{10... | collective-permute-start | bytes 196616 | tf_op jit(solution)/shard_map/ppermute | solution.py:85
  84.6 0.0 collective-permute-done.10.refs_4_
  84.6 0.0 collective-permute-done.9.refs_3_
  84.6 0.3 shard_map.113
  84.9 1.3 %collective-permute-start.11 = (f32[1,4,8,128]{3,2,1,0:T(8,128)S(1)}, f32[1,4,8,128]{3,2,1,0:T(8,128)S(1)}, u32[]{:S(2)}, u32[]{:S(2)}) collective-permute-start(f32[1,4,8,128]{3,2,1,0:T(8,128)S(1)} %shard_map.113), channel_id=1, source_target_pairs={{0,1},{1,0},{2,3},{3,2},{4,5},{5,4},{6,7},{7,6},{8,9},{9,8},{10,11... | collective-permute-start | bytes 49160 | tf_op jit(solution)/shard_map/ppermute | solution.py:84
  86.1 2.6 %collective-permute-done.11.refs_5_ = f32[1,4,8,128]{3,2,1,0:T(8,128)S(1)} collective-permute-done((f32[1,4,8,128]{3,2,1,0:T(8,128)S(1)}, f32[1,4,8,128]{3,2,1,0:T(8,128)S(1)}, u32[]{:S(2)}, u32[]{:S(2)}) %collective-permute-start.11) | collective-permute-done | bytes 16416 | tf_op jit(solution)/shard_map/ppermute | solution.py:84
  88.7 0.3 shard_map.114.wide
  89.0 0.0 collective-permute-done.12.xa
  89.0 0.0 collective-permute-done.13.xb
  89.0 3.8 %shard_map.117 = (f32[16,4,8,128]{3,2,1,0:T(8,128)}, f32[8,5,8,128]{3,2,1,0:T(8,128)S(1)}, f32[8,128]{1,0:T(8,128)}) custom-call(s32[8,32]{1,0:T(8,128)S(1)} %get-tuple-element.40.table.refs_0_, f32[24,2,40,128]{3,2,1,0:T(8,128)S(1)} %shard_map.114.wide, f32[24,2,40,128]{3,2,1,0:T(8,128)S(1)} %get-tuple-element.46.rate, ...), custom_call_target="tpu_custom_call" | custom-call | tf_op jit(solution)/shard_map/pallas_call | solution.py:38
  92.8 7.8 %all_to_all.26.got = f32[8,5,8,128]{3,2,1,0:T(8,128)S(1)} all-to-all(f32[8,5,8,128]{3,2,1,0:T(8,128)S(1)} %get-tuple-element.68), channel_id=1, replica_groups=mesh['gx'=4,'gy'=4,'gz'=2] {'gy','gz'}, dimensions={0} | all-to-all | bytes 327680 | tf_op jit(solution)/shard_map/all_to_all | solution.py:888
  100.6 0.2 collective-permute-start.14
  100.8 3.4 %collective-permute-done.14 = f32[8,128]{1,0:T(8,128)S(1)} collective-permute-done((f32[8,128]{1,0:T(8,128)S(1)}, f32[8,128]{1,0:T(8,128)S(1)}, u32[]{:S(2)}, u32[]{:S(2)}) %collective-permute-start.14) | collective-permute-done | bytes 4128 | tf_op jit(solution)/shard_map/ppermute | solution.py:1030
  104.2 0.3 collective-permute-start.15
  104.5 2.6 %shard_map.118 = f32[1024,128]{1,0:T(8,128)} custom-call(s32[8,32]{1,0:T(8,128)S(1)} %get-tuple-element.40.table.refs_0_, f32[8,5,8,128]{3,2,1,0:T(8,128)S(1)} %all_to_all.26.got, f32[4,32,8,128]{3,2,1,0:T(8,128)} %get-tuple-element.69.old_state, f32[4,16,8,128]{3,2,1,0:T(8,128)} %get-tuple-element.70.old_ghosts), custom_call_target="tpu_custom_call" | custom-call | tf_op jit(solution)/shard_map/pallas_call | solution.py:38
  107.2 1.6 %collective-permute-done.15 = f32[8,128]{1,0:T(8,128)S(1)} collective-permute-done((f32[8,128]{1,0:T(8,128)S(1)}, f32[8,128]{1,0:T(8,128)S(1)}, u32[]{:S(2)}, u32[]{:S(2)}) %collective-permute-start.15) | collective-permute-done | bytes 4128 | tf_op jit(solution)/shard_map/ppermute | solution.py:1030
  108.8 0.1 slice_reduce_fusion
  108.9 0.5 multiply_sqrt_fusion
  (3 shorter events, 0.0 us)
Async XLA Ops:
  0.6 0.7 copy-start
  0.6 0.7 copy-start.1
  3.9 13.0 %all-to-all-start = ((f32[8,5,8,128]{3,2,1,0:T(8,128)}), f32[8,5,8,128]{3,2,1,0:T(8,128)S(1)}, u32[]{:S(2)}, u32[]{:S(2)}) async-start(f32[8,5,8,128]{3,2,1,0:T(8,128)} %shard_map.103), calls=%async_computation | async-start | bytes 327680 | tf_op jit(solution)/shard_map/all_to_all | solution.py:888
  10.0 19.4 %collective-permute-start = (f32[3,4,4,8,128]{4,3,2,1,0:T(8,128)S(1)}, f32[3,4,4,8,128]{4,3,2,1,0:T(8,128)S(1)}, u32[]{:S(2)}, u32[]{:S(2)}) collective-permute-start(f32[3,4,4,8,128]{4,3,2,1,0:T(8,128)S(1)} %get-tuple-element.41), channel_id=1, source_target_pairs={{0,8},{8,0},{16,24},{24,16},{1,9},{9,1},{17,25},{25,17},{2,10},{10... | collective-permute-start | bytes 589832 | tf_op jit(solution)/shard_map/ppermute | solution.py:84
  11.8 17.5 %collective-permute-start.1 = (f32[3,4,4,8,128]{4,3,2,1,0:T(8,128)S(1)}, f32[3,4,4,8,128]{4,3,2,1,0:T(8,128)S(1)}, u32[]{:S(2)}, u32[]{:S(2)}) collective-permute-start(f32[3,4,4,8,128]{4,3,2,1,0:T(8,128)S(1)} %get-tuple-element.42), channel_id=1, source_target_pairs={{0,24},{8,16},{16,8},{24,0},{1,25},{9,17},{17,9},{25,1},{2,26},{10... | collective-permute-start | bytes 589832 | tf_op jit(solution)/shard_map/ppermute | solution.py:85
  25.2 10.6 %all-to-all-start.1 = ((f32[8,8,8,128]{3,2,1,0:T(8,128)}), f32[8,8,8,128]{3,2,1,0:T(8,128)S(1)}, u32[]{:S(2)}, u32[]{:S(2)}) async-start(f32[8,8,8,128]{3,2,1,0:T(8,128)} %get-tuple-element.48), calls=%async_computation.1 | async-start | bytes 524288 | tf_op jit(solution)/shard_map/all_to_all | solution.py:888
  30.5 9.6 %collective-permute-start.2 = (f32[3,12,8,128]{3,2,1,0:T(8,128)S(1)}, f32[3,12,8,128]{3,2,1,0:T(8,128)S(1)}, u32[]{:S(2)}, u32[]{:S(2)}) collective-permute-start(f32[3,12,8,128]{3,2,1,0:T(8,128)S(1)} %get-tuple-element.43), channel_id=1, source_target_pairs={{0,2},{2,0},{4,6},{6,4},{1,3},{3,1},{5,7},{7,5},{8,10},{10,8},{12,... | collective-permute-start | bytes 442376 | tf_op jit(solution)/shard_map/ppermute | solution.py:84
  31.0 9.0 %collective-permute-start.3 = (f32[3,12,8,128]{3,2,1,0:T(8,128)S(1)}, f32[3,12,8,128]{3,2,1,0:T(8,128)S(1)}, u32[]{:S(2)}, u32[]{:S(2)}) collective-permute-start(f32[3,12,8,128]{3,2,1,0:T(8,128)S(1)} %get-tuple-element.44), channel_id=1, source_target_pairs={{0,6},{2,4},{4,2},{6,0},{1,7},{3,5},{5,3},{7,1},{8,14},{10,12},{12... | collective-permute-start | bytes 442376 | tf_op jit(solution)/shard_map/ppermute | solution.py:85
  37.9 9.6 %collective-permute-start.5 = (f32[16,8,128]{2,1,0:T(8,128)S(1)}, f32[16,8,128]{2,1,0:T(8,128)S(1)}, u32[]{:S(2)}, u32[]{:S(2)}) collective-permute-start(f32[16,8,128]{2,1,0:T(8,128)S(1)} %get-tuple-element.50), channel_id=1, source_target_pairs={{0,8},{8,0},{16,24},{24,16},{1,9},{9,1},{17,25},{25,17},{2,10},{10... | collective-permute-start | bytes 196616 | tf_op jit(solution)/shard_map/ppermute | solution.py:84
  38.8 8.7 %collective-permute-start.6 = (f32[16,8,128]{2,1,0:T(8,128)S(1)}, f32[16,8,128]{2,1,0:T(8,128)S(1)}, u32[]{:S(2)}, u32[]{:S(2)}) collective-permute-start(f32[16,8,128]{2,1,0:T(8,128)S(1)} %get-tuple-element.51), channel_id=1, source_target_pairs={{0,24},{8,16},{16,8},{24,0},{1,25},{9,17},{17,9},{25,1},{2,26},{10... | collective-permute-start | bytes 196616 | tf_op jit(solution)/shard_map/ppermute | solution.py:85
  41.7 4.2 %collective-permute-start.4 = (f32[3,4,8,128]{3,2,1,0:T(8,128)S(1)}, f32[3,4,8,128]{3,2,1,0:T(8,128)S(1)}, u32[]{:S(2)}, u32[]{:S(2)}) collective-permute-start(f32[3,4,8,128]{3,2,1,0:T(8,128)S(1)} %shard_map.108), channel_id=1, source_target_pairs={{0,1},{1,0},{2,3},{3,2},{4,5},{5,4},{6,7},{7,6},{8,9},{9,8},{10,11... | collective-permute-start | bytes 147464 | tf_op jit(solution)/shard_map/ppermute | solution.py:84
  66.4 12.7 %all-to-all-start.3 = ((f32[8,8,8,128]{3,2,1,0:T(8,128)}), f32[8,8,8,128]{3,2,1,0:T(8,128)S(1)}, u32[]{:S(2)}, u32[]{:S(2)}) async-start(f32[8,8,8,128]{3,2,1,0:T(8,128)} %get-tuple-element.61), calls=%async_computation.3 | async-start | bytes 524288 | tf_op jit(solution)/shard_map/all_to_all | solution.py:888
  70.0 4.3 %collective-permute-start.7 = (f32[1,4,4,8,128]{4,3,2,1,0:T(8,128)S(1)}, f32[1,4,4,8,128]{4,3,2,1,0:T(8,128)S(1)}, u32[]{:S(2)}, u32[]{:S(2)}) collective-permute-start(f32[1,4,4,8,128]{4,3,2,1,0:T(8,128)S(1)} %get-tuple-element.54), channel_id=1, source_target_pairs={{0,8},{8,0},{16,24},{24,16},{1,9},{9,1},{17,25},{25,17},{2,10},{10... | collective-permute-start | bytes 196616 | tf_op jit(solution)/shard_map/ppermute | solution.py:84
  71.1 6.1 %collective-permute-start.8 = (f32[1,4,4,8,128]{4,3,2,1,0:T(8,128)S(1)}, f32[1,4,4,8,128]{4,3,2,1,0:T(8,128)S(1)}, u32[]{:S(2)}, u32[]{:S(2)}) collective-permute-start(f32[1,4,4,8,128]{4,3,2,1,0:T(8,128)S(1)} %get-tuple-element.55), channel_id=1, source_target_pairs={{0,24},{8,16},{16,8},{24,0},{1,25},{9,17},{17,9},{25,1},{2,26},{10... | collective-permute-start | bytes 196616 | tf_op jit(solution)/shard_map/ppermute | solution.py:85
  77.2 7.4 %collective-permute-start.10 = (f32[1,12,8,128]{3,2,1,0:T(8,128)S(1)}, f32[1,12,8,128]{3,2,1,0:T(8,128)S(1)}, u32[]{:S(2)}, u32[]{:S(2)}) collective-permute-start(f32[1,12,8,128]{3,2,1,0:T(8,128)S(1)} %get-tuple-element.57), channel_id=1, source_target_pairs={{0,6},{2,4},{4,2},{6,0},{1,7},{3,5},{5,3},{7,1},{8,14},{10,12},{12... | collective-permute-start | bytes 147464 | tf_op jit(solution)/shard_map/ppermute | solution.py:85
  77.4 7.2 %collective-permute-start.9 = (f32[1,12,8,128]{3,2,1,0:T(8,128)S(1)}, f32[1,12,8,128]{3,2,1,0:T(8,128)S(1)}, u32[]{:S(2)}, u32[]{:S(2)}) collective-permute-start(f32[1,12,8,128]{3,2,1,0:T(8,128)S(1)} %get-tuple-element.56), channel_id=1, source_target_pairs={{0,2},{2,0},{4,6},{6,4},{1,3},{3,1},{5,7},{7,5},{8,10},{10,8},{12,... | collective-permute-start | bytes 147464 | tf_op jit(solution)/shard_map/ppermute | solution.py:84
  81.2 7.8 %collective-permute-start.12 = (f32[16,8,128]{2,1,0:T(8,128)S(1)}, f32[16,8,128]{2,1,0:T(8,128)S(1)}, u32[]{:S(2)}, u32[]{:S(2)}) collective-permute-start(f32[16,8,128]{2,1,0:T(8,128)S(1)} %get-tuple-element.63), channel_id=1, source_target_pairs={{0,8},{8,0},{16,24},{24,16},{1,9},{9,1},{17,25},{25,17},{2,10},{10... | collective-permute-start | bytes 196616 | tf_op jit(solution)/shard_map/ppermute | solution.py:84
  81.8 7.2 %collective-permute-start.13 = (f32[16,8,128]{2,1,0:T(8,128)S(1)}, f32[16,8,128]{2,1,0:T(8,128)S(1)}, u32[]{:S(2)}, u32[]{:S(2)}) collective-permute-start(f32[16,8,128]{2,1,0:T(8,128)S(1)} %get-tuple-element.64), channel_id=1, source_target_pairs={{0,24},{8,16},{16,8},{24,0},{1,25},{9,17},{17,9},{25,1},{2,26},{10... | collective-permute-start | bytes 196616 | tf_op jit(solution)/shard_map/ppermute | solution.py:85
  84.9 3.8 %collective-permute-start.11 = (f32[1,4,8,128]{3,2,1,0:T(8,128)S(1)}, f32[1,4,8,128]{3,2,1,0:T(8,128)S(1)}, u32[]{:S(2)}, u32[]{:S(2)}) collective-permute-start(f32[1,4,8,128]{3,2,1,0:T(8,128)S(1)} %shard_map.113), channel_id=1, source_target_pairs={{0,1},{1,0},{2,3},{3,2},{4,5},{5,4},{6,7},{7,6},{8,9},{9,8},{10,11... | collective-permute-start | bytes 49160 | tf_op jit(solution)/shard_map/ppermute | solution.py:84
  100.6 3.6 %collective-permute-start.14 = (f32[8,128]{1,0:T(8,128)S(1)}, f32[8,128]{1,0:T(8,128)S(1)}, u32[]{:S(2)}, u32[]{:S(2)}) collective-permute-start(f32[8,128]{1,0:T(8,128)S(1)} %shard_map.119), channel_id=1, source_target_pairs={{0,8},{8,0},{16,24},{24,16},{1,9},{9,1},{17,25},{25,17},{2,10},{10... | collective-permute-start | bytes 12296 | tf_op jit(solution)/shard_map/ppermute | solution.py:1030
  104.2 4.5 %collective-permute-start.15 = (f32[8,128]{1,0:T(8,128)S(1)}, f32[8,128]{1,0:T(8,128)S(1)}, u32[]{:S(2)}, u32[]{:S(2)}) collective-permute-start(f32[8,128]{1,0:T(8,128)S(1)} %add.6), channel_id=1, source_target_pairs={{0,16},{8,24},{16,0},{24,8},{1,17},{9,25},{17,1},{25,9},{2,18},{10... | collective-permute-start | bytes 12296 | tf_op jit(solution)/shard_map/ppermute | solution.py:1030

commit v4 on v3

--- a/solution.py
+++ b/solution.py
@@ -108,11 +108,27 @@
 
 
 def send_start_body(dims):
-    group, slots, nbx, nby, nbz = dims
-
-    def body(corner, owner, field, send, start, sem):
-        copy = pltpu.make_async_copy(field, start, sem)
+    ex, group, slots, nbx, nby, nbz = dims
+
+    def body(
+        corner_in, owner_in, field, shift, source, send, side_a, side_b, start, corner, owner, sem, sems
+    ):
+        small = [
+            pltpu.make_async_copy(corner_in, corner, sem.at[1]),
+            pltpu.make_async_copy(owner_in, owner, sem.at[2]),
+        ]
+        fetch(small)
+        copy = pltpu.make_async_copy(field, start, sem.at[0])
         copy.start()
+        odd = lax.axis_index("gx") % 2
+        sides = []
+        for index, raw in enumerate((field, shift, source)):
+            for side, goal in enumerate((side_a, side_b)):
+                high = 1 - odd if side == 0 else odd
+                planes = raw.at[pl.ds(high * (ex - WIDE), WIDE)]
+                sides.append(pltpu.make_async_copy(planes, goal.at[index], sems.at[index, side]))
+        fetch(sides)
+        arrive(small)
         pos = place_of()
         lanes = lane_id()
         note = jnp.zeros((SUB, LANES), F32)
@@ -140,23 +156,7 @@
 
                 extract(start, write, *blocks[slot])
 
-    return body
-
-
-def sides_body(ex):
-    def body(start, shift, source, side_a, side_b, sems):
-        pos = place_of()
-        odd = pos[0] % 2
-        copies = []
-        for index, field in enumerate((start, shift, source)):
-            for side, goal in enumerate((side_a, side_b)):
-                high = 1 - odd if side == 0 else odd
-                planes = field.at[pl.ds(high * (ex - WIDE), WIDE)]
-                copies.append(pltpu.make_async_copy(planes, goal.at[index], sems.at[index, side]))
-        for copy in copies:
-            copy.start()
-        for copy in copies:
-            copy.wait()
+        arrive(sides)
 
     return body
 
@@ -402,53 +402,20 @@
     lax.fori_loop(0, slots, box, 0)
 
 
-def prepare_body(slots):
-    def body(source, shift, start, kept, rate, state, *scratch):
-        ins, outs, sems = scratch[:3], scratch[3:6], scratch[6]
-        arrive(
-            fetch(
-                [
-                    pltpu.make_async_copy(raw, local, sems.at[index])
-                    for index, (raw, local) in enumerate(zip((source, shift, start), ins))
-                ]
-            )
-        )
-
-        def load(index, carry):
-            for x in range(SIDE):
-                at = pl.ds(SIDE * x + index, SUB, stride=slots)
-                outs[0][index, x] = ins[0][at, :]
-                outs[1][index, x] = OMEGA / (6.0 + ins[1][at, :])
-                outs[2][index, x] = ins[2][at, :]
-            return carry
-
-        lax.fori_loop(0, slots, load, 0)
-        arrive(
-            fetch(
-                [
-                    pltpu.make_async_copy(local, goal, sems.at[3 + index])
-                    for index, (local, goal) in enumerate(zip(outs, (kept, rate, state)))
-                ]
-            )
-        )
-
-    return body
-
-
 def fine_body(dims, first):
     group, slots, _, _, size_z = dims
 
     def body(*refs):
         if first:
             got, *stored = refs[:4]
-            ret, state_out, ghosts_out, squares, table = refs[4:9]
-            packed, other, state, ghosts, kept, rate, homes, moved, copied, counts, sems = refs[9:]
-            old = (kept, rate, other)
+            ret, state_out, squares, table, kept_out, rate_out = refs[4:10]
+            packed, other, state, ghosts, kept, rate, homes, moved, copied, counts, sems = refs[10:21]
+            old = refs[21:]
         else:
-            table, got, *stored = refs[:6]
-            ret, state_out, ghosts_out, squares = refs[6:10]
-            packed, other, state, ghosts, kept, rate, homes, moved, old_ghosts = refs[10:]
-            old = (kept, rate, other, old_ghosts)
+            table, got, *stored = refs[:5]
+            ret, state_out, squares = refs[5:8]
+            packed, other, state, ghosts, kept, rate, homes, moved = refs[8:]
+            old = (other, kept, rate)
         loads = [
             pltpu.make_async_copy(source, goal, moved.at[index])
             for index, (source, goal) in enumerate(zip(stored, old))
@@ -486,20 +453,33 @@
             homes[slot, 2] = jnp.int32(0)
         live = assign(rank, table, group, slots, found)
         unpack(packed, ghosts, slots)
-        saves = [pltpu.make_async_copy(ghosts, ghosts_out, moved.at[4])]
-        fetch(saves)
-        arrive(loads)
+        saves = []
+        arrive(loads if first else loads[:1])
         masks = fine_masks()
         lanes, rows = lane_id(), sub_id()
 
+        def convert(index, carry):
+            for x in range(SIDE):
+                at = pl.ds(SIDE * x + index, SUB, stride=slots)
+                kept[index, x] = old[0][at, :]
+                rate[index, x] = OMEGA / (6.0 + old[1][at, :])
+                other[index, x] = old[2][at, :]
+            return carry
+
+        if first:
+            lax.fori_loop(0, slots, convert, 0)
+            saves.append(pltpu.make_async_copy(kept, kept_out, moved.at[6]))
+            saves.append(pltpu.make_async_copy(rate, rate_out, moved.at[7]))
+            fetch(saves)
+
         def begin(index, carry):
             for x in range(SIDE):
-                change = ghosts[index, x // 2] - old_ghosts[index, x // 2]
-                other[index, x] = other[index, x] + change
+                other[index, x] = other[index, x] + ghosts[index, x // 2]
             return carry
 
         if not first:
             lax.fori_loop(0, slots, begin, 0)
+            arrive(loads[1:])
 
         def residual(buffer, index, x):
             value = buffer[index, x]
@@ -521,11 +501,13 @@
 
             lax.fori_loop(0, slots, step, 0)
         final = state
-        saves.append(pltpu.make_async_copy(state, state_out, moved.at[5]))
-        fetch(saves[1:])
+
+        def save(index):
+            return pltpu.make_async_copy(other.at[index], state_out.at[index], moved.at[index])
 
         def remainder(index, x):
             value, rest = residual(final, index, x)
+            other[index, x] = value - ghosts[index, x // 2]
             return rest - (OMEGA / rate[index, x]) * value
 
 
@@ -561,6 +543,7 @@
                     z_slab = jnp.where(lanes // WIDE == 2 * xp + part, piece, z_slab)
                 if xp % 4 == 3:
                     packed[index, xp // 4] = whole
+            save(index).start()
             home_z = homes[index, 0] % size_z
             for target in range(group):
                 ret[target, 4 + index] = jnp.where(home_z == target % size_z, y_slab, z_slab)
@@ -576,6 +559,7 @@
                 ret[homes[index, 0], 0:4] = packed[index]
 
         arrive(saves)
+        arrive([save(index) for index in range(slots)])
 
     return body
 
@@ -583,11 +567,8 @@
 def last_body(dims):
     group, slots, size_z = dims
 
-    def body(table, got, old_state, old_ghosts, goal, packed, fresh, state, ghosts, result, sems):
-        loads = [
-            pltpu.make_async_copy(old_ghosts, ghosts, sems.at[0]),
-            pltpu.make_async_copy(old_state, state, sems.at[1]),
-        ]
+    def body(table, got, old_state, goal, packed, fresh, state, result, sems):
+        loads = [pltpu.make_async_copy(old_state, state, sems.at[0])]
         fetch(loads)
         rank = lax.axis_index("gy") * size_z + lax.axis_index("gz")
         packed[...] = jnp.zeros(packed.shape, F32)
@@ -601,13 +582,13 @@
 
         def box(index, carry):
             for x in range(SIDE):
-                value = state[index, x] + (fresh[index, x // 2] - ghosts[index, x // 2])
+                value = state[index, x] + fresh[index, x // 2]
                 value = jnp.where(index < live, value, 0.0)
                 result[pl.ds(SIDE * x + index, SUB, stride=slots), :] = value
             return carry
 
         lax.fori_loop(0, slots, box, 0)
-        arrive(fetch([pltpu.make_async_copy(result, goal, sems.at[2])]))
+        arrive(fetch([pltpu.make_async_copy(result, goal, sems.at[1])]))
 
     return body
 
@@ -929,20 +910,20 @@
             ],
         )
 
-    (send,) = call(
-        send_start_body((group, slots, nbx, nby, nbz)),
-        [(SMEM, corner), (SMEM, box_owner), (HBM, start)],
-        [(VMEM, out(group, 5, SUB, LANES))],
-        [pltpu.VMEM((ex, nt, SUB, LANES), F32), pltpu.SemaphoreType.DMA],
+    fields = [start, shift, source]
+    send, side_a, side_b = call(
+        send_start_body((ex, group, slots, nbx, nby, nbz)),
+        [(HBM, value) for value in (corner, box_owner, *fields)],
+        [(VMEM, out(group, 5, SUB, LANES))] + [(VMEM, out(3, WIDE, nt, SUB, LANES))] * 2,
+        [
+            pltpu.VMEM((ex, nt, SUB, LANES), F32),
+            pltpu.SMEM(corner.shape, jnp.int32),
+            pltpu.SMEM(box_owner.shape, jnp.int32),
+            pltpu.SemaphoreType.DMA((3,)),
+            pltpu.SemaphoreType.DMA((3, 2)),
+        ],
     )
     got = exchange(send)
-    fields = [start, shift, source]
-    side_a, side_b = call(
-        sides_body(ex),
-        [(HBM, field) for field in fields],
-        [(VMEM, out(3, WIDE, nt, SUB, LANES))] * 2,
-        [pltpu.SemaphoreType.DMA((3, 2))],
-    )
     wide, rate, source_wide = halos(fields, side_a, side_b, 3)
 
     box_shape = (slots, SIDE, SUB, LANES)
@@ -950,18 +931,11 @@
     whole = pltpu.VMEM(box_shape, F32)
     ghost = pltpu.VMEM((slots, FOOT, SUB, LANES), F32)
     packs = pltpu.VMEM((slots, 4, SUB, LANES), F32)
-    kept, f_rate, state = call(
-        prepare_body(slots),
-        [(HBM, value) for value in (f_source, f_shift, f_start)],
-        [(HBM, out(*box_shape))] * 3,
-        [flat] * 3 + [whole] * 3 + [pltpu.SemaphoreType.DMA((6,))],
-    )
     box_scratch = [packs, whole, whole, ghost, whole, whole]
-    box_scratch += [pltpu.SMEM((slots, 3), jnp.int32), pltpu.SemaphoreType.DMA((6,))]
+    box_scratch += [pltpu.SMEM((slots, 3), jnp.int32), pltpu.SemaphoreType.DMA((8,))]
     box_outs = [
         (VMEM, out(group, 4 + slots, SUB, LANES)),
         (HBM, out(*box_shape)),
-        (HBM, out(slots, FOOT, SUB, LANES)),
         (VMEM, out(SUB, LANES)),
     ]
     norms = []
@@ -970,24 +944,27 @@
         first = cycle == 0
         body = fine_body((group, slots, nby, nbz, size_z), first)
         if first:
-            ret, state, ghosts, squares, table = call(
+            ret, state, squares, table, kept, f_rate = call(
                 body,
-                [(VMEM, got)] + [(HBM, value) for value in (kept, f_rate, state)],
-                box_outs + [(SMEM, out(group, COLS * slots, dtype=jnp.int32))],
+                [(VMEM, got)] + [(HBM, value) for value in (f_source, f_shift, f_start)],
+                box_outs
+                + [(SMEM, out(group, COLS * slots, dtype=jnp.int32))]
+                + [(HBM, out(*box_shape))] * 2,
                 box_scratch
                 + [
                     pltpu.SMEM((group, LANES), F32),
                     pltpu.SMEM((group + 1,), jnp.int32),
                     pltpu.SemaphoreType.DMA((group,)),
-                ],
+                ]
+                + [flat] * 3,
             )
         else:
-            ret, state, ghosts, squares = call(
+            ret, state, squares = call(
                 body,
                 [(SMEM, table), (VMEM, got)]
-                + [(HBM, value) for value in (kept, f_rate, state, ghosts)],
+                + [(HBM, value) for value in (state, kept, f_rate)],
                 box_outs,
-                box_scratch + [ghost],
+                box_scratch,
             )
         back = exchange(ret)
         units = (WIDE - 1) * (nt + 1) + 1
@@ -1019,9 +996,9 @@
     (total,) = call(norm_body(group), [(VMEM, got)], [(VMEM, out(SUB, LANES))])
     (values,) = call(
         last_body((group, slots, size_z)),
-        [(SMEM, table), (VMEM, got), (HBM, state), (HBM, ghosts)],
+        [(SMEM, table), (VMEM, got), (HBM, state)],
         [(HBM, out(slots * fine // LANES, LANES))],
-        [packs, ghost, whole, ghost, flat, pltpu.SemaphoreType.DMA((3,))],
+        [packs, ghost, whole, flat, pltpu.SemaphoreType.DMA((2,))],
     )
     cells = float(ex * ey * ez * size_x * size_y * size_z)
     bit = 1

time: 110 us -> 107 us (0.973)
  Pallas kernels: 41.7 us -> 37.4 us
  waiting for transfers between devices: 17.8 us -> 19.4 us
    pallas_call x17 -> x15, Pallas kernels: 41.7 us -> 37.4 us  [call(): pl.pallas_call(body, in_specs=[spec for spec, _ in ins], out_specs=[spec...]
    ppermute x6, starting transfers between devices: 10 us -> 8.42 us  [swap(): got_b = lax.ppermute(second, axis, pairs_b) if count > 2 else got_a]
    ppermute x2, starting transfers between devices: 0.45 us -> 1.83 us  [work(): total = total + lax.ppermute(total, 'gx', pairs)]
    all_to_all x3, waiting for transfers between devices: 3.13 us -> 4.42 us  [exchange(): lax.all_to_all(value, GROUP_AXES, split_axis=0, concat_axis=0, tiled=True)]
    ppermute x2, waiting for transfers between devices: 5.02 us -> 3.74 us  [work(): total = total + lax.ppermute(total, 'gx', pairs)]
  transfers between devices with their start and end apart: 19 -> 19, of which waited for: 7 -> 9; matrix products, arithmetic and copies ran while one was open for 0% -> 0% of each run, Pallas kernels for 22% -> 19%
where the time goes in v4:
time: 107 us; the launch traced here: 106 us
  Pallas kernels  37.4 us (35%)
  starting transfers between devices  32.5 us (30%)
  waiting for transfers between devices  19.4 us (18%)
  blocking collectives  15.5 us (14%)
    pallas_call x15, Pallas kernels, call(): pl.pallas_call(body, in_specs=[spec for spec, _ in ins], out_specs=[spec...  37.4 us
    all_to_all x2, blocking collectives, exchange(): lax.all_to_all(value, GROUP_AXES, split_axis=0, concat_axis=0, tiled=True)  15.5 us
    all_to_all x3, starting transfers between devices, exchange(): lax.all_to_all(value, GROUP_AXES, split_axis=0, concat_axis=0, tiled=True)  12 us
    ppermute x8, starting transfers between devices, swap(): got_a = lax.ppermute(first, axis, pairs_a)  10.2 us
    ppermute x6, starting transfers between devices, swap(): got_b = lax.ppermute(second, axis, pairs_b) if count > 2 else got_a  8.42 us
    ppermute x8, waiting for transfers between devices, swap(): got_a = lax.ppermute(first, axis, pairs_a)  7.69 us
    all_to_all x3, waiting for transfers between devices, exchange(): lax.all_to_all(value, GROUP_AXES, split_axis=0, concat_axis=0, tiled=True)  4.42 us
    ppermute x2, waiting for transfers between devices, work(): total = total + lax.ppermute(total, 'gx', pairs)  3.74 us
  transfers between devices with their start and end apart: 19, of which 9 were waited for; matrix products, arithmetic and copies ran while one was open for 0% of the time, Pallas kernels for 19%

profile of v4, /device:TPU:0, one launch (start us, length us, event | category | flops | bytes accessed | tf_op | source)
XLA Modules:
  0.0 106.3 jit_solution(9135942318538247026)
XLA Ops:
  0.6 2.1 %shard_map.103 = (f32[8,5,8,128]{3,2,1,0:T(8,128)}, f32[3,4,4,8,128]{4,3,2,1,0:T(8,128)S(1)}, f32[3,4,4,8,128]{4,3,2,1,0:T(8,128)S(1)}) custom-call(s32[3,1,4]{2,1,0:T(1,128)} %bitcast.41, s32[1,4]{1,0:T(1,128)} %owner_in.1, f32[16,4,8,128]{3,2,1,0:T(8,128)} %bitcast.25, f32[16,4,8,128]{3,2,1,0:T(8,128)} %bitcast.29, f32[16,4,8,128]{3,2,1,0:T(8,128)} %bitcast.33), custom_call_target="tpu_custom_call" | custom-call | tf_op jit(solution)/shard_map/pallas_call | solution.py:38
  2.8 5.0 %all-to-all-start = ((f32[8,5,8,128]{3,2,1,0:T(8,128)}), f32[8,5,8,128]{3,2,1,0:T(8,128)S(1)}, u32[]{:S(2)}, u32[]{:S(2)}) async-start(f32[8,5,8,128]{3,2,1,0:T(8,128)} %get-tuple-element.35), calls=%async_computation | async-start | bytes 327680 | tf_op jit(solution)/shard_map/all_to_all | solution.py:869
  7.8 1.8 %collective-permute-start = (f32[3,4,4,8,128]{4,3,2,1,0:T(8,128)S(1)}, f32[3,4,4,8,128]{4,3,2,1,0:T(8,128)S(1)}, u32[]{:S(2)}, u32[]{:S(2)}) collective-permute-start(f32[3,4,4,8,128]{4,3,2,1,0:T(8,128)S(1)} %get-tuple-element.37), channel_id=1, source_target_pairs={{0,8},{8,0},{16,24},{24,16},{1,9},{9,1},{17,25},{25,17},{2,10},{10... | collective-permute-start | bytes 589832 | tf_op jit(solution)/shard_map/ppermute | solution.py:84
  9.6 2.3 %collective-permute-start.1 = (f32[3,4,4,8,128]{4,3,2,1,0:T(8,128)S(1)}, f32[3,4,4,8,128]{4,3,2,1,0:T(8,128)S(1)}, u32[]{:S(2)}, u32[]{:S(2)}) collective-permute-start(f32[3,4,4,8,128]{4,3,2,1,0:T(8,128)S(1)} %get-tuple-element.38), channel_id=1, source_target_pairs={{0,24},{8,16},{16,8},{24,0},{1,25},{9,17},{17,9},{25,1},{2,26},{10... | collective-permute-start | bytes 589832 | tf_op jit(solution)/shard_map/ppermute | solution.py:85
  11.8 1.4 %all-to-all-done.refs_0_ = f32[8,5,8,128]{3,2,1,0:T(8,128)S(1)} async-done(((f32[8,5,8,128]{3,2,1,0:T(8,128)}), f32[8,5,8,128]{3,2,1,0:T(8,128)S(1)}, u32[]{:S(2)}, u32[]{:S(2)}) %all-to-all-start) | async-done | bytes 163872 | tf_op jit(solution)/shard_map/all_to_all | solution.py:869
  13.2 8.5 %shard_map.104 = (f32[8,8,8,128]{3,2,1,0:T(8,128)}, f32[4,32,8,128]{3,2,1,0:T(8,128)}, f32[8,128]{1,0:T(8,128)S(1)}, s32[8,32]{1,0:T(8,128)S(1)}, f32[4,32,8,128]{3,2,1,0:T(8,128)}, /*index=5*/f32[4,32,8,128]{3,2,1,0:T(8,128)}) custom-call(f32[8,5,8,128]{3,2,1,0:T(8,128)S(1)} %all-to-all-done.refs_0_, f32[1024,128]{1,0:T(8,128)} %bitcast.38, ...), custom_call_target="tpu_custom_call" | custom-call | tf_op jit(solution)/shard_map/pallas_call | solution.py:38
  21.7 3.4 %all-to-all-start.1 = ((f32[8,8,8,128]{3,2,1,0:T(8,128)}), f32[8,8,8,128]{3,2,1,0:T(8,128)S(1)}, u32[]{:S(2)}, u32[]{:S(2)}) async-start(f32[8,8,8,128]{3,2,1,0:T(8,128)} %get-tuple-element.44), calls=%async_computation.1 | async-start | bytes 524288 | tf_op jit(solution)/shard_map/all_to_all | solution.py:869
  25.1 0.0 collective-permute-done.refs_3_
  25.1 0.0 collective-permute-done.1.refs_4_
  25.2 1.1 %shard_map.105 = (f32[3,12,8,128]{3,2,1,0:T(8,128)S(1)}, f32[3,12,8,128]{3,2,1,0:T(8,128)S(1)}) custom-call(f32[16,4,8,128]{3,2,1,0:T(8,128)} %bitcast.26, f32[16,4,8,128]{3,2,1,0:T(8,128)} %bitcast.30, f32[16,4,8,128]{3,2,1,0:T(8,128)} %bitcast.34, f32[3,4,4,8,128]{4,3,2,1,0:T(8,128)S(1)} %collective-permute-done.refs_3_, ...), custom_call_target="tpu_custom_call" | custom-call | tf_op jit(solution)/shard_map/pallas_call | solution.py:38
  26.2 0.5 collective-permute-start.2
  26.7 1.6 %collective-permute-start.3 = (f32[3,12,8,128]{3,2,1,0:T(8,128)S(1)}, f32[3,12,8,128]{3,2,1,0:T(8,128)S(1)}, u32[]{:S(2)}, u32[]{:S(2)}) collective-permute-start(f32[3,12,8,128]{3,2,1,0:T(8,128)S(1)} %get-tuple-element.40), channel_id=1, source_target_pairs={{0,6},{2,4},{4,2},{6,0},{1,7},{3,5},{5,3},{7,1},{8,14},{10,12},{12... | collective-permute-start | bytes 442376 | tf_op jit(solution)/shard_map/ppermute | solution.py:85
  28.4 3.1 %all-to-all-done.1.got = f32[8,8,8,128]{3,2,1,0:T(8,128)S(1)} async-done(((f32[8,8,8,128]{3,2,1,0:T(8,128)}), f32[8,8,8,128]{3,2,1,0:T(8,128)S(1)}, u32[]{:S(2)}, u32[]{:S(2)}) %all-to-all-start.1) | async-done | bytes 262176 | tf_op jit(solution)/shard_map/all_to_all | solution.py:869
  31.4 2.1 %shard_map.108 = (f32[16,2,5,8,128]{4,3,2,1,0:T(8,128)S(1)}, f32[16,8,128]{2,1,0:T(8,128)S(1)}, f32[16,8,128]{2,1,0:T(8,128)S(1)}) custom-call(s32[8,32]{1,0:T(8,128)S(1)} %get-tuple-element.36.table.refs_0_, f32[8,8,8,128]{3,2,1,0:T(8,128)S(1)} %all-to-all-done.1.got), custom_call_target="tpu_custom_call" | custom-call | tf_op jit(solution)/shard_map/pallas_call | solution.py:38
  33.5 1.8 %collective-permute-start.5 = (f32[16,8,128]{2,1,0:T(8,128)S(1)}, f32[16,8,128]{2,1,0:T(8,128)S(1)}, u32[]{:S(2)}, u32[]{:S(2)}) collective-permute-start(f32[16,8,128]{2,1,0:T(8,128)S(1)} %get-tuple-element.46), channel_id=1, source_target_pairs={{0,8},{8,0},{16,24},{24,16},{1,9},{9,1},{17,25},{25,17},{2,10},{10... | collective-permute-start | bytes 196616 | tf_op jit(solution)/shard_map/ppermute | solution.py:84
  35.3 2.6 %collective-permute-start.6 = (f32[16,8,128]{2,1,0:T(8,128)S(1)}, f32[16,8,128]{2,1,0:T(8,128)S(1)}, u32[]{:S(2)}, u32[]{:S(2)}) collective-permute-start(f32[16,8,128]{2,1,0:T(8,128)S(1)} %get-tuple-element.47), channel_id=1, source_target_pairs={{0,24},{8,16},{16,8},{24,0},{1,25},{9,17},{17,9},{25,1},{2,26},{10... | collective-permute-start | bytes 196616 | tf_op jit(solution)/shard_map/ppermute | solution.py:85
  37.9 0.0 collective-permute-done.2.refs_5_
  37.9 0.0 collective-permute-done.3.refs_6_
  37.9 1.6 %shard_map.106 = f32[3,4,8,128]{3,2,1,0:T(8,128)S(1)} custom-call(f32[16,4,8,128]{3,2,1,0:T(8,128)} %bitcast.27, f32[16,4,8,128]{3,2,1,0:T(8,128)} %bitcast.31, f32[16,4,8,128]{3,2,1,0:T(8,128)} %bitcast.35, f32[3,4,4,8,128]{4,3,2,1,0:T(8,128)S(1)} %collective-permute-done.refs_3_, f32[3,4,4,8,128]{4,3,2,1,0:T(8,128)S(1)} %collective-permute-done.1.refs_4_, ...), custom_call_target="tpu_custom_call" | custom-call | tf_op jit(solution)/shard_map/pallas_call | solution.py:38
  39.6 1.3 %collective-permute-start.4 = (f32[3,4,8,128]{3,2,1,0:T(8,128)S(1)}, f32[3,4,8,128]{3,2,1,0:T(8,128)S(1)}, u32[]{:S(2)}, u32[]{:S(2)}) collective-permute-start(f32[3,4,8,128]{3,2,1,0:T(8,128)S(1)} %shard_map.106), channel_id=1, source_target_pairs={{0,1},{1,0},{2,3},{3,2},{4,5},{5,4},{6,7},{7,6},{8,9},{9,8},{10,11... | collective-permute-start | bytes 147464 | tf_op jit(solution)/shard_map/ppermute | solution.py:84
  40.9 2.8 %collective-permute-done.4.refs_7_ = f32[3,4,8,128]{3,2,1,0:T(8,128)S(1)} collective-permute-done((f32[3,4,8,128]{3,2,1,0:T(8,128)S(1)}, f32[3,4,8,128]{3,2,1,0:T(8,128)S(1)}, u32[]{:S(2)}, u32[]{:S(2)}) %collective-permute-start.4) | collective-permute-done | bytes 49184 | tf_op jit(solution)/shard_map/ppermute | solution.py:84
  43.7 1.6 %shard_map.107 = (f32[24,2,40,128]{3,2,1,0:T(8,128)S(1)}, f32[24,2,40,128]{3,2,1,0:T(8,128)S(1)}, f32[24,2,40,128]{3,2,1,0:T(8,128)S(1)}) custom-call(f32[16,4,8,128]{3,2,1,0:T(8,128)} %bitcast.28, f32[16,4,8,128]{3,2,1,0:T(8,128)} %bitcast.32, f32[16,4,8,128]{3,2,1,0:T(8,128)} %bitcast.36, f32[3,4,4,8,128]{4,3,2,1,0:T(8,128)S(1)} %collective-permute-done.refs_3_, ...), custom_call_target="tpu_custom_call" | custom-call | tf_op jit(solution)/shard_map/pallas_call | solution.py:38
  45.3 0.0 collective-permute-done.5.xa
  45.3 0.0 collective-permute-done.6.xb
  45.4 3.0 %shard_map.109 = (f32[16,4,8,128]{3,2,1,0:T(8,128)S(1)}, f32[8,4,8,128]{3,2,1,0:T(8,128)S(1)}, f32[8,128]{1,0:T(8,128)S(1)}, f32[1,4,4,8,128]{4,3,2,1,0:T(8,128)S(1)}, f32[1,4,4,8,128]{4,3,2,1,0:T(8,128)S(1)}) custom-call(s32[8,32]{1,0:T(8,128)S(1)} %get-tuple-element.36.table.refs_0_, f32[24,2,40,128]{3,2,1,0:T(8,128)S(1)} %get-tuple-element.41.wide, ...), custom_call_target="tpu_custom_call" | custom-call | tf_op jit(solution)/shard_map/pallas_call | solution.py:38
  48.4 7.5 %all_to_all.25.refs_1_ = f32[8,4,8,128]{3,2,1,0:T(8,128)S(1)} all-to-all(f32[8,4,8,128]{3,2,1,0:T(8,128)S(1)} %get-tuple-element.54), channel_id=1, replica_groups=mesh['gx'=4,'gy'=4,'gz'=2] {'gy','gz'}, dimensions={0} | all-to-all | bytes 262144 | tf_op jit(solution)/shard_map/all_to_all | solution.py:869
  55.9 8.3 %shard_map.113 = (f32[8,8,8,128]{3,2,1,0:T(8,128)}, f32[4,32,8,128]{3,2,1,0:T(8,128)}, f32[8,128]{1,0:T(8,128)S(1)}) custom-call(s32[8,32]{1,0:T(8,128)S(1)} %get-tuple-element.36.table.refs_0_, f32[8,4,8,128]{3,2,1,0:T(8,128)S(1)} %all_to_all.25.refs_1_, f32[4,32,8,128]{3,2,1,0:T(8,128)} %get-tuple-element.55.refs_2_, ...), custom_call_target="tpu_custom_call" | custom-call | tf_op jit(solution)/shard_map/pallas_call | solution.py:38
  64.2 3.6 %all-to-all-start.3 = ((f32[8,8,8,128]{3,2,1,0:T(8,128)}), f32[8,8,8,128]{3,2,1,0:T(8,128)S(1)}, u32[]{:S(2)}, u32[]{:S(2)}) async-start(f32[8,8,8,128]{3,2,1,0:T(8,128)} %get-tuple-element.58), calls=%async_computation.3 | async-start | bytes 524288 | tf_op jit(solution)/shard_map/all_to_all | solution.py:869
  67.8 1.1 collective-permute-start.7
  68.9 0.8 collective-permute-start.8
  69.6 2.5 %collective-permute-done.7.refs_1_ = f32[1,4,4,8,128]{4,3,2,1,0:T(8,128)S(1)} collective-permute-done((f32[1,4,4,8,128]{4,3,2,1,0:T(8,128)S(1)}, f32[1,4,4,8,128]{4,3,2,1,0:T(8,128)S(1)}, u32[]{:S(2)}, u32[]{:S(2)}) %collective-permute-start.7) | collective-permute-done | bytes 65568 | tf_op jit(solution)/shard_map/ppermute | solution.py:84
  72.1 2.8 %collective-permute-done.8.refs_2_ = f32[1,4,4,8,128]{4,3,2,1,0:T(8,128)S(1)} collective-permute-done((f32[1,4,4,8,128]{4,3,2,1,0:T(8,128)S(1)}, f32[1,4,4,8,128]{4,3,2,1,0:T(8,128)S(1)}, u32[]{:S(2)}, u32[]{:S(2)}) %collective-permute-start.8) | collective-permute-done | bytes 65568 | tf_op jit(solution)/shard_map/ppermute | solution.py:85
  74.9 0.1 shard_map.110
  75.0 0.2 collective-permute-start.10
  75.2 1.7 %collective-permute-start.9 = (f32[1,12,8,128]{3,2,1,0:T(8,128)S(1)}, f32[1,12,8,128]{3,2,1,0:T(8,128)S(1)}, u32[]{:S(2)}, u32[]{:S(2)}) collective-permute-start(f32[1,12,8,128]{3,2,1,0:T(8,128)S(1)} %get-tuple-element.52), channel_id=1, source_target_pairs={{0,2},{2,0},{4,6},{6,4},{1,3},{3,1},{5,7},{7,5},{8,10},{10,8},{12,... | collective-permute-start | bytes 147464 | tf_op jit(solution)/shard_map/ppermute | solution.py:84
  76.9 0.0 all-to-all-done.3.got
  76.9 2.1 %shard_map.114 = (f32[16,2,5,8,128]{4,3,2,1,0:T(8,128)S(1)}, f32[16,8,128]{2,1,0:T(8,128)S(1)}, f32[16,8,128]{2,1,0:T(8,128)S(1)}) custom-call(s32[8,32]{1,0:T(8,128)S(1)} %get-tuple-element.36.table.refs_0_, f32[8,8,8,128]{3,2,1,0:T(8,128)S(1)} %all-to-all-done.3.got), custom_call_target="tpu_custom_call" | custom-call | tf_op jit(solution)/shard_map/pallas_call | solution.py:38
  79.0 0.6 collective-permute-start.12
  79.6 0.9 collective-permute-start.13
  80.5 0.0 collective-permute-done.10.refs_4_
  80.5 0.0 collective-permute-done.9.refs_3_
  80.5 0.3 shard_map.111
  80.8 1.4 %collective-permute-start.11 = (f32[1,4,8,128]{3,2,1,0:T(8,128)S(1)}, f32[1,4,8,128]{3,2,1,0:T(8,128)S(1)}, u32[]{:S(2)}, u32[]{:S(2)}) collective-permute-start(f32[1,4,8,128]{3,2,1,0:T(8,128)S(1)} %shard_map.111), channel_id=1, source_target_pairs={{0,1},{1,0},{2,3},{3,2},{4,5},{5,4},{6,7},{7,6},{8,9},{9,8},{10,11... | collective-permute-start | bytes 49160 | tf_op jit(solution)/shard_map/ppermute | solution.py:84
  82.3 2.4 %collective-permute-done.11.refs_5_ = f32[1,4,8,128]{3,2,1,0:T(8,128)S(1)} collective-permute-done((f32[1,4,8,128]{3,2,1,0:T(8,128)S(1)}, f32[1,4,8,128]{3,2,1,0:T(8,128)S(1)}, u32[]{:S(2)}, u32[]{:S(2)}) %collective-permute-start.11) | collective-permute-done | bytes 16416 | tf_op jit(solution)/shard_map/ppermute | solution.py:84
  84.6 0.3 shard_map.112.wide
  84.9 0.0 collective-permute-done.12.xa
  84.9 0.7 collective-permute-done.13.xb
  85.7 3.8 %shard_map.115 = (f32[16,4,8,128]{3,2,1,0:T(8,128)}, f32[8,5,8,128]{3,2,1,0:T(8,128)S(1)}, f32[8,128]{1,0:T(8,128)}) custom-call(s32[8,32]{1,0:T(8,128)S(1)} %get-tuple-element.36.table.refs_0_, f32[24,2,40,128]{3,2,1,0:T(8,128)S(1)} %shard_map.112.wide, f32[24,2,40,128]{3,2,1,0:T(8,128)S(1)} %get-tuple-element.42.rate, ...), custom_call_target="tpu_custom_call" | custom-call | tf_op jit(solution)/shard_map/pallas_call | solution.py:38
  89.5 8.0 %all_to_all.26.got = f32[8,5,8,128]{3,2,1,0:T(8,128)S(1)} all-to-all(f32[8,5,8,128]{3,2,1,0:T(8,128)S(1)} %get-tuple-element.65), channel_id=1, replica_groups=mesh['gx'=4,'gy'=4,'gz'=2] {'gy','gz'}, dimensions={0} | all-to-all | bytes 327680 | tf_op jit(solution)/shard_map/all_to_all | solution.py:869
  97.5 0.7 collective-permute-start.14
  98.2 2.9 %collective-permute-done.14 = f32[8,128]{1,0:T(8,128)S(1)} collective-permute-done((f32[8,128]{1,0:T(8,128)S(1)}, f32[8,128]{1,0:T(8,128)S(1)}, u32[]{:S(2)}, u32[]{:S(2)}) %collective-permute-start.14) | collective-permute-done | bytes 4128 | tf_op jit(solution)/shard_map/ppermute | solution.py:1007
  101.1 1.1 %collective-permute-start.15 = (f32[8,128]{1,0:T(8,128)S(1)}, f32[8,128]{1,0:T(8,128)S(1)}, u32[]{:S(2)}, u32[]{:S(2)}) collective-permute-start(f32[8,128]{1,0:T(8,128)S(1)} %add.6), channel_id=1, source_target_pairs={{0,16},{8,24},{16,0},{24,8},{1,17},{9,25},{17,1},{25,9},{2,18},{10... | collective-permute-start | bytes 12296 | tf_op jit(solution)/shard_map/ppermute | solution.py:1007
  102.2 2.5 %shard_map.116 = f32[1024,128]{1,0:T(8,128)} custom-call(s32[8,32]{1,0:T(8,128)S(1)} %get-tuple-element.36.table.refs_0_, f32[8,5,8,128]{3,2,1,0:T(8,128)S(1)} %all_to_all.26.got, f32[4,32,8,128]{3,2,1,0:T(8,128)} %get-tuple-element.66.old_state), custom_call_target="tpu_custom_call" | custom-call | tf_op jit(solution)/shard_map/pallas_call | solution.py:38
  104.7 0.9 collective-permute-done.15
  105.6 0.1 slice_reduce_fusion
  105.7 0.5 multiply_sqrt_fusion
  (3 shorter events, 0.0 us)
Async XLA Ops:
  2.8 10.4 %all-to-all-start = ((f32[8,5,8,128]{3,2,1,0:T(8,128)}), f32[8,5,8,128]{3,2,1,0:T(8,128)S(1)}, u32[]{:S(2)}, u32[]{:S(2)}) async-start(f32[8,5,8,128]{3,2,1,0:T(8,128)} %get-tuple-element.35), calls=%async_computation | async-start | bytes 327680 | tf_op jit(solution)/shard_map/all_to_all | solution.py:869
  7.8 17.4 %collective-permute-start = (f32[3,4,4,8,128]{4,3,2,1,0:T(8,128)S(1)}, f32[3,4,4,8,128]{4,3,2,1,0:T(8,128)S(1)}, u32[]{:S(2)}, u32[]{:S(2)}) collective-permute-start(f32[3,4,4,8,128]{4,3,2,1,0:T(8,128)S(1)} %get-tuple-element.37), channel_id=1, source_target_pairs={{0,8},{8,0},{16,24},{24,16},{1,9},{9,1},{17,25},{25,17},{2,10},{10... | collective-permute-start | bytes 589832 | tf_op jit(solution)/shard_map/ppermute | solution.py:84
  9.6 15.6 %collective-permute-start.1 = (f32[3,4,4,8,128]{4,3,2,1,0:T(8,128)S(1)}, f32[3,4,4,8,128]{4,3,2,1,0:T(8,128)S(1)}, u32[]{:S(2)}, u32[]{:S(2)}) collective-permute-start(f32[3,4,4,8,128]{4,3,2,1,0:T(8,128)S(1)} %get-tuple-element.38), channel_id=1, source_target_pairs={{0,24},{8,16},{16,8},{24,0},{1,25},{9,17},{17,9},{25,1},{2,26},{10... | collective-permute-start | bytes 589832 | tf_op jit(solution)/shard_map/ppermute | solution.py:85
  21.7 9.7 %all-to-all-start.1 = ((f32[8,8,8,128]{3,2,1,0:T(8,128)}), f32[8,8,8,128]{3,2,1,0:T(8,128)S(1)}, u32[]{:S(2)}, u32[]{:S(2)}) async-start(f32[8,8,8,128]{3,2,1,0:T(8,128)} %get-tuple-element.44), calls=%async_computation.1 | async-start | bytes 524288 | tf_op jit(solution)/shard_map/all_to_all | solution.py:869
  26.2 11.7 %collective-permute-start.2 = (f32[3,12,8,128]{3,2,1,0:T(8,128)S(1)}, f32[3,12,8,128]{3,2,1,0:T(8,128)S(1)}, u32[]{:S(2)}, u32[]{:S(2)}) collective-permute-start(f32[3,12,8,128]{3,2,1,0:T(8,128)S(1)} %get-tuple-element.39), channel_id=1, source_target_pairs={{0,2},{2,0},{4,6},{6,4},{1,3},{3,1},{5,7},{7,5},{8,10},{10,8},{12,... | collective-permute-start | bytes 442376 | tf_op jit(solution)/shard_map/ppermute | solution.py:84
  26.7 11.2 %collective-permute-start.3 = (f32[3,12,8,128]{3,2,1,0:T(8,128)S(1)}, f32[3,12,8,128]{3,2,1,0:T(8,128)S(1)}, u32[]{:S(2)}, u32[]{:S(2)}) collective-permute-start(f32[3,12,8,128]{3,2,1,0:T(8,128)S(1)} %get-tuple-element.40), channel_id=1, source_target_pairs={{0,6},{2,4},{4,2},{6,0},{1,7},{3,5},{5,3},{7,1},{8,14},{10,12},{12... | collective-permute-start | bytes 442376 | tf_op jit(solution)/shard_map/ppermute | solution.py:85
  33.5 11.8 %collective-permute-start.5 = (f32[16,8,128]{2,1,0:T(8,128)S(1)}, f32[16,8,128]{2,1,0:T(8,128)S(1)}, u32[]{:S(2)}, u32[]{:S(2)}) collective-permute-start(f32[16,8,128]{2,1,0:T(8,128)S(1)} %get-tuple-element.46), channel_id=1, source_target_pairs={{0,8},{8,0},{16,24},{24,16},{1,9},{9,1},{17,25},{25,17},{2,10},{10... | collective-permute-start | bytes 196616 | tf_op jit(solution)/shard_map/ppermute | solution.py:84
  35.3 10.1 %collective-permute-start.6 = (f32[16,8,128]{2,1,0:T(8,128)S(1)}, f32[16,8,128]{2,1,0:T(8,128)S(1)}, u32[]{:S(2)}, u32[]{:S(2)}) collective-permute-start(f32[16,8,128]{2,1,0:T(8,128)S(1)} %get-tuple-element.47), channel_id=1, source_target_pairs={{0,24},{8,16},{16,8},{24,0},{1,25},{9,17},{17,9},{25,1},{2,26},{10... | collective-permute-start | bytes 196616 | tf_op jit(solution)/shard_map/ppermute | solution.py:85
  39.6 4.2 %collective-permute-start.4 = (f32[3,4,8,128]{3,2,1,0:T(8,128)S(1)}, f32[3,4,8,128]{3,2,1,0:T(8,128)S(1)}, u32[]{:S(2)}, u32[]{:S(2)}) collective-permute-start(f32[3,4,8,128]{3,2,1,0:T(8,128)S(1)} %shard_map.106), channel_id=1, source_target_pairs={{0,1},{1,0},{2,3},{3,2},{4,5},{5,4},{6,7},{7,6},{8,9},{9,8},{10,11... | collective-permute-start | bytes 147464 | tf_op jit(solution)/shard_map/ppermute | solution.py:84
  64.2 12.7 %all-to-all-start.3 = ((f32[8,8,8,128]{3,2,1,0:T(8,128)}), f32[8,8,8,128]{3,2,1,0:T(8,128)S(1)}, u32[]{:S(2)}, u32[]{:S(2)}) async-start(f32[8,8,8,128]{3,2,1,0:T(8,128)} %get-tuple-element.58), calls=%async_computation.3 | async-start | bytes 524288 | tf_op jit(solution)/shard_map/all_to_all | solution.py:869
  67.8 4.3 %collective-permute-start.7 = (f32[1,4,4,8,128]{4,3,2,1,0:T(8,128)S(1)}, f32[1,4,4,8,128]{4,3,2,1,0:T(8,128)S(1)}, u32[]{:S(2)}, u32[]{:S(2)}) collective-permute-start(f32[1,4,4,8,128]{4,3,2,1,0:T(8,128)S(1)} %get-tuple-element.50), channel_id=1, source_target_pairs={{0,8},{8,0},{16,24},{24,16},{1,9},{9,1},{17,25},{25,17},{2,10},{10... | collective-permute-start | bytes 196616 | tf_op jit(solution)/shard_map/ppermute | solution.py:84
  68.9 6.1 %collective-permute-start.8 = (f32[1,4,4,8,128]{4,3,2,1,0:T(8,128)S(1)}, f32[1,4,4,8,128]{4,3,2,1,0:T(8,128)S(1)}, u32[]{:S(2)}, u32[]{:S(2)}) collective-permute-start(f32[1,4,4,8,128]{4,3,2,1,0:T(8,128)S(1)} %get-tuple-element.51), channel_id=1, source_target_pairs={{0,24},{8,16},{16,8},{24,0},{1,25},{9,17},{17,9},{25,1},{2,26},{10... | collective-permute-start | bytes 196616 | tf_op jit(solution)/shard_map/ppermute | solution.py:85
  75.0 5.5 %collective-permute-start.10 = (f32[1,12,8,128]{3,2,1,0:T(8,128)S(1)}, f32[1,12,8,128]{3,2,1,0:T(8,128)S(1)}, u32[]{:S(2)}, u32[]{:S(2)}) collective-permute-start(f32[1,12,8,128]{3,2,1,0:T(8,128)S(1)} %get-tuple-element.53), channel_id=1, source_target_pairs={{0,6},{2,4},{4,2},{6,0},{1,7},{3,5},{5,3},{7,1},{8,14},{10,12},{12... | collective-permute-start | bytes 147464 | tf_op jit(solution)/shard_map/ppermute | solution.py:85
  75.2 5.4 %collective-permute-start.9 = (f32[1,12,8,128]{3,2,1,0:T(8,128)S(1)}, f32[1,12,8,128]{3,2,1,0:T(8,128)S(1)}, u32[]{:S(2)}, u32[]{:S(2)}) collective-permute-start(f32[1,12,8,128]{3,2,1,0:T(8,128)S(1)} %get-tuple-element.52), channel_id=1, source_target_pairs={{0,2},{2,0},{4,6},{6,4},{1,3},{3,1},{5,7},{7,5},{8,10},{10,8},{12,... | collective-permute-start | bytes 147464 | tf_op jit(solution)/shard_map/ppermute | solution.py:84
  79.0 6.0 %collective-permute-start.12 = (f32[16,8,128]{2,1,0:T(8,128)S(1)}, f32[16,8,128]{2,1,0:T(8,128)S(1)}, u32[]{:S(2)}, u32[]{:S(2)}) collective-permute-start(f32[16,8,128]{2,1,0:T(8,128)S(1)} %get-tuple-element.60), channel_id=1, source_target_pairs={{0,8},{8,0},{16,24},{24,16},{1,9},{9,1},{17,25},{25,17},{2,10},{10... | collective-permute-start | bytes 196616 | tf_op jit(solution)/shard_map/ppermute | solution.py:84
  79.6 6.1 %collective-permute-start.13 = (f32[16,8,128]{2,1,0:T(8,128)S(1)}, f32[16,8,128]{2,1,0:T(8,128)S(1)}, u32[]{:S(2)}, u32[]{:S(2)}) collective-permute-start(f32[16,8,128]{2,1,0:T(8,128)S(1)} %get-tuple-element.61), channel_id=1, source_target_pairs={{0,24},{8,16},{16,8},{24,0},{1,25},{9,17},{17,9},{25,1},{2,26},{10... | collective-permute-start | bytes 196616 | tf_op jit(solution)/shard_map/ppermute | solution.py:85
  80.8 3.8 %collective-permute-start.11 = (f32[1,4,8,128]{3,2,1,0:T(8,128)S(1)}, f32[1,4,8,128]{3,2,1,0:T(8,128)S(1)}, u32[]{:S(2)}, u32[]{:S(2)}) collective-permute-start(f32[1,4,8,128]{3,2,1,0:T(8,128)S(1)} %shard_map.111), channel_id=1, source_target_pairs={{0,1},{1,0},{2,3},{3,2},{4,5},{5,4},{6,7},{7,6},{8,9},{9,8},{10,11... | collective-permute-start | bytes 49160 | tf_op jit(solution)/shard_map/ppermute | solution.py:84
  97.5 3.6 %collective-permute-start.14 = (f32[8,128]{1,0:T(8,128)S(1)}, f32[8,128]{1,0:T(8,128)S(1)}, u32[]{:S(2)}, u32[]{:S(2)}) collective-permute-start(f32[8,128]{1,0:T(8,128)S(1)} %shard_map.117), channel_id=1, source_target_pairs={{0,8},{8,0},{16,24},{24,16},{1,9},{9,1},{17,25},{25,17},{2,10},{10... | collective-permute-start | bytes 12296 | tf_op jit(solution)/shard_map/ppermute | solution.py:1007
  101.1 4.5 %collective-permute-start.15 = (f32[8,128]{1,0:T(8,128)S(1)}, f32[8,128]{1,0:T(8,128)S(1)}, u32[]{:S(2)}, u32[]{:S(2)}) collective-permute-start(f32[8,128]{1,0:T(8,128)S(1)} %add.6), channel_id=1, source_target_pairs={{0,16},{8,24},{16,0},{24,8},{1,17},{9,25},{17,1},{25,9},{2,18},{10... | collective-permute-start | bytes 12296 | tf_op jit(solution)/shard_map/ppermute | solution.py:1007

commit v5 on v4

--- a/solution.py
+++ b/solution.py
@@ -408,13 +408,16 @@
     def body(*refs):
         if first:
             got, *stored = refs[:4]
-            ret, state_out, squares, table, kept_out, rate_out = refs[4:10]
-            packed, other, state, ghosts, kept, rate, homes, moved, copied, counts, sems = refs[10:21]
-            old = refs[21:]
+            ret, state_out, squares, table_out, kept_out, rate_out = refs[4:10]
+            packed, other, state, ghosts, kept, rate, homes, table, moved = refs[10:19]
+            copied, counts, sems = refs[19:22]
+            old = refs[22:]
         else:
-            table, got, *stored = refs[:5]
+            table_in, got, *stored = refs[:5]
             ret, state_out, squares = refs[5:8]
-            packed, other, state, ghosts, kept, rate, homes, moved = refs[8:]
+            packed, other, state, ghosts, kept, rate, homes, table, moved = refs[8:]
+            tables = [pltpu.make_async_copy(table_in, table, moved.at[5])]
+            fetch(tables)
             old = (other, kept, rate)
         loads = [
             pltpu.make_async_copy(source, goal, moved.at[index])
@@ -441,6 +444,9 @@
                     table[home, COLS * slot + 4] = place
                     counts[owner] = place + 1
 
+        if not first:
+            arrive(tables)
+
         def found(count, home, slot):
             packed[count] = got[home, 0:4]
             homes[count, 0] = jnp.int32(home)
@@ -468,6 +474,7 @@
 
         if first:
             lax.fori_loop(0, slots, convert, 0)
+            saves.append(pltpu.make_async_copy(table, table_out, moved.at[5]))
             saves.append(pltpu.make_async_copy(kept, kept_out, moved.at[6]))
             saves.append(pltpu.make_async_copy(rate, rate_out, moved.at[7]))
             fetch(saves)
@@ -567,7 +574,8 @@
 def last_body(dims):
     group, slots, size_z = dims
 
-    def body(table, got, old_state, goal, packed, fresh, state, result, sems):
+    def body(table_in, got, old_state, goal, packed, fresh, state, result, table, sems):
+        tables = fetch([pltpu.make_async_copy(table_in, table, sems.at[2])])
         loads = [pltpu.make_async_copy(old_state, state, sems.at[0])]
         fetch(loads)
         rank = lax.axis_index("gy") * size_z + lax.axis_index("gz")
@@ -576,6 +584,7 @@
         def found(count, home, slot):
             packed[count] = got[home, 0:4]
 
+        arrive(tables)
         live = assign(rank, table, group, slots, found)
         unpack(packed, fresh, slots)
         arrive(loads)
@@ -607,12 +616,14 @@
     ex, nt, group, slots, size_y, size_z, nby, nbz = dims
     tiles = FOOT // SUB
 
-    def body(table, got, added, side_a, side_b):
+    def body(table_in, got, added, side_a, side_b, table, sem):
+        tables = fetch([pltpu.make_async_copy(table_in, table, sem)])
         pos = place_of()
         odd = pos[0] % 2 == 1
         rank = pos[1] * size_z + pos[2]
         lanes, rows = lane_id(), sub_id()
         added[...] = jnp.zeros(added.shape, F32)
+        arrive(tables)
 
         def own(slot, carry):
             owner = table[rank, COLS * slot]
@@ -725,14 +736,15 @@
     span = ex + 2 * WIDE
     rows_all = SUB * (nt + 1)
 
-    def body(table, wide, rate, source, added, xa, xb, *refs):
+    def body(table_in, wide, rate, source, added, xa, xb, *refs):
         pos = place_of()
         sq_in, refs = refs[: 1 if more else 2], refs[1 if more else 2 :]
         if more:
             potential, send, squares, side_a, side_b = refs[:5]
         else:
             potential, send, squares = refs[:3]
-        comp, one, two = refs[-3:]
+        comp, one, two, table, sem = refs[-5:]
+        tables = fetch([pltpu.make_async_copy(table_in, table, sem)])
         odd = pos[0] % 2 == 1
         rank = pos[1] * size_z + pos[2]
         lanes = lane_id()
@@ -816,6 +828,7 @@
             send[target, 0:4] = jnp.zeros((4, SUB, LANES), F32)
             if not more:
                 send[target, 4] = squares[...]
+        arrive(tables)
         for slot in range(slots):
             target = table[rank, COLS * slot]
 
@@ -932,7 +945,8 @@
     ghost = pltpu.VMEM((slots, FOOT, SUB, LANES), F32)
     packs = pltpu.VMEM((slots, 4, SUB, LANES), F32)
     box_scratch = [packs, whole, whole, ghost, whole, whole]
-    box_scratch += [pltpu.SMEM((slots, 3), jnp.int32), pltpu.SemaphoreType.DMA((8,))]
+    routes = pltpu.SMEM((group, COLS * slots), jnp.int32)
+    box_scratch += [pltpu.SMEM((slots, 3), jnp.int32), routes, pltpu.SemaphoreType.DMA((8,))]
     box_outs = [
         (VMEM, out(group, 4 + slots, SUB, LANES)),
         (HBM, out(*box_shape)),
@@ -948,7 +962,7 @@
                 body,
                 [(VMEM, got)] + [(HBM, value) for value in (f_source, f_shift, f_start)],
                 box_outs
-                + [(SMEM, out(group, COLS * slots, dtype=jnp.int32))]
+                + [(HBM, out(group, COLS * slots, dtype=jnp.int32))]
                 + [(HBM, out(*box_shape))] * 2,
                 box_scratch
                 + [
@@ -961,7 +975,7 @@
         else:
             ret, state, squares = call(
                 body,
-                [(SMEM, table), (VMEM, got)]
+                [(HBM, table), (VMEM, got)]
                 + [(HBM, value) for value in (state, kept, f_rate)],
                 box_outs,
                 box_scratch,
@@ -970,15 +984,16 @@
         units = (WIDE - 1) * (nt + 1) + 1
         added, side_a, side_b = call(
             place_body((ex, nt, group, slots, size_y, size_z, nby, nbz)),
-            [(SMEM, table), (VMEM, back)],
+            [(HBM, table), (VMEM, back)],
             [(VMEM, out(ex, 2, nt + 1, SUB, LANES))] + [(VMEM, out(units, SUB, LANES))] * 2,
+            [routes, pltpu.SemaphoreType.DMA],
         )
         xa, xb = swap("gx", side_a, side_b)
         more = cycle < CYCLES - 1
         wide_shape = (span, 2, SUB * (nt + 1), LANES)
         result = call(
             coarse_body((ex, nt, group, slots, size_z), more),
-            [(SMEM, table)]
+            [(HBM, table)]
             + [(VMEM, v) for v in (wide, rate, source_wide, added, xa, xb, squares, *norms)],
             [
                 (VMEM, out(ex, nt, SUB, LANES)),
@@ -986,7 +1001,7 @@
                 (VMEM, out(SUB, LANES)),
             ]
             + [(VMEM, out(1, WIDE, nt, SUB, LANES))] * (2 if more else 0),
-            [pltpu.VMEM(wide_shape, F32)] * 3,
+            [pltpu.VMEM(wide_shape, F32)] * 3 + [routes, pltpu.SemaphoreType.DMA],
         )
         potential, send = result[:2]
         norms.append(result[2])
@@ -996,9 +1011,9 @@
     (total,) = call(norm_body(group), [(VMEM, got)], [(VMEM, out(SUB, LANES))])
     (values,) = call(
         last_body((group, slots, size_z)),
-        [(SMEM, table), (VMEM, got), (HBM, state)],
+        [(HBM, table), (VMEM, got), (HBM, state)],
         [(HBM, out(slots * fine // LANES, LANES))],
-        [packs, ghost, whole, flat, pltpu.SemaphoreType.DMA((2,))],
+        [packs, ghost, whole, flat, routes, pltpu.SemaphoreType.DMA((3,))],
     )
     cells = float(ex * ey * ez * size_x * size_y * size_z)
     bit = 1

time: 107 us -> 106 us (level)
  Pallas kernels: 37.4 us -> 36.3 us
    pallas_call x15, Pallas kernels: 37.4 us -> 36.3 us  [call(): pl.pallas_call(body, in_specs=[spec for spec, _ in ins], out_specs=[spec...]
where the time goes in v5:
time: 106 us; the launch traced here: 105 us
  Pallas kernels  36.3 us (34%)
  starting transfers between devices  32.5 us (31%)
  waiting for transfers between devices  19.3 us (18%)
  blocking collectives  15.5 us (15%)
    pallas_call x15, Pallas kernels, call(): pl.pallas_call(body, in_specs=[spec for spec, _ in ins], out_specs=[spec...  36.3 us
    all_to_all x2, blocking collectives, exchange(): lax.all_to_all(value, GROUP_AXES, split_axis=0, concat_axis=0, tiled=True)  15.5 us
    all_to_all x3, starting transfers between devices, exchange(): lax.all_to_all(value, GROUP_AXES, split_axis=0, concat_axis=0, tiled=True)  12 us
    ppermute x8, starting transfers between devices, swap(): got_a = lax.ppermute(first, axis, pairs_a)  10.2 us
    ppermute x6, starting transfers between devices, swap(): got_b = lax.ppermute(second, axis, pairs_b) if count > 2 else got_a  8.42 us
    ppermute x8, waiting for transfers between devices, swap(): got_a = lax.ppermute(first, axis, pairs_a)  7.69 us
    all_to_all x3, waiting for transfers between devices, exchange(): lax.all_to_all(value, GROUP_AXES, split_axis=0, concat_axis=0, tiled=True)  4.42 us
    ppermute x2, waiting for transfers between devices, work(): total = total + lax.ppermute(total, 'gx', pairs)  3.72 us
  transfers between devices with their start and end apart: 19, of which 9 were waited for; matrix products, arithmetic and copies ran while one was open for 0% of the time, Pallas kernels for 19%

profile of v5, /device:TPU:0, one launch (start us, length us, event | category | flops | bytes accessed | tf_op | source)
XLA Modules:
  0.0 105.1 jit_solution(16919205701674896777)
XLA Ops:
  0.6 2.1 %shard_map.103 = (f32[8,5,8,128]{3,2,1,0:T(8,128)}, f32[3,4,4,8,128]{4,3,2,1,0:T(8,128)S(1)}, f32[3,4,4,8,128]{4,3,2,1,0:T(8,128)S(1)}) custom-call(s32[3,1,4]{2,1,0:T(1,128)} %bitcast.41, s32[1,4]{1,0:T(1,128)} %owner_in.1, f32[16,4,8,128]{3,2,1,0:T(8,128)} %bitcast.25, f32[16,4,8,128]{3,2,1,0:T(8,128)} %bitcast.29, f32[16,4,8,128]{3,2,1,0:T(8,128)} %bitcast.33), custom_call_target="tpu_custom_call" | custom-call | tf_op jit(solution)/shard_map/pallas_call | solution.py:38
  2.8 5.0 %all-to-all-start = ((f32[8,5,8,128]{3,2,1,0:T(8,128)}), f32[8,5,8,128]{3,2,1,0:T(8,128)S(1)}, u32[]{:S(2)}, u32[]{:S(2)}) async-start(f32[8,5,8,128]{3,2,1,0:T(8,128)} %get-tuple-element.35), calls=%async_computation | async-start | bytes 327680 | tf_op jit(solution)/shard_map/all_to_all | solution.py:882
  7.8 1.8 %collective-permute-start = (f32[3,4,4,8,128]{4,3,2,1,0:T(8,128)S(1)}, f32[3,4,4,8,128]{4,3,2,1,0:T(8,128)S(1)}, u32[]{:S(2)}, u32[]{:S(2)}) collective-permute-start(f32[3,4,4,8,128]{4,3,2,1,0:T(8,128)S(1)} %get-tuple-element.37), channel_id=1, source_target_pairs={{0,8},{8,0},{16,24},{24,16},{1,9},{9,1},{17,25},{25,17},{2,10},{10... | collective-permute-start | bytes 589832 | tf_op jit(solution)/shard_map/ppermute | solution.py:84
  9.6 2.3 %collective-permute-start.1 = (f32[3,4,4,8,128]{4,3,2,1,0:T(8,128)S(1)}, f32[3,4,4,8,128]{4,3,2,1,0:T(8,128)S(1)}, u32[]{:S(2)}, u32[]{:S(2)}) collective-permute-start(f32[3,4,4,8,128]{4,3,2,1,0:T(8,128)S(1)} %get-tuple-element.38), channel_id=1, source_target_pairs={{0,24},{8,16},{16,8},{24,0},{1,25},{9,17},{17,9},{25,1},{2,26},{10... | collective-permute-start | bytes 589832 | tf_op jit(solution)/shard_map/ppermute | solution.py:85
  11.8 1.4 %all-to-all-done.refs_0_ = f32[8,5,8,128]{3,2,1,0:T(8,128)S(1)} async-done(((f32[8,5,8,128]{3,2,1,0:T(8,128)}), f32[8,5,8,128]{3,2,1,0:T(8,128)S(1)}, u32[]{:S(2)}, u32[]{:S(2)}) %all-to-all-start) | async-done | bytes 163872 | tf_op jit(solution)/shard_map/all_to_all | solution.py:882
  13.2 8.5 %shard_map.104 = (f32[8,8,8,128]{3,2,1,0:T(8,128)}, f32[4,32,8,128]{3,2,1,0:T(8,128)}, f32[8,128]{1,0:T(8,128)S(1)}, s32[8,32]{1,0:T(8,128)}, f32[4,32,8,128]{3,2,1,0:T(8,128)}, /*index=5*/f32[4,32,8,128]{3,2,1,0:T(8,128)}) custom-call(f32[8,5,8,128]{3,2,1,0:T(8,128)S(1)} %all-to-all-done.refs_0_, f32[1024,128]{1,0:T(8,128)} %bitcast.38, ...), custom_call_target="tpu_custom_call" | custom-call | tf_op jit(solution)/shard_map/pallas_call | solution.py:38
  21.7 3.4 %all-to-all-start.1 = ((f32[8,8,8,128]{3,2,1,0:T(8,128)}), f32[8,8,8,128]{3,2,1,0:T(8,128)S(1)}, u32[]{:S(2)}, u32[]{:S(2)}) async-start(f32[8,8,8,128]{3,2,1,0:T(8,128)} %get-tuple-element.44), calls=%async_computation.1 | async-start | bytes 524288 | tf_op jit(solution)/shard_map/all_to_all | solution.py:882
  25.1 0.0 collective-permute-done.refs_3_
  25.1 0.0 collective-permute-done.1.refs_4_
  25.1 1.1 %shard_map.105 = (f32[3,12,8,128]{3,2,1,0:T(8,128)S(1)}, f32[3,12,8,128]{3,2,1,0:T(8,128)S(1)}) custom-call(f32[16,4,8,128]{3,2,1,0:T(8,128)} %bitcast.26, f32[16,4,8,128]{3,2,1,0:T(8,128)} %bitcast.30, f32[16,4,8,128]{3,2,1,0:T(8,128)} %bitcast.34, f32[3,4,4,8,128]{4,3,2,1,0:T(8,128)S(1)} %collective-permute-done.refs_3_, ...), custom_call_target="tpu_custom_call" | custom-call | tf_op jit(solution)/shard_map/pallas_call | solution.py:38
  26.2 0.5 collective-permute-start.2
  26.7 1.6 %collective-permute-start.3 = (f32[3,12,8,128]{3,2,1,0:T(8,128)S(1)}, f32[3,12,8,128]{3,2,1,0:T(8,128)S(1)}, u32[]{:S(2)}, u32[]{:S(2)}) collective-permute-start(f32[3,12,8,128]{3,2,1,0:T(8,128)S(1)} %get-tuple-element.40), channel_id=1, source_target_pairs={{0,6},{2,4},{4,2},{6,0},{1,7},{3,5},{5,3},{7,1},{8,14},{10,12},{12... | collective-permute-start | bytes 442376 | tf_op jit(solution)/shard_map/ppermute | solution.py:85
  28.3 3.1 %all-to-all-done.1.got = f32[8,8,8,128]{3,2,1,0:T(8,128)S(1)} async-done(((f32[8,8,8,128]{3,2,1,0:T(8,128)}), f32[8,8,8,128]{3,2,1,0:T(8,128)S(1)}, u32[]{:S(2)}, u32[]{:S(2)}) %all-to-all-start.1) | async-done | bytes 262176 | tf_op jit(solution)/shard_map/all_to_all | solution.py:882
  31.4 2.2 %shard_map.108 = (f32[16,2,5,8,128]{4,3,2,1,0:T(8,128)S(1)}, f32[16,8,128]{2,1,0:T(8,128)S(1)}, f32[16,8,128]{2,1,0:T(8,128)S(1)}) custom-call(s32[8,32]{1,0:T(8,128)} %get-tuple-element.36.table_in.refs_0_, f32[8,8,8,128]{3,2,1,0:T(8,128)S(1)} %all-to-all-done.1.got), custom_call_target="tpu_custom_call" | custom-call | tf_op jit(solution)/shard_map/pallas_call | solution.py:38
  33.6 1.8 %collective-permute-start.5 = (f32[16,8,128]{2,1,0:T(8,128)S(1)}, f32[16,8,128]{2,1,0:T(8,128)S(1)}, u32[]{:S(2)}, u32[]{:S(2)}) collective-permute-start(f32[16,8,128]{2,1,0:T(8,128)S(1)} %get-tuple-element.46), channel_id=1, source_target_pairs={{0,8},{8,0},{16,24},{24,16},{1,9},{9,1},{17,25},{25,17},{2,10},{10... | collective-permute-start | bytes 196616 | tf_op jit(solution)/shard_map/ppermute | solution.py:84
  35.4 2.6 %collective-permute-start.6 = (f32[16,8,128]{2,1,0:T(8,128)S(1)}, f32[16,8,128]{2,1,0:T(8,128)S(1)}, u32[]{:S(2)}, u32[]{:S(2)}) collective-permute-start(f32[16,8,128]{2,1,0:T(8,128)S(1)} %get-tuple-element.47), channel_id=1, source_target_pairs={{0,24},{8,16},{16,8},{24,0},{1,25},{9,17},{17,9},{25,1},{2,26},{10... | collective-permute-start | bytes 196616 | tf_op jit(solution)/shard_map/ppermute | solution.py:85
  38.0 0.0 collective-permute-done.2.refs_5_
  38.0 0.0 collective-permute-done.3.refs_6_
  38.0 1.6 %shard_map.106 = f32[3,4,8,128]{3,2,1,0:T(8,128)S(1)} custom-call(f32[16,4,8,128]{3,2,1,0:T(8,128)} %bitcast.27, f32[16,4,8,128]{3,2,1,0:T(8,128)} %bitcast.31, f32[16,4,8,128]{3,2,1,0:T(8,128)} %bitcast.35, f32[3,4,4,8,128]{4,3,2,1,0:T(8,128)S(1)} %collective-permute-done.refs_3_, f32[3,4,4,8,128]{4,3,2,1,0:T(8,128)S(1)} %collective-permute-done.1.refs_4_, ...), custom_call_target="tpu_custom_call" | custom-call | tf_op jit(solution)/shard_map/pallas_call | solution.py:38
  39.7 1.3 %collective-permute-start.4 = (f32[3,4,8,128]{3,2,1,0:T(8,128)S(1)}, f32[3,4,8,128]{3,2,1,0:T(8,128)S(1)}, u32[]{:S(2)}, u32[]{:S(2)}) collective-permute-start(f32[3,4,8,128]{3,2,1,0:T(8,128)S(1)} %shard_map.106), channel_id=1, source_target_pairs={{0,1},{1,0},{2,3},{3,2},{4,5},{5,4},{6,7},{7,6},{8,9},{9,8},{10,11... | collective-permute-start | bytes 147464 | tf_op jit(solution)/shard_map/ppermute | solution.py:84
  41.0 2.8 %collective-permute-done.4.refs_7_ = f32[3,4,8,128]{3,2,1,0:T(8,128)S(1)} collective-permute-done((f32[3,4,8,128]{3,2,1,0:T(8,128)S(1)}, f32[3,4,8,128]{3,2,1,0:T(8,128)S(1)}, u32[]{:S(2)}, u32[]{:S(2)}) %collective-permute-start.4) | collective-permute-done | bytes 49184 | tf_op jit(solution)/shard_map/ppermute | solution.py:84
  43.8 1.6 %shard_map.107 = (f32[24,2,40,128]{3,2,1,0:T(8,128)S(1)}, f32[24,2,40,128]{3,2,1,0:T(8,128)S(1)}, f32[24,2,40,128]{3,2,1,0:T(8,128)S(1)}) custom-call(f32[16,4,8,128]{3,2,1,0:T(8,128)} %bitcast.28, f32[16,4,8,128]{3,2,1,0:T(8,128)} %bitcast.32, f32[16,4,8,128]{3,2,1,0:T(8,128)} %bitcast.36, f32[3,4,4,8,128]{4,3,2,1,0:T(8,128)S(1)} %collective-permute-done.refs_3_, ...), custom_call_target="tpu_custom_call" | custom-call | tf_op jit(solution)/shard_map/pallas_call | solution.py:38
  45.4 0.0 collective-permute-done.5.xa
  45.4 0.0 collective-permute-done.6.xb
  45.5 2.4 %shard_map.109 = (f32[16,4,8,128]{3,2,1,0:T(8,128)S(1)}, f32[8,4,8,128]{3,2,1,0:T(8,128)S(1)}, f32[8,128]{1,0:T(8,128)S(1)}, f32[1,4,4,8,128]{4,3,2,1,0:T(8,128)S(1)}, f32[1,4,4,8,128]{4,3,2,1,0:T(8,128)S(1)}) custom-call(s32[8,32]{1,0:T(8,128)} %get-tuple-element.36.table_in.refs_0_, f32[24,2,40,128]{3,2,1,0:T(8,128)S(1)} %get-tuple-element.41.wide, ...), custom_call_target="tpu_custom_call" | custom-call | tf_op jit(solution)/shard_map/pallas_call | solution.py:38
  47.9 7.5 %all_to_all.25.refs_1_ = f32[8,4,8,128]{3,2,1,0:T(8,128)S(1)} all-to-all(f32[8,4,8,128]{3,2,1,0:T(8,128)S(1)} %get-tuple-element.54), channel_id=1, replica_groups=mesh['gx'=4,'gy'=4,'gz'=2] {'gy','gz'}, dimensions={0} | all-to-all | bytes 262144 | tf_op jit(solution)/shard_map/all_to_all | solution.py:882
  55.4 8.1 %shard_map.113 = (f32[8,8,8,128]{3,2,1,0:T(8,128)}, f32[4,32,8,128]{3,2,1,0:T(8,128)}, f32[8,128]{1,0:T(8,128)S(1)}) custom-call(s32[8,32]{1,0:T(8,128)} %get-tuple-element.36.table_in.refs_0_, f32[8,4,8,128]{3,2,1,0:T(8,128)S(1)} %all_to_all.25.refs_1_, f32[4,32,8,128]{3,2,1,0:T(8,128)} %get-tuple-element.55.refs_2_, ...), custom_call_target="tpu_custom_call" | custom-call | tf_op jit(solution)/shard_map/pallas_call | solution.py:38
  63.5 3.6 %all-to-all-start.3 = ((f32[8,8,8,128]{3,2,1,0:T(8,128)}), f32[8,8,8,128]{3,2,1,0:T(8,128)S(1)}, u32[]{:S(2)}, u32[]{:S(2)}) async-start(f32[8,8,8,128]{3,2,1,0:T(8,128)} %get-tuple-element.58), calls=%async_computation.3 | async-start | bytes 524288 | tf_op jit(solution)/shard_map/all_to_all | solution.py:882
  67.1 1.1 %collective-permute-start.7 = (f32[1,4,4,8,128]{4,3,2,1,0:T(8,128)S(1)}, f32[1,4,4,8,128]{4,3,2,1,0:T(8,128)S(1)}, u32[]{:S(2)}, u32[]{:S(2)}) collective-permute-start(f32[1,4,4,8,128]{4,3,2,1,0:T(8,128)S(1)} %get-tuple-element.50), channel_id=1, source_target_pairs={{0,8},{8,0},{16,24},{24,16},{1,9},{9,1},{17,25},{25,17},{2,10},{10... | collective-permute-start | bytes 196616 | tf_op jit(solution)/shard_map/ppermute | solution.py:84
  68.2 0.8 collective-permute-start.8
  68.9 2.5 %collective-permute-done.7.refs_1_ = f32[1,4,4,8,128]{4,3,2,1,0:T(8,128)S(1)} collective-permute-done((f32[1,4,4,8,128]{4,3,2,1,0:T(8,128)S(1)}, f32[1,4,4,8,128]{4,3,2,1,0:T(8,128)S(1)}, u32[]{:S(2)}, u32[]{:S(2)}) %collective-permute-start.7) | collective-permute-done | bytes 65568 | tf_op jit(solution)/shard_map/ppermute | solution.py:84
  71.4 2.8 %collective-permute-done.8.refs_2_ = f32[1,4,4,8,128]{4,3,2,1,0:T(8,128)S(1)} collective-permute-done((f32[1,4,4,8,128]{4,3,2,1,0:T(8,128)S(1)}, f32[1,4,4,8,128]{4,3,2,1,0:T(8,128)S(1)}, u32[]{:S(2)}, u32[]{:S(2)}) %collective-permute-start.8) | collective-permute-done | bytes 65568 | tf_op jit(solution)/shard_map/ppermute | solution.py:85
  74.2 0.1 shard_map.110
  74.3 0.2 collective-permute-start.10
  74.5 1.7 %collective-permute-start.9 = (f32[1,12,8,128]{3,2,1,0:T(8,128)S(1)}, f32[1,12,8,128]{3,2,1,0:T(8,128)S(1)}, u32[]{:S(2)}, u32[]{:S(2)}) collective-permute-start(f32[1,12,8,128]{3,2,1,0:T(8,128)S(1)} %get-tuple-element.52), channel_id=1, source_target_pairs={{0,2},{2,0},{4,6},{6,4},{1,3},{3,1},{5,7},{7,5},{8,10},{10,8},{12,... | collective-permute-start | bytes 147464 | tf_op jit(solution)/shard_map/ppermute | solution.py:84
  76.2 0.0 all-to-all-done.3.got
  76.2 2.2 %shard_map.114 = (f32[16,2,5,8,128]{4,3,2,1,0:T(8,128)S(1)}, f32[16,8,128]{2,1,0:T(8,128)S(1)}, f32[16,8,128]{2,1,0:T(8,128)S(1)}) custom-call(s32[8,32]{1,0:T(8,128)} %get-tuple-element.36.table_in.refs_0_, f32[8,8,8,128]{3,2,1,0:T(8,128)S(1)} %all-to-all-done.3.got), custom_call_target="tpu_custom_call" | custom-call | tf_op jit(solution)/shard_map/pallas_call | solution.py:38
  78.4 0.6 collective-permute-start.12
  79.0 0.9 collective-permute-start.13
  80.0 0.0 collective-permute-done.10.refs_4_
  80.0 0.0 collective-permute-done.9.refs_3_
  80.0 0.3 shard_map.111
  80.3 1.4 %collective-permute-start.11 = (f32[1,4,8,128]{3,2,1,0:T(8,128)S(1)}, f32[1,4,8,128]{3,2,1,0:T(8,128)S(1)}, u32[]{:S(2)}, u32[]{:S(2)}) collective-permute-start(f32[1,4,8,128]{3,2,1,0:T(8,128)S(1)} %shard_map.111), channel_id=1, source_target_pairs={{0,1},{1,0},{2,3},{3,2},{4,5},{5,4},{6,7},{7,6},{8,9},{9,8},{10,11... | collective-permute-start | bytes 49160 | tf_op jit(solution)/shard_map/ppermute | solution.py:84
  81.7 2.4 %collective-permute-done.11.refs_5_ = f32[1,4,8,128]{3,2,1,0:T(8,128)S(1)} collective-permute-done((f32[1,4,8,128]{3,2,1,0:T(8,128)S(1)}, f32[1,4,8,128]{3,2,1,0:T(8,128)S(1)}, u32[]{:S(2)}, u32[]{:S(2)}) %collective-permute-start.11) | collective-permute-done | bytes 16416 | tf_op jit(solution)/shard_map/ppermute | solution.py:84
  84.1 0.3 shard_map.112.wide
  84.3 0.0 collective-permute-done.12.xa
  84.4 0.7 collective-permute-done.13.xb
  85.1 3.3 %shard_map.115 = (f32[16,4,8,128]{3,2,1,0:T(8,128)}, f32[8,5,8,128]{3,2,1,0:T(8,128)S(1)}, f32[8,128]{1,0:T(8,128)}) custom-call(s32[8,32]{1,0:T(8,128)} %get-tuple-element.36.table_in.refs_0_, f32[24,2,40,128]{3,2,1,0:T(8,128)S(1)} %shard_map.112.wide, f32[24,2,40,128]{3,2,1,0:T(8,128)S(1)} %get-tuple-element.42.rate, ...), custom_call_target="tpu_custom_call" | custom-call | tf_op jit(solution)/shard_map/pallas_call | solution.py:38
  88.3 8.0 %all_to_all.26.got = f32[8,5,8,128]{3,2,1,0:T(8,128)S(1)} all-to-all(f32[8,5,8,128]{3,2,1,0:T(8,128)S(1)} %get-tuple-element.65), channel_id=1, replica_groups=mesh['gx'=4,'gy'=4,'gz'=2] {'gy','gz'}, dimensions={0} | all-to-all | bytes 327680 | tf_op jit(solution)/shard_map/all_to_all | solution.py:882
  96.3 0.7 collective-permute-start.14
  97.1 2.9 %collective-permute-done.14 = f32[8,128]{1,0:T(8,128)S(1)} collective-permute-done((f32[8,128]{1,0:T(8,128)S(1)}, f32[8,128]{1,0:T(8,128)S(1)}, u32[]{:S(2)}, u32[]{:S(2)}) %collective-permute-start.14) | collective-permute-done | bytes 4128 | tf_op jit(solution)/shard_map/ppermute | solution.py:1022
  99.9 1.1 %collective-permute-start.15 = (f32[8,128]{1,0:T(8,128)S(1)}, f32[8,128]{1,0:T(8,128)S(1)}, u32[]{:S(2)}, u32[]{:S(2)}) collective-permute-start(f32[8,128]{1,0:T(8,128)S(1)} %add.6), channel_id=1, source_target_pairs={{0,16},{8,24},{16,0},{24,8},{1,17},{9,25},{17,1},{25,9},{2,18},{10... | collective-permute-start | bytes 12296 | tf_op jit(solution)/shard_map/ppermute | solution.py:1022
  101.0 2.6 %shard_map.116 = f32[1024,128]{1,0:T(8,128)} custom-call(s32[8,32]{1,0:T(8,128)} %get-tuple-element.36.table_in.refs_0_, f32[8,5,8,128]{3,2,1,0:T(8,128)S(1)} %all_to_all.26.got, f32[4,32,8,128]{3,2,1,0:T(8,128)} %get-tuple-element.66.old_state), custom_call_target="tpu_custom_call" | custom-call | tf_op jit(solution)/shard_map/pallas_call | solution.py:38
  103.6 0.8 collective-permute-done.15
  104.5 0.1 slice_reduce_fusion
  104.6 0.5 multiply_sqrt_fusion
  (3 shorter events, 0.0 us)
Async XLA Ops:
  2.8 10.4 %all-to-all-start = ((f32[8,5,8,128]{3,2,1,0:T(8,128)}), f32[8,5,8,128]{3,2,1,0:T(8,128)S(1)}, u32[]{:S(2)}, u32[]{:S(2)}) async-start(f32[8,5,8,128]{3,2,1,0:T(8,128)} %get-tuple-element.35), calls=%async_computation | async-start | bytes 327680 | tf_op jit(solution)/shard_map/all_to_all | solution.py:882
  7.8 17.3 %collective-permute-start = (f32[3,4,4,8,128]{4,3,2,1,0:T(8,128)S(1)}, f32[3,4,4,8,128]{4,3,2,1,0:T(8,128)S(1)}, u32[]{:S(2)}, u32[]{:S(2)}) collective-permute-start(f32[3,4,4,8,128]{4,3,2,1,0:T(8,128)S(1)} %get-tuple-element.37), channel_id=1, source_target_pairs={{0,8},{8,0},{16,24},{24,16},{1,9},{9,1},{17,25},{25,17},{2,10},{10... | collective-permute-start | bytes 589832 | tf_op jit(solution)/shard_map/ppermute | solution.py:84
  9.6 15.6 %collective-permute-start.1 = (f32[3,4,4,8,128]{4,3,2,1,0:T(8,128)S(1)}, f32[3,4,4,8,128]{4,3,2,1,0:T(8,128)S(1)}, u32[]{:S(2)}, u32[]{:S(2)}) collective-permute-start(f32[3,4,4,8,128]{4,3,2,1,0:T(8,128)S(1)} %get-tuple-element.38), channel_id=1, source_target_pairs={{0,24},{8,16},{16,8},{24,0},{1,25},{9,17},{17,9},{25,1},{2,26},{10... | collective-permute-start | bytes 589832 | tf_op jit(solution)/shard_map/ppermute | solution.py:85
  21.7 9.7 %all-to-all-start.1 = ((f32[8,8,8,128]{3,2,1,0:T(8,128)}), f32[8,8,8,128]{3,2,1,0:T(8,128)S(1)}, u32[]{:S(2)}, u32[]{:S(2)}) async-start(f32[8,8,8,128]{3,2,1,0:T(8,128)} %get-tuple-element.44), calls=%async_computation.1 | async-start | bytes 524288 | tf_op jit(solution)/shard_map/all_to_all | solution.py:882
  26.2 11.8 %collective-permute-start.2 = (f32[3,12,8,128]{3,2,1,0:T(8,128)S(1)}, f32[3,12,8,128]{3,2,1,0:T(8,128)S(1)}, u32[]{:S(2)}, u32[]{:S(2)}) collective-permute-start(f32[3,12,8,128]{3,2,1,0:T(8,128)S(1)} %get-tuple-element.39), channel_id=1, source_target_pairs={{0,2},{2,0},{4,6},{6,4},{1,3},{3,1},{5,7},{7,5},{8,10},{10,8},{12,... | collective-permute-start | bytes 442376 | tf_op jit(solution)/shard_map/ppermute | solution.py:84
  26.7 11.3 %collective-permute-start.3 = (f32[3,12,8,128]{3,2,1,0:T(8,128)S(1)}, f32[3,12,8,128]{3,2,1,0:T(8,128)S(1)}, u32[]{:S(2)}, u32[]{:S(2)}) collective-permute-start(f32[3,12,8,128]{3,2,1,0:T(8,128)S(1)} %get-tuple-element.40), channel_id=1, source_target_pairs={{0,6},{2,4},{4,2},{6,0},{1,7},{3,5},{5,3},{7,1},{8,14},{10,12},{12... | collective-permute-start | bytes 442376 | tf_op jit(solution)/shard_map/ppermute | solution.py:85
  33.6 11.8 %collective-permute-start.5 = (f32[16,8,128]{2,1,0:T(8,128)S(1)}, f32[16,8,128]{2,1,0:T(8,128)S(1)}, u32[]{:S(2)}, u32[]{:S(2)}) collective-permute-start(f32[16,8,128]{2,1,0:T(8,128)S(1)} %get-tuple-element.46), channel_id=1, source_target_pairs={{0,8},{8,0},{16,24},{24,16},{1,9},{9,1},{17,25},{25,17},{2,10},{10... | collective-permute-start | bytes 196616 | tf_op jit(solution)/shard_map/ppermute | solution.py:84
  35.4 10.1 %collective-permute-start.6 = (f32[16,8,128]{2,1,0:T(8,128)S(1)}, f32[16,8,128]{2,1,0:T(8,128)S(1)}, u32[]{:S(2)}, u32[]{:S(2)}) collective-permute-start(f32[16,8,128]{2,1,0:T(8,128)S(1)} %get-tuple-element.47), channel_id=1, source_target_pairs={{0,24},{8,16},{16,8},{24,0},{1,25},{9,17},{17,9},{25,1},{2,26},{10... | collective-permute-start | bytes 196616 | tf_op jit(solution)/shard_map/ppermute | solution.py:85
  39.7 4.2 %collective-permute-start.4 = (f32[3,4,8,128]{3,2,1,0:T(8,128)S(1)}, f32[3,4,8,128]{3,2,1,0:T(8,128)S(1)}, u32[]{:S(2)}, u32[]{:S(2)}) collective-permute-start(f32[3,4,8,128]{3,2,1,0:T(8,128)S(1)} %shard_map.106), channel_id=1, source_target_pairs={{0,1},{1,0},{2,3},{3,2},{4,5},{5,4},{6,7},{7,6},{8,9},{9,8},{10,11... | collective-permute-start | bytes 147464 | tf_op jit(solution)/shard_map/ppermute | solution.py:84
  63.5 12.7 %all-to-all-start.3 = ((f32[8,8,8,128]{3,2,1,0:T(8,128)}), f32[8,8,8,128]{3,2,1,0:T(8,128)S(1)}, u32[]{:S(2)}, u32[]{:S(2)}) async-start(f32[8,8,8,128]{3,2,1,0:T(8,128)} %get-tuple-element.58), calls=%async_computation.3 | async-start | bytes 524288 | tf_op jit(solution)/shard_map/all_to_all | solution.py:882
  67.1 4.3 %collective-permute-start.7 = (f32[1,4,4,8,128]{4,3,2,1,0:T(8,128)S(1)}, f32[1,4,4,8,128]{4,3,2,1,0:T(8,128)S(1)}, u32[]{:S(2)}, u32[]{:S(2)}) collective-permute-start(f32[1,4,4,8,128]{4,3,2,1,0:T(8,128)S(1)} %get-tuple-element.50), channel_id=1, source_target_pairs={{0,8},{8,0},{16,24},{24,16},{1,9},{9,1},{17,25},{25,17},{2,10},{10... | collective-permute-start | bytes 196616 | tf_op jit(solution)/shard_map/ppermute | solution.py:84
  68.2 6.1 %collective-permute-start.8 = (f32[1,4,4,8,128]{4,3,2,1,0:T(8,128)S(1)}, f32[1,4,4,8,128]{4,3,2,1,0:T(8,128)S(1)}, u32[]{:S(2)}, u32[]{:S(2)}) collective-permute-start(f32[1,4,4,8,128]{4,3,2,1,0:T(8,128)S(1)} %get-tuple-element.51), channel_id=1, source_target_pairs={{0,24},{8,16},{16,8},{24,0},{1,25},{9,17},{17,9},{25,1},{2,26},{10... | collective-permute-start | bytes 196616 | tf_op jit(solution)/shard_map/ppermute | solution.py:85
  74.3 5.6 %collective-permute-start.10 = (f32[1,12,8,128]{3,2,1,0:T(8,128)S(1)}, f32[1,12,8,128]{3,2,1,0:T(8,128)S(1)}, u32[]{:S(2)}, u32[]{:S(2)}) collective-permute-start(f32[1,12,8,128]{3,2,1,0:T(8,128)S(1)} %get-tuple-element.53), channel_id=1, source_target_pairs={{0,6},{2,4},{4,2},{6,0},{1,7},{3,5},{5,3},{7,1},{8,14},{10,12},{12... | collective-permute-start | bytes 147464 | tf_op jit(solution)/shard_map/ppermute | solution.py:85
  74.5 5.5 %collective-permute-start.9 = (f32[1,12,8,128]{3,2,1,0:T(8,128)S(1)}, f32[1,12,8,128]{3,2,1,0:T(8,128)S(1)}, u32[]{:S(2)}, u32[]{:S(2)}) collective-permute-start(f32[1,12,8,128]{3,2,1,0:T(8,128)S(1)} %get-tuple-element.52), channel_id=1, source_target_pairs={{0,2},{2,0},{4,6},{6,4},{1,3},{3,1},{5,7},{7,5},{8,10},{10,8},{12,... | collective-permute-start | bytes 147464 | tf_op jit(solution)/shard_map/ppermute | solution.py:84
  78.4 6.0 %collective-permute-start.12 = (f32[16,8,128]{2,1,0:T(8,128)S(1)}, f32[16,8,128]{2,1,0:T(8,128)S(1)}, u32[]{:S(2)}, u32[]{:S(2)}) collective-permute-start(f32[16,8,128]{2,1,0:T(8,128)S(1)} %get-tuple-element.60), channel_id=1, source_target_pairs={{0,8},{8,0},{16,24},{24,16},{1,9},{9,1},{17,25},{25,17},{2,10},{10... | collective-permute-start | bytes 196616 | tf_op jit(solution)/shard_map/ppermute | solution.py:84
  79.0 6.1 %collective-permute-start.13 = (f32[16,8,128]{2,1,0:T(8,128)S(1)}, f32[16,8,128]{2,1,0:T(8,128)S(1)}, u32[]{:S(2)}, u32[]{:S(2)}) collective-permute-start(f32[16,8,128]{2,1,0:T(8,128)S(1)} %get-tuple-element.61), channel_id=1, source_target_pairs={{0,24},{8,16},{16,8},{24,0},{1,25},{9,17},{17,9},{25,1},{2,26},{10... | collective-permute-start | bytes 196616 | tf_op jit(solution)/shard_map/ppermute | solution.py:85
  80.3 3.8 %collective-permute-start.11 = (f32[1,4,8,128]{3,2,1,0:T(8,128)S(1)}, f32[1,4,8,128]{3,2,1,0:T(8,128)S(1)}, u32[]{:S(2)}, u32[]{:S(2)}) collective-permute-start(f32[1,4,8,128]{3,2,1,0:T(8,128)S(1)} %shard_map.111), channel_id=1, source_target_pairs={{0,1},{1,0},{2,3},{3,2},{4,5},{5,4},{6,7},{7,6},{8,9},{9,8},{10,11... | collective-permute-start | bytes 49160 | tf_op jit(solution)/shard_map/ppermute | solution.py:84
  96.3 3.6 %collective-permute-start.14 = (f32[8,128]{1,0:T(8,128)S(1)}, f32[8,128]{1,0:T(8,128)S(1)}, u32[]{:S(2)}, u32[]{:S(2)}) collective-permute-start(f32[8,128]{1,0:T(8,128)S(1)} %shard_map.117), channel_id=1, source_target_pairs={{0,8},{8,0},{16,24},{24,16},{1,9},{9,1},{17,25},{25,17},{2,10},{10... | collective-permute-start | bytes 12296 | tf_op jit(solution)/shard_map/ppermute | solution.py:1022
  99.9 4.5 %collective-permute-start.15 = (f32[8,128]{1,0:T(8,128)S(1)}, f32[8,128]{1,0:T(8,128)S(1)}, u32[]{:S(2)}, u32[]{:S(2)}) collective-permute-start(f32[8,128]{1,0:T(8,128)S(1)} %add.6), channel_id=1, source_target_pairs={{0,16},{8,24},{16,0},{24,8},{1,17},{9,25},{17,1},{25,9},{2,18},{10... | collective-permute-start | bytes 12296 | tf_op jit(solution)/shard_map/ppermute | solution.py:1022
